TPU v7x, 32 devices: a whole 2x2x4 slice. The times are simulated.
32 devices in a mesh: tp: 4 (over z), dp: 8 (over y, x, core).
Axes of the slice: x: 2, y: 2, z: 4, core: 2. Of those that a mesh axis runs over, the one named last changes fastest.
Arguments:
- tokens: int32 [32, 448], P('dp')
- labels: int32 [32, 448], P('dp')
- lossmask: int32 [32, 448], P('dp')
- hidden: bfloat16 [32, 448, 1280], P('dp')
- grad_x0: bfloat16 [32, 448, 1280], P('dp')
- embed_table: bfloat16 [51968, 1280], P('tp')
- pos_table: bfloat16 [448, 1280], replicated
- ln_gain: float32 [1280], replicated
- ln_bias: float32 [1280], replicated
Outputs:
- output 1: float32 [], replicated
- output 2: bfloat16 [32, 448, 1280], P('dp')
- output 3: bfloat16 [32, 448, 1280], P('dp')
- output 4: float32 [51968, 1280], P('tp')
- output 5: float32 [448, 1280], replicated
All inputs are finite; a program needn't handle non-finite values.
Results may differ from a plain program's by a relative error of at most 0.001.
Values sent between devices are 32-bit elements.
A program may use at most 1 GiB of HBM per device.

v0:
```python
import jax
import jax.numpy as jnp
from jax import lax
from jax.sharding import PartitionSpec as P


def layer_norm(h_f32, ln_gain, ln_bias):
    mean_val = jnp.mean(h_f32, axis=-1, keepdims=True)
    centered = h_f32 - mean_val
    var_val = jnp.mean(centered * centered, axis=-1, keepdims=True)
    return centered * lax.rsqrt(var_val + 1e-5) * ln_gain + ln_bias


def solution(mesh):
    def device_fn(tokens, labels, lossmask, hidden, grad_x0, embed_loc, pos_table, ln_gain, ln_bias):
        vocab_loc, d_model = embed_loc.shape
        shard_start = lax.axis_index('tp') * vocab_loc
        tok_local = tokens - shard_start
        tok_here = (tok_local >= 0) & (tok_local < vocab_loc)
        rows = jnp.take(embed_loc, jnp.where(tok_here, tok_local, 0), axis=0)
        rows = jnp.where(tok_here[..., None], rows.astype(jnp.float32), 0.0)
        rows = lax.psum(rows, 'tp')
        embed_out = (rows + pos_table.astype(jnp.float32)[None]).astype(jnp.bfloat16)

        z_f32, norm_vjp = jax.vjp(lambda h_in: layer_norm(h_in, ln_gain, ln_bias), hidden.astype(jnp.float32))
        z_bf16 = z_f32.astype(jnp.bfloat16)
        logits = jnp.einsum('btd,vd->btv', z_bf16, embed_loc, preferred_element_type=jnp.float32)
        row_max = lax.pmax(jnp.max(logits, axis=-1), 'tp')
        shifted = jnp.exp(logits - row_max[..., None])
        lab_local = labels - shard_start
        hit = jnp.arange(vocab_loc, dtype=jnp.int32) == lab_local[..., None]
        exp_sum, lab_logit = lax.psum((jnp.sum(shifted, axis=-1), jnp.sum(jnp.where(hit, logits, 0.0), axis=-1)), 'tp')
        tok_nll = row_max + jnp.log(exp_sum) - lab_logit
        mask_f = lossmask.astype(jnp.float32)
        loss_sum, mask_count = lax.psum((jnp.sum(mask_f * tok_nll), jnp.sum(mask_f)), 'dp')
        mean_loss = loss_sum / mask_count

        weight = mask_f / mask_count
        g_bf16 = ((shifted / exp_sum[..., None] - hit.astype(jnp.float32)) * weight[..., None]).astype(jnp.bfloat16)
        grad_z = lax.psum(jnp.einsum('btv,vd->btd', g_bf16, embed_loc, preferred_element_type=jnp.float32), 'tp')
        grad_hidden = norm_vjp(grad_z)[0].astype(jnp.bfloat16)
        dx_f32 = grad_x0.astype(jnp.float32)
        tok_seg = jnp.where(tok_here, tok_local, vocab_loc).reshape(-1)
        embed_part = jnp.einsum('btv,btd->vd', g_bf16, z_bf16, preferred_element_type=jnp.float32) + jax.ops.segment_sum(dx_f32.reshape(-1, d_model), tok_seg, num_segments=vocab_loc)
        grad_embed = lax.psum(embed_part, 'dp')
        grad_pos = lax.psum(jnp.sum(dx_f32, axis=0), 'dp')
        return mean_loss, embed_out, grad_hidden, grad_embed, grad_pos

    row_spec = P('dp', None)
    act_spec = P('dp', None, None)
    return jax.shard_map(device_fn, mesh=mesh, in_specs=(row_spec, row_spec, row_spec, act_spec, act_spec, P('tp', None), P(None, None), P(None), P(None)), out_specs=(P(), act_spec, act_spec, P('tp', None), P(None, None)), check_vma=False)
```

profile of v0, /device:TPU:0, one launch (start us, length us, event | category | flops | bytes accessed | tf_op | source)
XLA Modules:
  0.0 1780.2 jit_solution(9355402104212864609)
XLA Ops:
  7.2 0.0 copy-start.14
  7.2 0.0 copy-start.5
  7.2 0.0 all-reduce.9.cloned.1.call-start
  7.2 0.0 copy-start
  7.3 3.1 convert_reduce_fusion
  10.4 0.0 copy-start.3
  10.4 3.7 fusion.10
  14.1 0.0 copy-start.9
  14.1 0.6 copy-done.9
  14.7 0.0 copy-done.3
  14.7 0.0 copy-start.7
  14.7 0.6 copy-done.7
  15.3 0.0 copy-done.14
  15.3 0.0 copy-done.5
  15.3 1.9 fusion.21.clone.4
  17.2 0.0 copy-start.18
  17.2 0.0 copy-start.12
  17.2 72.0 %fusion.23 = (f32[4,448]{1,0:T(4,128)S(1)}, f32[4,448,12992]{2,1,0:T(8,128)}) fusion(bf16[12992,1280]{1,0:T(8,128)(2,1)} %param.14, bf16[4,448,1280]{2,1,0:T(8,128)(2,1)S(1)} %fusion.21.clone.4), kind=kOutput, calls=%fused_computation.47 | convolution fusion | flops 59624341504 | bytes 130980864 | tf_op jit(solution)/shard_map/btd,vd->btv/dot_general | solution.py:27
  89.2 13.7 pmax.7
  102.9 0.0 copy-done.18
  103.0 0.6 compare_and_fusion
  103.6 0.1 reshape.53
  103.7 53.2 %gather_fusion = bf16[1792,1280]{1,0:T(8,128)(2,1)} fusion(bf16[12992,1280]{1,0:T(8,128)(2,1)} %param.14, s32[2048]{0:T(1024)S(1)} %pad_clamp_fusion.1), kind=kCustom, calls=%fused_computation | custom fusion | bytes 9182208 | tf_op jit(solution)/shard_map/jit(_take)/gather | solution.py:20
  156.9 29.5 %fusion.1 = (f32[4,448]{1,0:T(4,128)S(1)}, f32[4,448]{1,0:T(4,128)S(1)}) fusion(f32[4,448,12992]{2,1,0:T(8,128)} %get-tuple-element.23, f32[4,448]{1,0:T(4,128)S(1)} %pmax.7, s32[4,448]{1,0:T(4,128)S(1)} %broadcast_subtract_fusion), kind=kLoop, calls=%fused_computation.7 | loop fusion | flops 116404736 | bytes 93155328 | tf_op jit(solution)/shard_map/reduce_sum | solution.py:32
  186.4 15.6 all-reduce.2
  202.0 0.0 copy-done.11
  202.0 0.6 convert_reduce_fusion.2
  202.6 12.9 all-reduce
  215.5 0.6 convert_divide_fusion
  216.2 0.0 slice-start.4
  216.2 46.2 %multiply_convert_fusion = bf16[4,448,12992]{2,1,0:T(8,128)(2,1)} fusion(f32[4,448,12992]{2,1,0:T(8,128)} %get-tuple-element.23, f32[4,448]{1,0:T(4,128)S(1)} %convert_divide_fusion, f32[4,448]{1,0:T(4,128)S(1)} %get-tuple-element.16, s32[4,448]{1,0:T(4,128)S(1)} %broadcast_subtract_fusion, f32[4,448]{1,0:T(4,128)S(1)} %pmax.7), kind=kLoop, calls=%fused_computation.3 | loop fusion | flops 162971648 | bytes 139718656 | tf_op jit(solution)/shard_map/convert_element_type | solution.py:39
  262.4 70.3 %fusion.2 = f32[4,448,1280]{2,1,0:T(8,128)} fusion(bf16[4,448,12992]{2,1,0:T(8,128)(2,1)} %multiply_convert_fusion, bf16[12992,1280]{1,0:T(8,128)(2,1)} %param.14), kind=kOutput, calls=%fused_computation.9 | convolution fusion | flops 59601059840 | bytes 88997888 | tf_op jit(solution)/shard_map/btv,vd->btd/dot_general | solution.py:40
  332.8 0.0 copy-done.17
  332.8 4.0 convert_select_fusion
  336.8 0.0 all-reduce.9.cloned.1.call-update
  336.9 0.0 slice-start
  336.9 0.0 copy-start.4
  336.9 0.0 copy-start.6
  336.9 0.0 copy-start.8
  336.9 0.0 copy-start.15
  336.9 0.0 all-reduce.7.cloned.1.call-start
  337.0 0.6 copy-done.13
  337.5 0.1 reshape.61
  337.6 4.4 sort
  342.1 0.0 slice-start.1
  342.1 6.7 bitcast_convert_fusion
  348.8 73.3 %convolution_bitcast_fusion = f32[12992,1280]{1,0:T(8,128)} fusion(bf16[4,448,12992]{2,1,0:T(8,128)(2,1)} %multiply_convert_fusion, bf16[4,448,1280]{2,1,0:T(8,128)(2,1)S(1)} %bitcast.20, f32[1280]{0:T(1024)S(1)} %copy-done.15, f32[1280]{0:T(1024)S(1)} %copy-done.6, f32[4,448]{1,0:T(4,128)S(1)} %copy-done.8, f32[4,448]{1,0:T(4,128)S(1)} %copy-done.4), kind=kOutput, calls=%fused_computation.8 | convolution fusion | flops 59614822400 | bytes 117694464 | tf_op jit(solution)/shard_map/btv,btd->vd/dot_general | solution.py:44
  422.1 87.2 %scatter_custom_fusion = f32[12992,1280]{1,0:T(8,128)} fusion(f32[12992,1280]{1,0:T(8,128)} %convolution_bitcast_fusion, s32[1792]{0:T(1024)S(1)} %get-tuple-element.5, f32[1792,1280]{1,0:T(8,128)} %bitcast_convert_fusion, s32[2048]{0:T(1024)S(1)} %pad_clamp_fusion), kind=kCustom, calls=%fused_computation.25 | custom fusion | flops 2293760 | bytes 66519040 | tf_op jit(solution)/shard_map/scatter-add | solution.py:44
  509.3 4.6 convert_reduce_fusion.1
  513.8 0.0 all-reduce.7.cloned.1.call-update
  513.9 0.0 copy-start.10
  513.9 0.0 slice-start.2
  515.3 1.4 convert_element_type.34
  516.7 428.0 %all-reduce.9.cloned.1.call-done = (f32[4,448,1280]{2,1,0:T(8,128)}, f32[4,448,1280]{2,1,0:T(8,128)}) async-done(((f32[4,448,1280]{2,1,0:T(8,128)}, f32[4,448,1280]{2,1,0:T(8,128)}), (f32[4,448,1280]{2,1,0:T(8,128)}, f32[4,448,1280]{2,1,0:T(8,128)})) %all-reduce.9.cloned.1.call-update) | async-done | bytes 18350096 | tf_op jit(solution)/shard_map/psum | solution.py:22
  944.7 6.8 fusion.14
  951.6 0.0 slice-done.2
  951.6 0.7 copy-done.1
  952.3 1.2 slice-done.3
  953.5 3.1 fusion.19
  956.6 6.6 add_convert_fusion.1
  963.2 8.0 add_convert_fusion
  971.2 754.3 %all-reduce.7.cloned.1.call-done = (f32[12992,1280]{1,0:T(8,128)}, f32[448,1280]{1,0:T(8,128)}) async-done(((f32[12992,1280]{1,0:T(8,128)}, f32[448,1280]{1,0:T(8,128)}), (f32[12992,1280]{1,0:T(8,128)}, f32[448,1280]{1,0:T(8,128)})) %all-reduce.7.cloned.1.call-update) | async-done | bytes 68812816 | tf_op jit(solution)/shard_map/psum | solution.py:45
  1725.5 44.9 %copy.19 = f32[12992,1280]{1,0:T(8,128)} copy(f32[12992,1280]{1,0:T(8,128)} %get-tuple-element.27) | data formatting | bytes 133038080
  1770.4 1.4 copy.20
  (33 shorter events, 0.1 us)
Async XLA Ops:
  7.2 8.1 copy-start.14
  7.2 8.1 copy-start.5
  7.2 937.5 %all-reduce.9.cloned.1.call-start = ((), (), s32[]{:S(2)}) async-start(), calls=%async_computation.1 | async-start | bytes 36700160 | tf_op jit(solution)/shard_map/psum | solution.py:22
  7.2 8.1 copy-start
  10.4 4.3 copy-start.3
  14.1 0.6 copy-start.9
  14.7 0.6 copy-start.7
  17.2 85.8 %copy-start.18 = (s32[4,448]{1,0:T(4,128)S(1)}, s32[4,448]{1,0:T(4,128)}, u32[]{:S(2)}) copy-start(s32[4,448]{1,0:T(4,128)} %param.10) | copy-start | bytes 21508
  17.2 85.8 %copy-start.12 = (s32[4,448]{1,0:T(4,128)S(1)}, s32[4,448]{1,0:T(4,128)}, u32[]{:S(2)}) copy-start(s32[4,448]{1,0:T(4,128)} %param.9) | copy-start | bytes 21508
  156.9 45.1 %copy-start.11 = (s32[4,448]{1,0:T(4,128)S(1)}, s32[4,448]{1,0:T(4,128)}, u32[]{:S(2)}) copy-start(s32[4,448]{1,0:T(4,128)} %param.11) | copy-start | bytes 21508
  216.2 116.6 %slice-start.4 = ((s8[4587520]{0:T(1024)(128)(4,1)}), s8[393216]{0:T(1024)(128)(4,1)S(1)}, s32[]{:S(2)}) async-start(s8[4587520]{0:T(1024)(128)(4,1)} %bitcast.23), calls=%async_computation.6 | async-start | bytes 786432
  262.4 70.4 %slice-start.5 = ((s8[4587520]{0:T(1024)(128)(4,1)}), s8[4194304]{0:T(1024)(128)(4,1)S(1)}, s32[]{:S(2)}) async-start(s8[4587520]{0:T(1024)(128)(4,1)} %bitcast.23), calls=%async_computation.7 | async-start | bytes 8388608
  262.4 70.4 %copy-start.16 = (pred[4,448]{1,0:T(4,128)(4,1)S(1)}, pred[4,448]{1,0:T(4,128)(4,1)}, u32[]{:S(2)}) copy-start(pred[4,448]{1,0:T(4,128)(4,1)} %get-tuple-element.19) | copy-start | bytes 5380
  262.4 70.4 %copy-start.17 = (pred[4,448]{1,0:T(4,128)(4,1)S(1)}, pred[4,448]{1,0:T(4,128)(4,1)}, u32[]{:S(2)}) copy-start(pred[4,448]{1,0:T(4,128)(4,1)} %get-tuple-element.21) | copy-start | bytes 5380
  336.8 0.7 copy-start.13
  336.9 11.9 slice-start
  336.9 11.9 copy-start.4
  336.9 11.9 copy-start.6
  336.9 11.9 copy-start.8
  336.9 11.9 copy-start.15
  336.9 1388.5 %all-reduce.7.cloned.1.call-start = ((), (), s32[]{:S(2)}) async-start(), calls=%async_computation | async-start | bytes 137625600 | tf_op jit(solution)/shard_map/psum | solution.py:45
  342.1 6.7 slice-start.1
  513.9 437.7 %copy-start.10 = (f32[4,448]{1,0:T(4,128)S(1)}, f32[4,448]{1,0:T(4,128)}, u32[]{:S(2)}) copy-start(f32[4,448]{1,0:T(4,128)} %copy-done.9) | copy-start | bytes 21508
  513.9 437.7 %slice-start.2 = ((s8[4587520]{0:T(1024)(128)(4,1)}), s8[393216]{0:T(1024)(128)(4,1)S(1)}, s32[]{:S(2)}) async-start(s8[4587520]{0:T(1024)(128)(4,1)} %bitcast.21), calls=%async_computation.4 | async-start | bytes 786432
  944.7 7.6 copy-start.1
  944.7 8.8 slice-start.3
  1725.5 44.9 %copy-start.2 = (f32[448,1280]{1,0:T(8,128)S(1)}, f32[448,1280]{1,0:T(8,128)}, u32[]{:S(2)}) copy-start(f32[448,1280]{1,0:T(8,128)} %get-tuple-element.28) | copy-start | bytes 6881284
Sparse Core Ops, SparseCore 0:
  337.0 607.6 all-reduce.8
  949.3 776.1 all-reduce.6
where the time goes:
time: 1790 us; the launch traced here: 1780 us
  waiting for transfers between devices  1180 us (66%)
  other arithmetic  219 us (12%)
  matrix products  216 us (12%)
  local copies, waits for them, and re-layouts  103 us (6%)
  blocking collectives  42.2 us (2%)
    psum x1, waiting for transfers between devices, device_fn(): grad_embed = lax.psum(embed_part, 'dp')  754 us
    psum x1, waiting for transfers between devices, device_fn(): rows = lax.psum(rows, 'tp')  428 us
    scatter-add x3, other arithmetic, device_fn(): jax.ops.segment_sum(dx_f32.reshape(-1, d_model), tok_seg, num_segments=vo...  91.6 us
    dot_general x1, matrix products, device_fn(): jnp.einsum('btv,btd->vd', g_bf16, z_bf16, preferred_element_type=jnp.floa...  73.3 us
    dot_general x1, matrix products, device_fn(): jnp.einsum('btd,vd->btv', z_bf16, embed_loc, preferred_element_type=jnp.f...  72 us
    dot_general x1, matrix products, device_fn(): jnp.einsum('btv,vd->btd', g_bf16, embed_loc, preferred_element_type=jnp.f...  70.3 us
    gather x1, local copies, waits for them, and re-layouts, device_fn(): rows = jnp.take(embed_loc, jnp.where(tok_here, tok_local, 0), axis=0)  53.2 us
    unnamed x52, local copies, waits for them, and re-layouts  50.1 us
  transfers between devices with their start and end apart: 2, of which 2 were waited for; matrix products, arithmetic and copies ran while one was open for 11% of the time, Pallas kernels for 0%

commit v1 on v0

v1 whole, which is shorter than its diff:
```python
import functools

import jax
import jax.numpy as jnp
from jax import lax
from jax.experimental import pallas as pl
from jax.experimental.pallas import tpu as pltpu
from jax.sharding import PartitionSpec as P

MESH = pl.DeviceIdType.MESH
F32 = jnp.float32
BF16 = jnp.bfloat16
NT = (((1,), (1,)), ((), ()))
TN = (((0,), (0,)), ((), ()))
RING = 4
SLOTS = 8
VMEM_LIMIT = 66_000_000


def sizes(tokens, vocab_loc):
    if vocab_loc % 448 == 0 and tokens % 1792 == 0:
        return 448, 256, 56
    return 64, 128, 8


def stats_kernel(chunk, tile, hidden, gain, bias, lab, embed, zb, stats, m_ref, s_ref, l_ref):
    step = pl.program_id(0)
    tokens = hidden.shape[0]
    tiles = tokens // tile

    @pl.when(step == 0)
    def _():
        def norm(j, carry):
            rows = pl.ds(pl.multiple_of(j * tile, tile), tile)
            h = hidden[rows, :].astype(F32)
            centered = h - jnp.mean(h, axis=-1, keepdims=True)
            var = jnp.mean(centered * centered, axis=-1, keepdims=True)
            zb[rows, :] = (centered * lax.rsqrt(var + 1e-5) * gain[...] + bias[...]).astype(BF16)
            return carry
        lax.fori_loop(0, tiles, norm, 0)
        m_ref[...] = jnp.full_like(m_ref, -jnp.inf)
        s_ref[...] = jnp.zeros_like(s_ref)
        l_ref[...] = jnp.zeros_like(l_ref)

    e = embed[...]
    ids = lax.broadcasted_iota(jnp.int32, (chunk, tile), 0) + step * chunk
    for j in range(tiles):
        cols = slice(j * tile, (j + 1) * tile)
        logits = lax.dot_general(e, zb[cols, :], NT, preferred_element_type=F32)
        m_old = m_ref[:, cols]
        m_new = jnp.maximum(m_old, jnp.max(logits, axis=0, keepdims=True))
        m_ref[:, cols] = m_new
        s_ref[:, cols] = s_ref[:, cols] * jnp.exp(m_old - m_new) + jnp.sum(jnp.exp(logits - m_new), axis=0, keepdims=True)
        l_ref[:, cols] += jnp.sum(jnp.where(ids == lab[:, cols], logits, 0.0), axis=0, keepdims=True)

    @pl.when(step == pl.num_programs(0) - 1)
    def _():
        stats[0:1, :] = m_ref[...] + jnp.log(s_ref[...])
        stats[1:2, :] = l_ref[...]


def token_stats(hidden, gain, bias, lab, embed, chunk, tile):
    tokens, d = hidden.shape
    steps = embed.shape[0] // chunk
    whole = lambda shape: pl.BlockSpec(shape, lambda i: (0, 0))
    return pl.pallas_call(
        functools.partial(stats_kernel, chunk, tile),
        grid=(steps,),
        out_shape=(jax.ShapeDtypeStruct((tokens, d), BF16), jax.ShapeDtypeStruct((2, tokens), F32)),
        in_specs=[whole((tokens, d)), whole((1, d)), whole((1, d)), whole((1, tokens)),
                  pl.BlockSpec((chunk, d), lambda i: (i, 0))],
        out_specs=(whole((tokens, d)), whole((2, tokens))),
        scratch_shapes=[pltpu.VMEM((1, tokens), F32)] * 3,
        compiler_params=pltpu.CompilerParams(vmem_limit_bytes=VMEM_LIMIT),
        cost_estimate=pl.CostEstimate(flops=2 * tokens * d * embed.shape[0], bytes_accessed=2 * embed.size,
                                      transcendentals=tokens * embed.shape[0]),
        name='token_stats',
    )(hidden, gain, bias, lab, embed)


def grad_kernel(ntp, chunk, tile, zrows,
                zb, dx, lse, wgt, lab, tok, embed,
                out, gz, own, d2d, rs_r, rs_l,
                ebuf, gt, oh, acc, gbuf, ld_own, ld_d2d, s1, s2, fin, rs1, rs2, zin_r, zin_l, zout_r, zout_l, zfin,
                e_sem, own_sem, d2d_s, d2d_r, ld_sem, rs1_s, rs1_r, rs2_s, rs2_r, fin_s, ag1_r, ag2_r, fwd_s, part_r,
                zld, zrs_sr, zrs_sl, zrs_rr, zrs_rl, zfin_s, zag_rr, zag_rl, zfw_r, zfw_l):
    tokens, d = zb.shape
    vocab_loc = embed.shape[0]
    nc = vocab_loc // chunk
    tiles = tokens // tile
    ntile = 256 if d % 256 == 0 and d > 256 else 128
    half, quarter, eighth = chunk // 2, chunk // 4, chunk // 8
    dp, z = lax.axis_index('dp'), lax.axis_index('tp')
    core = lax.rem(dp, 2)
    xpos = lax.rem(lax.div(dp, 2), 2)
    ypos = lax.div(dp, 4)
    partner = dp + 1 - 2 * core
    x_nbr = dp + 2 - 4 * xpos
    y_nbr = dp + 4 - 8 * ypos

    def place(k):
        odd = lax.rem(k, 2)
        n1 = x_nbr + (y_nbr - x_nbr) * odd
        n2 = y_nbr + (x_nbr - y_nbr) * odd
        a1 = xpos + (ypos - xpos) * odd
        a2 = ypos + (xpos - ypos) * odd
        return n1, n2, a1, a2

    def rdma(src, dst, ssem, rsem, dev):
        return pltpu.make_async_remote_copy(src_ref=src, dst_ref=dst, send_sem=ssem, recv_sem=rsem,
                                            device_id={'dp': dev}, device_id_type=MESH)

    def zdma(src, dst, ssem, rsem, dev):
        return pltpu.make_async_remote_copy(src_ref=src, dst_ref=dst, send_sem=ssem, recv_sem=rsem,
                                            device_id={'tp': dev}, device_id_type=MESH)

    def rows8(start, n):
        return pl.ds(pl.multiple_of(start, 8), n)

    def valid(k, limit=None):
        return (k >= 0) & (k < (nc if limit is None else limit))

    def e_copy(k):
        return pltpu.make_async_copy(embed.at[rows8(k * chunk, chunk)], ebuf.at[lax.rem(k, 2)], e_sem.at[lax.rem(k, 2)])

    def own_copy(k):
        b = lax.rem(k, 2)
        return pltpu.make_async_copy(gbuf.at[b, rows8(core * half, half)], own.at[k], own_sem.at[b])

    def d2d_copy(k):
        b = lax.rem(k, 2)
        return rdma(gbuf.at[b, rows8((1 - core) * half, half)], d2d.at[k], d2d_s.at[b], d2d_r.at[k], partner)

    def rs1_copy(k):
        n1, _, a1, _ = place(k)
        b, r = lax.rem(k, RING), lax.rem(k, SLOTS)
        return rdma(s1.at[b, rows8((1 - a1) * quarter, quarter)], rs1.at[r], rs1_s.at[b], rs1_r.at[r], n1)

    def rs2_copy(k):
        _, n2, _, a2 = place(k)
        b, r = lax.rem(k, RING), lax.rem(k, SLOTS)
        return rdma(s2.at[b, rows8((1 - a2) * eighth, eighth)], rs2.at[r], rs2_s.at[b], rs2_r.at[r], n2)

    def fin_copies(k):
        n1, n2, a1, a2 = place(k)
        b = lax.rem(k, RING)
        dst = out.at[rows8(k * chunk + core * half + a1 * quarter + a2 * eighth, eighth)]
        src = fin.at[b]
        return (pltpu.make_async_copy(src, dst, fin_s.at[0, b]),
                rdma(src, dst, fin_s.at[1, b], ag1_r.at[k], n2),
                rdma(src, dst, fin_s.at[2, b], ag2_r.at[0, k], n1),
                rdma(src, dst, fin_s.at[3, b], part_r.at[0, k], partner))

    def fwd_copies(k):
        n1, _, a1, a2 = place(k)
        b = lax.rem(k, RING)
        ref = out.at[rows8(k * chunk + core * half + a1 * quarter + (1 - a2) * eighth, eighth)]
        return (rdma(ref, ref, fwd_s.at[0, b], ag2_r.at[1, k], n1),
                rdma(ref, ref, fwd_s.at[1, b], part_r.at[1, k], partner))

    def last_copy(k):
        _, _, a1, _ = place(k)
        ref = out.at[rows8(k * chunk + core * half + (1 - a1) * quarter, quarter)]
        return rdma(ref, ref, fwd_s.at[2, lax.rem(k, RING)], part_r.at[2, k], partner)

    def compute(k, carry):
        slot = lax.rem(k, 2)
        e_copy(k).wait()

        @pl.when(k + 1 < nc)
        def _():
            e_copy(k + 1).start()

        ids = lax.broadcasted_iota(jnp.int32, (chunk, tile), 0) + k * chunk

        def per_tile(j, c):
            cols = pl.ds(pl.multiple_of(j * tile, tile), tile)
            e = ebuf[slot]
            logits = lax.dot_general(e, zb[cols, :], NT, preferred_element_type=F32)
            hit = jnp.where(ids == lab[j], 1.0, 0.0)
            g = ((jnp.exp(logits - lse[j]) - hit) * wgt[j]).astype(BF16)
            gt[:, cols] = g
            oh[:, cols] = jnp.where(ids == tok[j], 1.0, 0.0).astype(BF16)
            acc[cols, :] += lax.dot_general(g, e, TN, preferred_element_type=F32)
            return c
        lax.fori_loop(0, tiles, per_tile, 0)

        @pl.when(k >= 1)
        def _():
            own_copy(k - 1).wait()
            d2d_copy(k - 1).wait_send()

        def per_cols(n, c):
            cols = pl.ds(pl.multiple_of(n * ntile, ntile), ntile)
            gbuf[slot, :, cols] = (jnp.dot(gt[...], zb[:, cols], preferred_element_type=F32)
                                   + jnp.dot(oh[...], dx[:, cols], preferred_element_type=F32))
            return c
        lax.fori_loop(0, d // ntile, per_cols, 0)
        own_copy(k).start()
        d2d_copy(k).start()

        @pl.when(k == nc - 1)
        def _():
            own_copy(k).wait()
            d2d_copy(k).wait_send()
        return carry

    def load_start(k):
        d2d_copy(k).wait_recv()
        pltpu.make_async_copy(own.at[k], ld_own, ld_sem.at[0]).start()
        pltpu.make_async_copy(d2d.at[k], ld_d2d, ld_sem.at[1]).start()

    def stage_a(k):
        pltpu.make_async_copy(own.at[k], ld_own, ld_sem.at[0]).wait()
        pltpu.make_async_copy(d2d.at[k], ld_d2d, ld_sem.at[1]).wait()

        @pl.when(k >= RING)
        def _():
            rs1_copy(k - RING).wait_send()
        b = lax.rem(k, RING)

        def add(i, c):
            r = rows8(i * eighth, eighth)
            s1[b, r, :] = ld_own[r, :] + ld_d2d[r, :]
            return c
        lax.fori_loop(0, half // eighth, add, 0)
        rs1_copy(k).start()

    def stage_b(k):
        _, _, a1, _ = place(k)
        rs1_copy(k).wait_recv()

        @pl.when(k >= RING)
        def _():
            rs2_copy(k - RING).wait_send()
        b, r = lax.rem(k, RING), lax.rem(k, SLOTS)

        def add(i, c):
            s2[b, rows8(i * eighth, eighth), :] = (s1[b, rows8(a1 * quarter + i * eighth, eighth), :]
                                                   + rs1[r, rows8(i * eighth, eighth), :])
            return c
        lax.fori_loop(0, quarter // eighth, add, 0)
        rs2_copy(k).start()

    def stage_c(k):
        _, _, _, a2 = place(k)
        rs2_copy(k).wait_recv()

        @pl.when(k >= RING)
        def _():
            for i, c in enumerate(fin_copies(k - RING)):
                c.wait() if i == 0 else c.wait_send()
        b, r = lax.rem(k, RING), lax.rem(k, SLOTS)
        fin[b] = s2[b, rows8(a2 * eighth, eighth), :] + rs2[r]
        for c in fin_copies(k):
            c.start()

    def stage_d(k):
        fin_copies(k)[1].wait_recv()

        @pl.when(k >= RING)
        def _():
            for c in fwd_copies(k - RING):
                c.wait_send()
        for c in fwd_copies(k):
            c.start()

    def stage_e(k):
        fin_copies(k)[2].wait_recv()
        fwd_copies(k)[0].wait_recv()

        @pl.when(k >= RING)
        def _():
            last_copy(k - RING).wait_send()
        last_copy(k).start()

    def stage_f(k):
        fin_copies(k)[3].wait_recv()
        fwd_copies(k)[1].wait_recv()
        last_copy(k).wait_recv()

    nb = tokens // ntp // zrows
    qrows = tokens // ntp

    def zacc(q, b):
        return pl.multiple_of(q * qrows + b * zrows, 8)

    def right_copy(b, i, src=None):
        n = ntp - 1 - i
        s = zout_r.at[lax.rem(b, 2), pl.ds(i, n)] if src is None else src
        return zdma(s, rs_r.at[b, pl.ds(i, n)], zrs_sr.at[lax.rem(b, 2)], zrs_rr.at[b], i + 1)

    def left_copy(b, i):
        return zdma(zout_l.at[lax.rem(b, 2), pl.ds(0, i)], rs_l.at[b, pl.ds(0, i)], zrs_sl.at[lax.rem(b, 2)],
                    zrs_rl.at[b], i - 1)

    def z_right(b):
        for i in range(ntp - 1):
            @pl.when(z == i)
            def _(i=i):
                n = ntp - 1 - i
                if i > 0:
                    right_copy(b, i - 1).wait_recv()
                    load = pltpu.make_async_copy(rs_r.at[b, pl.ds(i, n)], zin_r.at[pl.ds(i, n)], zld.at[0])
                    load.start()
                    load.wait()

                @pl.when(b >= 2)
                def _():
                    right_copy(b - 2, i).wait_send()
                for q in range(i + 1, ntp):
                    mine = acc[pl.ds(zacc(q, b), zrows), :]
                    zout_r[lax.rem(b, 2), q - 1] = mine if i == 0 else zin_r[q - 1] + mine
                right_copy(b, i).start()

    def z_left(b):
        for i in range(1, ntp):
            @pl.when(z == i)
            def _(i=i):
                if i < ntp - 1:
                    left_copy(b, i + 1).wait_recv()
                    load = pltpu.make_async_copy(rs_l.at[b, pl.ds(0, i)], zin_l.at[pl.ds(0, i)], zld.at[0])
                    load.start()
                    load.wait()

                @pl.when(b >= 2)
                def _():
                    left_copy(b - 2, i).wait_send()
                for q in range(i):
                    mine = acc[pl.ds(zacc(q, b), zrows), :]
                    zout_l[lax.rem(b, 2), q] = mine if i == ntp - 1 else zin_l[q] + mine
                left_copy(b, i).start()

    def zfin_copies(b):
        s = lax.rem(b, 2)
        dst = gz.at[rows8(z * qrows + b * zrows, zrows)]
        return (pltpu.make_async_copy(zfin.at[s], dst, zfin_s.at[0, s]),
                zdma(zfin.at[s], dst, zfin_s.at[1, s], zag_rr.at[b, 0], z + 1),
                zdma(zfin.at[s], dst, zfin_s.at[2, s], zag_rl.at[b, 0], z - 1))

    def z_final(b):
        for i in range(ntp):
            @pl.when(z == i)
            def _(i=i):
                if i > 0:
                    right_copy(b, i - 1).wait_recv() if i == ntp - 1 else None
                    load = pltpu.make_async_copy(rs_r.at[b, i - 1], zin_r.at[i - 1], zld.at[0])
                    load.start()
                    load.wait()
                if i < ntp - 1:
                    left_copy(b, i + 1).wait_recv() if i == 0 else None
                    load = pltpu.make_async_copy(rs_l.at[b, i], zin_l.at[i], zld.at[0])
                    load.start()
                    load.wait()
                z_wait_fin(b - 2, b >= 2)
                total = acc[pl.ds(zacc(i, b), zrows), :]
                if i > 0:
                    total = zin_r[i - 1] + total
                if i < ntp - 1:
                    total = total + zin_l[i]
                zfin[lax.rem(b, 2)] = total
        copies = zfin_copies(b)
        copies[0].start()

        @pl.when(z < ntp - 1)
        def _():
            copies[1].start()

        @pl.when(z > 0)
        def _():
            copies[2].start()

    def z_wait_fin(b, cond):
        @pl.when(cond)
        def _():
            copies = zfin_copies(b)
            copies[0].wait()

            @pl.when(z < ntp - 1)
            def _():
                copies[1].wait_send()

            @pl.when(z > 0)
            def _():
                copies[2].wait_send()

    def zag(b, h, sign, ssem, rsem):
        ref = gz.at[rows8((z - sign * h) * qrows + b * zrows, zrows)]
        return zdma(ref, ref, ssem.at[b, h - 1], rsem.at[b, h], z + sign)

    def z_hop(b, h):
        ref_r = gz.at[rows8((z - h) * qrows + b * zrows, zrows)]
        ref_l = gz.at[rows8((z + h) * qrows + b * zrows, zrows)]

        @pl.when(z >= h)
        def _():
            zdma(ref_r, ref_r, zfw_r.at[b, 0], zag_rr.at[b, h - 1], z).wait_recv()
            if h < ntp - 1:
                @pl.when(z < ntp - 1)
                def _():
                    zag(b, h, 1, zfw_r, zag_rr).start()

        @pl.when(z + h <= ntp - 1)
        def _():
            zdma(ref_l, ref_l, zfw_l.at[b, 0], zag_rl.at[b, h - 1], z).wait_recv()
            if h < ntp - 1:
                @pl.when(z > 0)
                def _():
                    zag(b, h, -1, zfw_l, zag_rl).start()

    lead = min(8, nc)

    def cs(t):
        late = t - lead
        c = lead + lax.div(late * 3, 2)
        return jnp.minimum(jnp.where(t <= lead, t, c), nc)

    z_start = lead + -(-(nc - lead) * 2 // 3)
    ticks = max(nc + 13, z_start + nb + 2 * ntp)
    acc[...] = jnp.zeros_like(acc)
    e_copy(0).start()

    def tick(t, carry):
        ka = t - 2

        @pl.when(valid(ka))
        def _():
            load_start(ka)
        lax.fori_loop(cs(t), cs(t + 1), compute, 0)
        for stage, lag in ((stage_e, 10), (stage_d, 8), (stage_c, 6), (stage_b, 4), (stage_a, 2), (stage_f, 12)):
            @pl.when(valid(t - lag))
            def _(stage=stage, lag=lag):
                stage(t - lag)
        zt = t - z_start

        @pl.when(valid(zt - z, nb))
        def _():
            z_right(zt - z)

        @pl.when(valid(zt - (ntp - 1 - z), nb))
        def _():
            z_left(zt - (ntp - 1 - z))

        @pl.when(valid(zt - (ntp - 1), nb))
        def _():
            z_final(zt - (ntp - 1))
        for h in range(1, ntp):
            @pl.when(valid(zt - (ntp - 1) - h, nb))
            def _(h=h):
                z_hop(zt - (ntp - 1) - h, h)
        return carry
    lax.fori_loop(0, ticks, tick, 0)

    for k in range(max(nc - RING, 0), nc):
        rs1_copy(k).wait_send()
        rs2_copy(k).wait_send()
        for i, c in enumerate(fin_copies(k)):
            c.wait() if i == 0 else c.wait_send()
        for c in fwd_copies(k):
            c.wait_send()
        last_copy(k).wait_send()
    for b in range(max(nb - 2, 0), nb):
        for i in range(ntp - 1):
            @pl.when(z == i)
            def _(i=i, b=b):
                right_copy(b, i).wait_send()
        for i in range(1, ntp):
            @pl.when(z == i)
            def _(i=i, b=b):
                left_copy(b, i).wait_send()
        z_wait_fin(b, z >= 0)

    def drain(b, carry):
        for h in range(1, ntp - 1):
            @pl.when((z >= h) & (z < ntp - 1))
            def _(h=h):
                zag(b, h, 1, zfw_r, zag_rr).wait_send()

            @pl.when((z + h <= ntp - 1) & (z > 0))
            def _(h=h):
                zag(b, h, -1, zfw_l, zag_rl).wait_send()
        return carry
    lax.fori_loop(0, nb, drain, 0)


def gradients(ntp, zb, dx, lse, wgt, lab, tok, embed, chunk, tile, zrows):
    tokens, d = zb.shape
    vocab_loc = embed.shape[0]
    nc = vocab_loc // chunk
    half, quarter, eighth = chunk // 2, chunk // 4, chunk // 8
    nb = tokens // ntp // zrows
    vm = pl.BlockSpec(memory_space=pltpu.VMEM)
    hbm = pl.BlockSpec(memory_space=pl.ANY)
    dma = lambda *s: pltpu.SemaphoreType.DMA(s)
    vf = lambda *s: pltpu.VMEM(s, F32)
    sds = lambda *s: jax.ShapeDtypeStruct(s, F32)
    flops = 2 * tokens * d * vocab_loc
    rows = lambda a: a.reshape(tokens // tile, 1, tile)
    res = pl.pallas_call(
        functools.partial(grad_kernel, ntp, chunk, tile, zrows),
        out_shape=(sds(vocab_loc, d), sds(tokens, d), sds(nc, half, d), sds(nc, half, d),
                   sds(nb, ntp - 1, zrows, d), sds(nb, ntp - 1, zrows, d)),
        in_specs=[vm] * 6 + [hbm],
        out_specs=(hbm,) * 6,
        scratch_shapes=[
            pltpu.VMEM((2, chunk, d), BF16), pltpu.VMEM((chunk, tokens), BF16), pltpu.VMEM((chunk, tokens), BF16),
            vf(tokens, d), vf(2, chunk, d), vf(half, d), vf(half, d),
            vf(RING, half, d), vf(RING, quarter, d), vf(RING, eighth, d), vf(SLOTS, quarter, d), vf(SLOTS, eighth, d),
            vf(ntp - 1, zrows, d), vf(ntp - 1, zrows, d), vf(2, ntp - 1, zrows, d), vf(2, ntp - 1, zrows, d),
            vf(2, zrows, d),
            dma(2), dma(2), dma(2), dma(nc), dma(2), dma(RING), dma(SLOTS), dma(RING), dma(SLOTS), dma(4, RING),
            dma(nc), dma(2, nc), dma(3, RING), dma(3, nc),
            dma(1), dma(2), dma(2), dma(nb), dma(nb), dma(3, 2), dma(nb, ntp - 1), dma(nb, ntp - 1),
            dma(nb, ntp - 1), dma(nb, ntp - 1),
        ],
        compiler_params=pltpu.CompilerParams(vmem_limit_bytes=VMEM_LIMIT, has_side_effects=True),
        cost_estimate=pl.CostEstimate(flops=4 * flops, bytes_accessed=4 * vocab_loc * d * 4,
                                      transcendentals=tokens * vocab_loc),
        name='gradients',
    )(zb, dx, rows(lse), rows(wgt), rows(lab), rows(tok), embed)
    return res[0], res[1]


def layer_norm(h_f32, ln_gain, ln_bias):
    mean_val = jnp.mean(h_f32, axis=-1, keepdims=True)
    centered = h_f32 - mean_val
    var_val = jnp.mean(centered * centered, axis=-1, keepdims=True)
    return centered * lax.rsqrt(var_val + 1e-5) * ln_gain + ln_bias


def solution(mesh):
    ntp, ndp = mesh.shape['tp'], mesh.shape['dp']

    def device_fn(tokens, labels, lossmask, hidden, grad_x0, embed_loc, pos_table, ln_gain, ln_bias):
        vocab_loc, d = embed_loc.shape
        batch, ctx = tokens.shape
        ntok = batch * ctx
        chunk, tile, zrows = sizes(ntok, vocab_loc)
        shard_start = lax.axis_index('tp') * vocab_loc
        tok_local = tokens - shard_start
        tok_here = (tok_local >= 0) & (tok_local < vocab_loc)
        rows = jnp.take(embed_loc, jnp.where(tok_here, tok_local, 0), axis=0)
        rows = jnp.where(tok_here[..., None], rows.astype(F32), 0.0)
        rows = lax.psum(rows, 'tp')
        embed_out = (rows + pos_table.astype(F32)[None]).astype(BF16)
        grad_pos = lax.psum(jnp.sum(grad_x0.astype(F32), axis=0), 'dp')

        lab_local = (labels - shard_start).reshape(1, ntok)
        hidden2 = hidden.reshape(ntok, d)
        zb, stats = token_stats(hidden2, ln_gain.reshape(1, d), ln_bias.reshape(1, d), lab_local, embed_loc, chunk, tile)
        mask_f = lossmask.astype(F32).reshape(1, ntok)
        every = lax.all_gather(jnp.concatenate([stats, mask_f]), ('tp', 'dp'))
        every = every.reshape(ntp, ndp, 3, ntok)
        top = jnp.max(every[:, :, 0], axis=0)
        lse_all = top + jnp.log(jnp.sum(jnp.exp(every[:, :, 0] - top), axis=0))
        lab_all = jnp.sum(every[:, :, 1], axis=0)
        mask_all = every[0, :, 2]
        count = jnp.sum(mask_all)
        mean_loss = jnp.sum(mask_all * (lse_all - lab_all)) / count
        lse = lax.dynamic_index_in_dim(lse_all, lax.axis_index('dp'), 0, keepdims=True)
        wgt = mask_f / count

        grad_embed, grad_z = gradients(ntp, zb, grad_x0.reshape(ntok, d), lse, wgt, lab_local, tok_local.reshape(1, ntok),
                                       embed_loc, chunk, tile, zrows)
        norm_vjp = jax.vjp(lambda h: layer_norm(h, ln_gain, ln_bias), hidden2.astype(F32))[1]
        grad_hidden = norm_vjp(grad_z)[0].astype(BF16).reshape(batch, ctx, d)
        return mean_loss, embed_out, grad_hidden, grad_embed, grad_pos

    row_spec = P('dp', None)
    act_spec = P('dp', None, None)
    return jax.shard_map(device_fn, mesh=mesh, in_specs=(row_spec, row_spec, row_spec, act_spec, act_spec, P('tp', None), P(None, None), P(None), P(None)), out_specs=(P(), act_spec, act_spec, P('tp', None), P(None, None)), check_vma=False)
```

time: 1790 us -> 1080 us (0.60)
  waiting for transfers between devices: 1180 us -> 0.06 us
  Pallas kernels: 0 us -> 861 us
  matrix products: 216 us -> 0 us
  other arithmetic: 219 us -> 46.7 us
    pallas_call x0 -> x2, Pallas kernels: none -> 861 us  [the longest x1 777 us: gradients(): pl.pallas_call(functools.partial(grad_kernel, ntp, chunk, tile, zrows), o...]
    psum x1, waiting for transfers between devices: 754 us -> 0.01 us  [device_fn(): grad_pos = lax.psum(jnp.sum(grad_x0.astype(F32), axis=0), 'dp')]
    psum x1, waiting for transfers between devices: 428 us -> 0.02 us  [device_fn(): rows = lax.psum(rows, 'tp')]
    dot_general x3 -> x0, matrix products: 216 us -> none  [the longest x1 73.3 us: device_fn(): jnp.einsum('btv,btd->vd', g_bf16, z_bf16, preferred_element_type=jnp.floa...]
    scatter-add x3 -> x0, other arithmetic: 91.6 us -> none  [device_fn(): jax.ops.segment_sum(dx_f32.reshape(-1, d_model), tok_seg, num_segments=vo...]
    all_gather x0 -> x1, blocking collectives: none -> 51.7 us  [device_fn(): every = lax.all_gather(jnp.concatenate([stats, mask_f]), ('tp', 'dp'))]
    convert_element_type x4, other arithmetic: 62.2 us -> 13.2 us  [the longest x2 6.76 us: device_fn(): embed_out = (rows + pos_table.astype(F32)[None]).astype(BF16)]
    psum x2 -> x0, blocking collectives: 28.5 us -> none  [the longest x1 15.6 us: device_fn(): lax.psum((jnp.sum(shifted, axis=-1), jnp.sum(jnp.where(hit, logits, 0.0),...]
  transfers between devices with their start and end apart: 2 -> 2, of which waited for: 2 -> 0; matrix products, arithmetic and copies ran while one was open for 11% -> 4% of each run, Pallas kernels for 0% -> 80%
where the time goes in v1:
time: 1080 us
  Pallas kernels  861 us (80%)
  local copies, waits for them, and re-layouts  106 us (10%)
  blocking collectives  51.7 us (5%)
  other arithmetic  46.7 us (4%)
  between operations  16.6 us (2%)
    pallas_call x1, Pallas kernels, gradients(): pl.pallas_call(functools.partial(grad_kernel, ntp, chunk, tile, zrows), o...  777 us
    pallas_call x1, Pallas kernels, token_stats(): pl.pallas_call(functools.partial(stats_kernel, chunk, tile), grid=(steps,...  83.5 us
    gather x1, local copies, waits for them, and re-layouts, device_fn(): rows = jnp.take(embed_loc, jnp.where(tok_here, tok_local, 0), axis=0)  51.9 us
    all_gather x1, blocking collectives, device_fn(): every = lax.all_gather(jnp.concatenate([stats, mask_f]), ('tp', 'dp'))  51.7 us
    unnamed x26, local copies, waits for them, and re-layouts  48.3 us
  transfers between devices with their start and end apart: 2, of which 0 were waited for; matrix products, arithmetic and copies ran while one was open for 4% of the time, Pallas kernels for 80%

profile of v1, /device:TPU:0, one launch (start us, length us, event | category | flops | bytes accessed | tf_op | source)
XLA Modules:
  0.0 1082.2 jit_solution(16584869871658578189)
XLA Ops:
  7.2 0.0 all-reduce.3.cloned.1.call-start
  7.2 0.7 compare_and_fusion.1
  7.9 0.1 reshape.116
  8.0 51.9 %gather_fusion = bf16[1792,1280]{1,0:T(8,128)(2,1)} fusion(bf16[12992,1280]{1,0:T(8,128)(2,1)} %embed.3, s32[2048]{0:T(1024)S(1)} %pad_clamp_fusion), kind=kCustom, calls=%fused_computation | custom fusion | bytes 9182208 | tf_op jit(solution)/shard_map/jit(_take)/gather | solution.py:542
  59.9 5.9 convert_select_fusion
  65.8 0.0 copy-start.8
  65.8 0.0 copy-start.4
  65.8 0.0 copy-start.9
  65.8 0.0 copy-start.6
  65.8 0.0 all-reduce.3.cloned.1.call-update
  65.8 0.0 all-reduce.5.cloned.1.call-start
  65.9 4.6 convert_reduce_fusion.1
  70.4 0.0 all-reduce.5.cloned.1.call-update
  70.5 0.0 copy-done.8
  70.5 0.7 reshape.108.lab
  71.2 0.0 copy-done.4
  71.2 0.6 reshape.106.gain
  71.8 0.0 copy-done.9
  71.8 0.6 reshape.107.bias
  72.4 0.0 copy-done.6
  72.4 0.1 reshape.109
  72.5 83.5 %token_stats.1 = (bf16[1792,1280]{1,0:T(8,128)(2,1)}, f32[2,1792]{1,0:T(2,128)}) custom-call(bf16[1792,1280]{1,0:T(8,128)(2,1)} %bitcast.23, f32[1,1280]{1,0:T(1,128)} %reshape.106.gain, f32[1,1280]{1,0:T(1,128)} %reshape.107.bias, s32[1,1792]{1,0:T(1,128)} %reshape.108.lab, bf16[12992,1280]{1,0:T(8,128)(2,1)} %embed.3), custom_call_target="tpu_custom_call" | custom-call | flops 59601059840 | bytes 33259520 | tf_op jit(solution)/shard_map/token_stats/pallas_call | solution.py:66
  156.0 0.7 maximum_bitcast_fusion
  156.7 51.7 %all-gather.1 = f32[32,3,1792]{2,1,0:T(4,128)S(1)} all-gather(f32[1,3,1792]{2,1,0:T(4,128)S(1)} %maximum_bitcast_fusion), channel_id=2, replica_groups=mesh['tp'=4,'dp'=8] {'tp','dp'}, dimensions={0}, use_global_device_ids=true | all-gather | bytes 709632 | tf_op jit(solution)/shard_map/all_gather | solution.py:552
  208.4 0.6 slice_reduce_fusion
  209.1 0.7 slice_reduce_fusion.1
  209.8 0.7 reshape_reshape.7.tok
  210.5 0.7 reshape_reshape.6.lab
  211.2 3.0 convert_reduce_fusion
  214.1 0.7 div.47
  214.8 3.7 fusion.1
  218.5 0.7 broadcast_divide_fusion
  219.1 0.7 div.44.wgt
  219.8 0.7 add.48
  220.5 0.6 fusion.5
  221.2 0.6 constant_dynamic-slice_fusion
  221.8 0.0 copy-start.3
  221.8 0.0 copy-start.5
  221.8 777.3 %gradients.1 = (f32[12992,1280]{1,0:T(8,128)}, f32[1792,1280]{1,0:T(8,128)}, f32[29,224,1280]{2,1,0:T(8,128)}, f32[29,224,1280]{2,1,0:T(8,128)}, f32[8,3,56,1280]{3,2,1,0:T(8,128)}, /*index=5*/f32[8,3,56,1280]{3,2,1,0:T(8,128)}) custom-call(bf16[1792,1280]{1,0:T(8,128)(2,1)} %get-tuple-element.10.zb, bf16[1792,1280]{1,0:T(8,128)(2,1)} %bitcast.28, ...), custom_call_target="tpu_custom_call" | custom-call | flops 238404239360 | bytes 266076160 | tf_op jit(solution)/shard_map/gradients/pallas_call | solution.py:499
  999.0 0.0 copy-start.7
  999.1 0.0 slice-start
  999.1 0.0 copy-start
  999.1 0.0 copy-done.3
  999.1 0.0 copy-done.5
  999.1 0.0 slice-start.1
  999.1 6.7 multiply_reduce_fusion
  1005.8 0.0 copy-done.7
  1005.8 0.0 slice-done
  1005.8 2.0 copy-done
  1007.9 0.0 slice-done.1
  1007.9 5.6 fusion.6
  1013.5 0.0 copy-start.2
  1013.5 6.4 add_convert_fusion
  1021.1 0.0 copy-done.2
  1021.1 0.2 convert_element_type.27
  1021.3 0.0 all-reduce.3.cloned.1.call-done
  1021.3 6.6 add_convert_fusion.1
  1027.9 0.0 all-reduce.5.cloned.1.call-done
  1027.9 0.0 copy-start.1
  1027.9 44.9 %copy.28 = f32[12992,1280]{1,0:T(8,128)} copy(f32[12992,1280]{1,0:T(8,128)} %get-tuple-element.36) | data formatting | bytes 133038080
  1072.8 0.0 copy-done.1
  1072.8 1.4 copy.29
  (10 shorter events, 0.1 us)
Async XLA Ops:
  7.2 1014.2 %all-reduce.3.cloned.1.call-start = ((), (), s32[]{:S(2)}) async-start(), calls=%async_computation | async-start | bytes 18350080 | tf_op jit(solution)/shard_map/psum | solution.py:544
  65.8 4.7 copy-start.8
  65.8 5.4 copy-start.4
  65.8 6.0 copy-start.9
  65.8 6.6 copy-start.6
  65.8 962.1 %all-reduce.5.cloned.1.call-start = ((), (), s32[]{:S(2)}) async-start(), calls=%async_computation.1 | async-start | bytes 4587520 | tf_op jit(solution)/shard_map/psum | solution.py:546
  221.8 777.3 %copy-start.3 = (f32[1792]{0:T(1024)S(1)}, f32[1792]{0:T(1024)}, u32[]{:S(2)}) copy-start(f32[1792]{0:T(1024)} %div.47) | copy-start | bytes 21508
  221.8 777.3 %copy-start.5 = (f32[1280]{0:T(1024)S(1)}, f32[1280]{0:T(1024)}, u32[]{:S(2)}) copy-start(f32[1280]{0:T(1024)} %param.16) | copy-start | bytes 15364
  999.0 6.8 copy-start.7
  999.1 6.8 slice-start
  999.1 8.8 copy-start
  999.1 8.8 slice-start.1
  1013.5 7.7 copy-start.2
  1027.9 44.9 %copy-start.1 = (f32[448,1280]{1,0:T(8,128)S(1)}, f32[448,1280]{1,0:T(8,128)}, u32[]{:S(2)}) copy-start(f32[448,1280]{1,0:T(8,128)} %all-reduce.5.cloned.1.call-done) | copy-start | bytes 6881284
Sparse Core Ops, SparseCore 0:
  65.9 323.8 all-reduce.2
  393.7 84.6 all-reduce.4

commit v2 on v1

--- a/solution.py
+++ b/solution.py
@@ -23,9 +23,9 @@
     return 64, 128, 8
 
 
-def stats_kernel(chunk, tile, hidden, gain, bias, lab, embed, zb, stats, m_ref, s_ref, l_ref):
+def stats_kernel(chunk, tile, starts, order, skey, hidden, gain, bias, lab, embed, zb, stats, logits_out, rows_out, m_ref, s_ref, l_ref):
     step = pl.program_id(0)
-    tokens = hidden.shape[0]
+    tokens, d = hidden.shape
     tiles = tokens // tile
 
     @pl.when(step == 0)
@@ -36,17 +36,28 @@
             centered = h - jnp.mean(h, axis=-1, keepdims=True)
             var = jnp.mean(centered * centered, axis=-1, keepdims=True)
             zb[rows, :] = (centered * lax.rsqrt(var + 1e-5) * gain[...] + bias[...]).astype(BF16)
+            rows_out[rows, :] = jnp.zeros((tile, d), F32)
             return carry
         lax.fori_loop(0, tiles, norm, 0)
         m_ref[...] = jnp.full_like(m_ref, -jnp.inf)
         s_ref[...] = jnp.zeros_like(s_ref)
         l_ref[...] = jnp.zeros_like(l_ref)
 
+    def token_row(i, carry):
+        row = skey[i] - step * chunk
+        first = lax.div(row, 16) * 16
+        block = embed[pl.ds(pl.multiple_of(first, 16), 16), :].astype(F32)
+        pick = lax.broadcasted_iota(jnp.int32, (16, 1), 0) == row - first
+        rows_out[pl.ds(order[i], 1), :] = jnp.sum(jnp.where(pick, block, 0.0), axis=0, keepdims=True)
+        return carry
+    lax.fori_loop(starts[step], starts[step + 1], token_row, 0)
+
     e = embed[...]
     ids = lax.broadcasted_iota(jnp.int32, (chunk, tile), 0) + step * chunk
     for j in range(tiles):
         cols = slice(j * tile, (j + 1) * tile)
         logits = lax.dot_general(e, zb[cols, :], NT, preferred_element_type=F32)
+        logits_out[:, cols] = logits
         m_old = m_ref[:, cols]
         m_new = jnp.maximum(m_old, jnp.max(logits, axis=0, keepdims=True))
         m_ref[:, cols] = m_new
@@ -55,34 +66,46 @@
 
     @pl.when(step == pl.num_programs(0) - 1)
     def _():
-        stats[0:1, :] = m_ref[...] + jnp.log(s_ref[...])
-        stats[1:2, :] = l_ref[...]
-
-
-def token_stats(hidden, gain, bias, lab, embed, chunk, tile):
+        for j in range(tiles):
+            cols = slice(j * tile, (j + 1) * tile)
+            stats[j, 0:1, :] = m_ref[:, cols] + jnp.log(s_ref[:, cols])
+            stats[j, 1:2, :] = l_ref[:, cols]
+            stats[j, 2:8, :] = jnp.zeros((6, tile), F32)
+
+
+def token_stats(hidden, gain, bias, lab, tok, here, embed, chunk, tile):
     tokens, d = hidden.shape
-    steps = embed.shape[0] // chunk
-    whole = lambda shape: pl.BlockSpec(shape, lambda i: (0, 0))
+    vocab_loc = embed.shape[0]
+    steps = vocab_loc // chunk
+    key = jnp.where(here, tok, vocab_loc).reshape(tokens)
+    skey, order = lax.sort_key_val(key, lax.iota(jnp.int32, tokens))
+    bounds = lax.iota(jnp.int32, steps + 1) * chunk
+    starts = jnp.sum((key[None, :] < bounds[:, None]).astype(jnp.int32), axis=1)
+    whole = lambda *shape: pl.BlockSpec(shape, lambda i, *_: (0,) * len(shape))
     return pl.pallas_call(
         functools.partial(stats_kernel, chunk, tile),
-        grid=(steps,),
-        out_shape=(jax.ShapeDtypeStruct((tokens, d), BF16), jax.ShapeDtypeStruct((2, tokens), F32)),
-        in_specs=[whole((tokens, d)), whole((1, d)), whole((1, d)), whole((1, tokens)),
-                  pl.BlockSpec((chunk, d), lambda i: (i, 0))],
-        out_specs=(whole((tokens, d)), whole((2, tokens))),
-        scratch_shapes=[pltpu.VMEM((1, tokens), F32)] * 3,
+        grid_spec=pltpu.PrefetchScalarGridSpec(
+            num_scalar_prefetch=3,
+            grid=(steps,),
+            in_specs=[whole(tokens, d), whole(1, d), whole(1, d), whole(1, tokens),
+                      pl.BlockSpec((chunk, d), lambda i, *_: (i, 0))],
+            out_specs=(whole(tokens, d), whole(tokens // tile, 8, tile), pl.BlockSpec((chunk, tokens), lambda i, *_: (i, 0)),
+                       whole(tokens, d)),
+            scratch_shapes=[pltpu.VMEM((1, tokens), F32)] * 3),
+        out_shape=(jax.ShapeDtypeStruct((tokens, d), BF16), jax.ShapeDtypeStruct((tokens // tile, 8, tile), F32),
+                   jax.ShapeDtypeStruct((vocab_loc, tokens), F32), jax.ShapeDtypeStruct((tokens, d), F32)),
         compiler_params=pltpu.CompilerParams(vmem_limit_bytes=VMEM_LIMIT),
-        cost_estimate=pl.CostEstimate(flops=2 * tokens * d * embed.shape[0], bytes_accessed=2 * embed.size,
-                                      transcendentals=tokens * embed.shape[0]),
+        cost_estimate=pl.CostEstimate(flops=2 * tokens * d * vocab_loc, bytes_accessed=2 * embed.size + 4 * vocab_loc * tokens,
+                                      transcendentals=tokens * vocab_loc),
         name='token_stats',
-    )(hidden, gain, bias, lab, embed)
-
-
-def grad_kernel(ntp, chunk, tile, zrows,
-                zb, dx, lse, wgt, lab, tok, embed,
-                out, gz, own, d2d, rs_r, rs_l,
-                ebuf, gt, oh, acc, gbuf, ld_own, ld_d2d, s1, s2, fin, rs1, rs2, zin_r, zin_l, zout_r, zout_l, zfin,
-                e_sem, own_sem, d2d_s, d2d_r, ld_sem, rs1_s, rs1_r, rs2_s, rs2_r, fin_s, ag1_r, ag2_r, fwd_s, part_r,
+    )(starts, order, skey, hidden, gain, bias, lab, embed)
+
+
+def grad_kernel(ntp, ndp, chunk, tile, zrows,
+                zb, dx, stats, mask, lab, tok, embed, logits,
+                out, loss, gz, own, d2d, rs_r, rs_l,
+                lse, wgt, st_in, cnt_in, loss_in, lbuf, ebuf, gt, oh, acc, gbuf, ld_own, ld_d2d, s1, s2, fin, rs1, rs2, zin_r, zin_l, zout_r, zout_l, zfin,
+                st_s, st_r, cnt_s, cnt_r, loss_s, loss_r, l_sem, e_sem, own_sem, d2d_s, d2d_r, ld_sem, rs1_s, rs1_r, rs2_s, rs2_r, fin_s, ag1_r, ag2_r, fwd_s, part_r,
                 zld, zrs_sr, zrs_sl, zrs_rr, zrs_rl, zfin_s, zag_rr, zag_rl, zfw_r, zfw_l):
     tokens, d = zb.shape
     vocab_loc = embed.shape[0]
@@ -123,6 +146,9 @@
     def e_copy(k):
         return pltpu.make_async_copy(embed.at[rows8(k * chunk, chunk)], ebuf.at[lax.rem(k, 2)], e_sem.at[lax.rem(k, 2)])
 
+    def l_copy(k):
+        return pltpu.make_async_copy(logits.at[rows8(k * chunk, chunk)], lbuf.at[lax.rem(k, 2)], l_sem.at[lax.rem(k, 2)])
+
     def own_copy(k):
         b = lax.rem(k, 2)
         return pltpu.make_async_copy(gbuf.at[b, rows8(core * half, half)], own.at[k], own_sem.at[b])
@@ -163,25 +189,77 @@
         ref = out.at[rows8(k * chunk + core * half + (1 - a1) * quarter, quarter)]
         return rdma(ref, ref, fwd_s.at[2, lax.rem(k, RING)], part_r.at[2, k], partner)
 
+    def peer(i, n, me):
+        return lax.rem(me + i, n)
+
+    def st_copy(i, src_of):
+        return zdma(st_in.at[z], st_in.at[src_of], st_s.at[i - 1], st_r.at[src_of], peer(i, ntp, z))
+
+    def tile_copy(buf, ssem, rsem, i, src_of):
+        return rdma(buf.at[dp], buf.at[src_of], ssem.at[i - 1], rsem.at[src_of], peer(i, ndp, dp))
+
+    def share_start():
+        st_in[z] = stats[...]
+        for i in range(1, ntp):
+            st_copy(i, z).start()
+        cnt_in[dp] = jnp.broadcast_to(jnp.sum(jnp.sum(mask[...], axis=0), axis=-1, keepdims=True), (8, 128))
+        for i in range(1, ndp):
+            tile_copy(cnt_in, cnt_s, cnt_r, i, dp).start()
+
+    def in_order_sum(buf):
+        total = buf[0]
+        for i in range(1, ndp):
+            total = total + buf[i]
+        return total[0:1, 0:1]
+
+    def share_use():
+        for i in range(1, ndp):
+            tile_copy(cnt_in, cnt_s, cnt_r, i, peer(i, ndp, dp)).wait_recv()
+        for i in range(1, ntp):
+            st_copy(i, peer(i, ntp, z)).wait_recv()
+        count = in_order_sum(cnt_in)
+        part = jnp.zeros((1, tile), F32)
+        for j in range(tiles):
+            shard = [st_in[q, j] for q in range(ntp)]
+            top = functools.reduce(jnp.maximum, [a[0:1] for a in shard])
+            total = functools.reduce(jnp.add, [jnp.exp(a[0:1] - top) for a in shard])
+            lse_j = top + jnp.log(total)
+            lse[j] = lse_j
+            wgt[j] = mask[j] / count
+            part = part + mask[j] * (lse_j - functools.reduce(jnp.add, [a[1:2] for a in shard]))
+        loss_in[dp] = jnp.broadcast_to(jnp.sum(part, axis=-1, keepdims=True), (8, 128))
+        for i in range(1, ndp):
+            tile_copy(loss_in, loss_s, loss_r, i, dp).start()
+
+    def share_end():
+        for i in range(1, ndp):
+            tile_copy(loss_in, loss_s, loss_r, i, peer(i, ndp, dp)).wait_recv()
+        loss[...] = jnp.broadcast_to(in_order_sum(loss_in) / in_order_sum(cnt_in), (8, 128))
+        for i in range(1, ndp):
+            tile_copy(cnt_in, cnt_s, cnt_r, i, dp).wait_send()
+            tile_copy(loss_in, loss_s, loss_r, i, dp).wait_send()
+        for i in range(1, ntp):
+            st_copy(i, z).wait_send()
+
     def compute(k, carry):
         slot = lax.rem(k, 2)
         e_copy(k).wait()
+        l_copy(k).wait()
 
         @pl.when(k + 1 < nc)
         def _():
             e_copy(k + 1).start()
+            l_copy(k + 1).start()
 
         ids = lax.broadcasted_iota(jnp.int32, (chunk, tile), 0) + k * chunk
 
         def per_tile(j, c):
             cols = pl.ds(pl.multiple_of(j * tile, tile), tile)
-            e = ebuf[slot]
-            logits = lax.dot_general(e, zb[cols, :], NT, preferred_element_type=F32)
             hit = jnp.where(ids == lab[j], 1.0, 0.0)
-            g = ((jnp.exp(logits - lse[j]) - hit) * wgt[j]).astype(BF16)
+            g = ((jnp.exp(lbuf[slot, :, cols] - lse[j]) - hit) * wgt[j]).astype(BF16)
             gt[:, cols] = g
             oh[:, cols] = jnp.where(ids == tok[j], 1.0, 0.0).astype(BF16)
-            acc[cols, :] += lax.dot_general(g, e, TN, preferred_element_type=F32)
+            acc[cols, :] += lax.dot_general(g, ebuf[slot], TN, preferred_element_type=F32)
             return c
         lax.fori_loop(0, tiles, per_tile, 0)
 
@@ -408,7 +486,7 @@
                 def _():
                     zag(b, h, -1, zfw_l, zag_rl).start()
 
-    lead = min(8, nc)
+    lead = min(5, nc)
 
     def cs(t):
         late = t - lead
@@ -416,9 +494,16 @@
         return jnp.minimum(jnp.where(t <= lead, t, c), nc)
 
     z_start = lead + -(-(nc - lead) * 2 // 3)
-    ticks = max(nc + 13, z_start + nb + 2 * ntp)
-    acc[...] = jnp.zeros_like(acc)
+    ticks = max(nc + 9, z_start + nb + 2 * ntp)
+    share_start()
     e_copy(0).start()
+    l_copy(0).start()
+
+    def clear(j, carry):
+        acc[pl.ds(pl.multiple_of(j * tile, tile), tile), :] = jnp.zeros((tile, d), F32)
+        return carry
+    lax.fori_loop(0, tiles, clear, 0)
+    share_use()
 
     def tick(t, carry):
         ka = t - 2
@@ -427,7 +512,7 @@
         def _():
             load_start(ka)
         lax.fori_loop(cs(t), cs(t + 1), compute, 0)
-        for stage, lag in ((stage_e, 10), (stage_d, 8), (stage_c, 6), (stage_b, 4), (stage_a, 2), (stage_f, 12)):
+        for stage, lag in ((stage_e, 7), (stage_d, 6), (stage_c, 5), (stage_b, 4), (stage_a, 2), (stage_f, 8)):
             @pl.when(valid(t - lag))
             def _(stage=stage, lag=lag):
                 stage(t - lag)
@@ -450,6 +535,8 @@
                 z_hop(zt - (ntp - 1) - h, h)
         return carry
     lax.fori_loop(0, ticks, tick, 0)
+
+    share_end()
 
     for k in range(max(nc - RING, 0), nc):
         rs1_copy(k).wait_send()
@@ -483,11 +570,12 @@
     lax.fori_loop(0, nb, drain, 0)
 
 
-def gradients(ntp, zb, dx, lse, wgt, lab, tok, embed, chunk, tile, zrows):
+def gradients(ntp, ndp, zb, dx, stats, mask, lab, tok, embed, logits, chunk, tile, zrows):
     tokens, d = zb.shape
     vocab_loc = embed.shape[0]
     nc = vocab_loc // chunk
     half, quarter, eighth = chunk // 2, chunk // 4, chunk // 8
+    tiles = tokens // tile
     nb = tokens // ntp // zrows
     vm = pl.BlockSpec(memory_space=pltpu.VMEM)
     hbm = pl.BlockSpec(memory_space=pl.ANY)
@@ -495,30 +583,33 @@
     vf = lambda *s: pltpu.VMEM(s, F32)
     sds = lambda *s: jax.ShapeDtypeStruct(s, F32)
     flops = 2 * tokens * d * vocab_loc
-    rows = lambda a: a.reshape(tokens // tile, 1, tile)
+    rows = lambda a: a.reshape(tiles, 1, tile)
     res = pl.pallas_call(
-        functools.partial(grad_kernel, ntp, chunk, tile, zrows),
-        out_shape=(sds(vocab_loc, d), sds(tokens, d), sds(nc, half, d), sds(nc, half, d),
+        functools.partial(grad_kernel, ntp, ndp, chunk, tile, zrows),
+        out_shape=(sds(vocab_loc, d), sds(8, 128), sds(tokens, d), sds(nc, half, d), sds(nc, half, d),
                    sds(nb, ntp - 1, zrows, d), sds(nb, ntp - 1, zrows, d)),
-        in_specs=[vm] * 6 + [hbm],
-        out_specs=(hbm,) * 6,
+        in_specs=[vm] * 6 + [hbm] * 2,
+        out_specs=(hbm, vm) + (hbm,) * 5,
         scratch_shapes=[
+            vf(tiles, 1, tile), vf(tiles, 1, tile), vf(ntp, tiles, 8, tile), vf(ndp, 8, 128), vf(ndp, 8, 128),
+            vf(2, chunk, tokens),
             pltpu.VMEM((2, chunk, d), BF16), pltpu.VMEM((chunk, tokens), BF16), pltpu.VMEM((chunk, tokens), BF16),
             vf(tokens, d), vf(2, chunk, d), vf(half, d), vf(half, d),
             vf(RING, half, d), vf(RING, quarter, d), vf(RING, eighth, d), vf(SLOTS, quarter, d), vf(SLOTS, eighth, d),
             vf(ntp - 1, zrows, d), vf(ntp - 1, zrows, d), vf(2, ntp - 1, zrows, d), vf(2, ntp - 1, zrows, d),
             vf(2, zrows, d),
+            dma(ntp - 1), dma(ntp), dma(ndp - 1), dma(ndp), dma(ndp - 1), dma(ndp), dma(2),
             dma(2), dma(2), dma(2), dma(nc), dma(2), dma(RING), dma(SLOTS), dma(RING), dma(SLOTS), dma(4, RING),
             dma(nc), dma(2, nc), dma(3, RING), dma(3, nc),
             dma(1), dma(2), dma(2), dma(nb), dma(nb), dma(3, 2), dma(nb, ntp - 1), dma(nb, ntp - 1),
             dma(nb, ntp - 1), dma(nb, ntp - 1),
         ],
         compiler_params=pltpu.CompilerParams(vmem_limit_bytes=VMEM_LIMIT, has_side_effects=True),
-        cost_estimate=pl.CostEstimate(flops=4 * flops, bytes_accessed=4 * vocab_loc * d * 4,
+        cost_estimate=pl.CostEstimate(flops=3 * flops, bytes_accessed=4 * vocab_loc * (4 * d + tokens),
                                       transcendentals=tokens * vocab_loc),
         name='gradients',
-    )(zb, dx, rows(lse), rows(wgt), rows(lab), rows(tok), embed)
-    return res[0], res[1]
+    )(zb, dx, stats, rows(mask), rows(lab), rows(tok), embed, logits)
+    return res[:3]
 
 
 def layer_norm(h_f32, ln_gain, ln_bias):
@@ -537,31 +628,19 @@
         ntok = batch * ctx
         chunk, tile, zrows = sizes(ntok, vocab_loc)
         shard_start = lax.axis_index('tp') * vocab_loc
-        tok_local = tokens - shard_start
+        tok_local = (tokens - shard_start).reshape(1, ntok)
+        lab_local = (labels - shard_start).reshape(1, ntok)
         tok_here = (tok_local >= 0) & (tok_local < vocab_loc)
-        rows = jnp.take(embed_loc, jnp.where(tok_here, tok_local, 0), axis=0)
-        rows = jnp.where(tok_here[..., None], rows.astype(F32), 0.0)
-        rows = lax.psum(rows, 'tp')
+        grad_pos = lax.psum(jnp.sum(grad_x0.astype(F32), axis=0), 'dp')
+
+        hidden2 = hidden.reshape(ntok, d)
+        zb, stats, logits, rows = token_stats(hidden2, ln_gain.reshape(1, d), ln_bias.reshape(1, d), lab_local, tok_local,
+                                              tok_here, embed_loc, chunk, tile)
+        rows = lax.psum(rows, 'tp').reshape(batch, ctx, d)
         embed_out = (rows + pos_table.astype(F32)[None]).astype(BF16)
-        grad_pos = lax.psum(jnp.sum(grad_x0.astype(F32), axis=0), 'dp')
-
-        lab_local = (labels - shard_start).reshape(1, ntok)
-        hidden2 = hidden.reshape(ntok, d)
-        zb, stats = token_stats(hidden2, ln_gain.reshape(1, d), ln_bias.reshape(1, d), lab_local, embed_loc, chunk, tile)
-        mask_f = lossmask.astype(F32).reshape(1, ntok)
-        every = lax.all_gather(jnp.concatenate([stats, mask_f]), ('tp', 'dp'))
-        every = every.reshape(ntp, ndp, 3, ntok)
-        top = jnp.max(every[:, :, 0], axis=0)
-        lse_all = top + jnp.log(jnp.sum(jnp.exp(every[:, :, 0] - top), axis=0))
-        lab_all = jnp.sum(every[:, :, 1], axis=0)
-        mask_all = every[0, :, 2]
-        count = jnp.sum(mask_all)
-        mean_loss = jnp.sum(mask_all * (lse_all - lab_all)) / count
-        lse = lax.dynamic_index_in_dim(lse_all, lax.axis_index('dp'), 0, keepdims=True)
-        wgt = mask_f / count
-
-        grad_embed, grad_z = gradients(ntp, zb, grad_x0.reshape(ntok, d), lse, wgt, lab_local, tok_local.reshape(1, ntok),
-                                       embed_loc, chunk, tile, zrows)
+        grad_embed, loss, grad_z = gradients(ntp, ndp, zb, grad_x0.reshape(ntok, d), stats, lossmask.astype(F32), lab_local,
+                                             tok_local, embed_loc, logits, chunk, tile, zrows)
+        mean_loss = loss[0, 0]
         norm_vjp = jax.vjp(lambda h: layer_norm(h, ln_gain, ln_bias), hidden2.astype(F32))[1]
         grad_hidden = norm_vjp(grad_z)[0].astype(BF16).reshape(batch, ctx, d)
         return mean_loss, embed_out, grad_hidden, grad_embed, grad_pos

time: 1080 us -> 898 us (0.83)
  Pallas kernels: 861 us -> 782 us
  blocking collectives: 51.7 us -> 0 us
  local copies, waits for them, and re-layouts: 106 us -> 56.3 us
    pallas_call x2, Pallas kernels: 861 us -> 782 us  [the longest x1 676 us: gradients(): pl.pallas_call(functools.partial(grad_kernel, ntp, ndp, chunk, tile, zrow...]
    gather x1 -> x0, local copies, waits for them, and re-layouts: 51.9 us -> none  [device_fn(): rows = jnp.take(embed_loc, jnp.where(tok_here, tok_local, 0), axis=0)]
    all_gather x1 -> x0, blocking collectives: 51.7 us -> none  [device_fn(): every = lax.all_gather(jnp.concatenate([stats, mask_f]), ('tp', 'dp'))]
    unnamed x26 -> x20, local copies, waits for them, and re-layouts: 48.3 us -> 48.3 us
  transfers between devices with their start and end apart: 2 -> 2, of which waited for: 0 -> 0; matrix products, arithmetic and copies ran while one was open for 4% -> 5% of each run, Pallas kernels for 80% -> 75%
where the time goes in v2:
time: 898 us; the launch traced here: 896 us
  Pallas kernels  782 us (87%)
  local copies, waits for them, and re-layouts  56.3 us (6%)
  other arithmetic  43.2 us (5%)
  between operations  14.2 us (2%)
    pallas_call x1, Pallas kernels, gradients(): pl.pallas_call(functools.partial(grad_kernel, ntp, ndp, chunk, tile, zrow...  676 us
    pallas_call x1, Pallas kernels, token_stats(): pl.pallas_call(functools.partial(stats_kernel, chunk, tile), grid_spec=pl...  106 us
    unnamed x20, local copies, waits for them, and re-layouts  48.3 us
  transfers between devices with their start and end apart: 2, of which 0 were waited for; matrix products, arithmetic and copies ran while one was open for 5% of the time, Pallas kernels for 75%

profile of v2, /device:TPU:0, one launch (start us, length us, event | category | flops | bytes accessed | tf_op | source)
XLA Modules:
  0.0 895.7 jit_solution(684810517050539637)
XLA Ops:
  7.2 0.0 all-reduce.3.cloned.1.call-start
  7.2 1.3 reshape.116.bias
  8.5 1.3 reshape.115.gain
  9.8 0.7 broadcast_subtract_fusion
  10.5 0.7 reshape.117.lab
  11.2 0.1 reshape.113
  11.3 0.7 convert_reduce_fusion.2.starts
  12.0 5.0 sort.15
  17.1 106.3 %token_stats.1 = (bf16[1792,1280]{1,0:T(8,128)(2,1)}, f32[7,8,256]{2,1,0:T(8,128)}, f32[12992,1792]{1,0:T(8,128)}, f32[1792,1280]{1,0:T(8,128)}) custom-call(s32[30]{0:T(128)} %convert_reduce_fusion.2.starts, s32[1792]{0:T(1024)} %get-tuple-element.14.order, s32[1792]{0:T(1024)} %get-tuple-element.15.skey, bf16[1792,1280]{1,0:T(8,128)(2,1)} %bitcast.8, ...), custom_call_target="tpu_custom_call" | custom-call | flops 59601059840 | bytes 126386176 | tf_op jit(solution)/shard_map/token_stats/pallas_call | solution.py:85
  123.4 0.0 all-reduce.3.cloned.1.call-update
  123.4 0.0 copy-start.6
  123.4 0.0 all-reduce.5.cloned.1.call-start
  123.5 4.6 convert_reduce_fusion.1
  128.0 0.0 all-reduce.5.cloned.1.call-update
  128.1 3.0 convert_reduce_fusion
  131.1 0.7 div.22
  131.7 3.7 fusion.1
  135.4 0.7 reshape_reshape.6.lab
  136.1 0.7 reshape_reshape.7.tok
  136.8 0.0 copy-done.6
  136.8 0.7 reshape.119.mask
  137.5 0.7 add.32
  138.1 0.0 copy-start.3
  138.1 0.0 copy-start.4
  138.1 675.7 %gradients.1 = (f32[12992,1280]{1,0:T(8,128)}, f32[8,128]{1,0:T(8,128)}, f32[1792,1280]{1,0:T(8,128)}, f32[29,224,1280]{2,1,0:T(8,128)}, f32[29,224,1280]{2,1,0:...) custom-call(bf16[1792,1280]{1,0:T(8,128)(2,1)} %get-tuple-element.16.zb, bf16[1792,1280]{1,0:T(8,128)(2,1)} %bitcast.13, ...), custom_call_target="tpu_custom_call" | custom-call | flops 178803179520 | bytes 359202816 | tf_op jit(solution)/shard_map/gradients/pallas_call | solution.py:587
  813.8 0.0 copy-start.5
  813.8 0.0 slice-start
  813.8 0.0 copy-start
  813.8 0.0 copy-done.3
  813.8 0.0 copy-done.4
  813.9 0.0 slice-start.1
  813.9 6.7 multiply_reduce_fusion
  820.6 0.0 copy-done.5
  820.6 0.0 slice-done
  820.6 2.0 copy-done
  822.6 0.0 slice-done.1
  822.6 5.6 fusion.2
  828.2 0.0 copy-start.2
  828.2 6.4 add_convert_fusion
  834.6 0.0 copy-done.2
  834.6 0.1 convert_element_type.27
  834.8 1.2 slice.3
  836.0 0.0 all-reduce.3.cloned.1.call-done
  836.0 6.6 add_convert_fusion.1
  842.6 0.0 all-reduce.5.cloned.1.call-done
  842.6 0.0 copy-start.1
  842.6 44.9 %copy.17 = f32[12992,1280]{1,0:T(8,128)} copy(f32[12992,1280]{1,0:T(8,128)} %get-tuple-element.37) | data formatting | bytes 133038080
  887.5 0.0 copy-done.1
  887.5 1.4 copy.18
  (9 shorter events, 0.0 us)
Async XLA Ops:
  7.2 828.8 %all-reduce.3.cloned.1.call-start = ((), (), s32[]{:S(2)}) async-start(), calls=%async_computation | async-start | bytes 18350080 | tf_op jit(solution)/shard_map/psum | solution.py:639
  123.4 13.3 %copy-start.6 = (s32[4,448]{1,0:T(4,128)S(1)}, s32[4,448]{1,0:T(4,128)}, u32[]{:S(2)}) copy-start(s32[4,448]{1,0:T(4,128)} %param.11) | copy-start | bytes 21508
  123.4 719.1 %all-reduce.5.cloned.1.call-start = ((), (), s32[]{:S(2)}) async-start(), calls=%async_computation.1 | async-start | bytes 4587520 | tf_op jit(solution)/shard_map/psum | solution.py:634
  138.1 675.7 %copy-start.3 = (f32[1792]{0:T(1024)S(1)}, f32[1792]{0:T(1024)}, u32[]{:S(2)}) copy-start(f32[1792]{0:T(1024)} %div.22) | copy-start | bytes 21508
  138.1 675.7 %copy-start.4 = (f32[1280]{0:T(1024)S(1)}, f32[1280]{0:T(1024)}, u32[]{:S(2)}) copy-start(f32[1280]{0:T(1024)} %param.16) | copy-start | bytes 15364
  813.8 6.8 copy-start.5
  813.8 6.8 slice-start
  813.8 8.8 copy-start
  813.9 8.8 slice-start.1
  828.2 6.4 copy-start.2
  842.6 44.9 %copy-start.1 = (f32[448,1280]{1,0:T(8,128)S(1)}, f32[448,1280]{1,0:T(8,128)}, u32[]{:S(2)}) copy-start(f32[448,1280]{1,0:T(8,128)} %all-reduce.5.cloned.1.call-done) | copy-start | bytes 6881284
Sparse Core Ops, SparseCore 0:
  123.5 322.2 all-reduce.2
  449.7 84.7 all-reduce.4

commit v3 on v2

--- a/solution.py
+++ b/solution.py
@@ -14,13 +14,14 @@
 TN = (((0,), (0,)), ((), ()))
 RING = 4
 SLOTS = 8
+STEPS = 2
 VMEM_LIMIT = 66_000_000
 
 
 def sizes(tokens, vocab_loc):
     if vocab_loc % 448 == 0 and tokens % 1792 == 0:
-        return 448, 256, 56
-    return 64, 128, 8
+        return (928 if vocab_loc % 928 == 0 else 448), 448, 256, 32
+    return 64, 64, 128, 8
 
 
 def stats_kernel(chunk, tile, starts, order, skey, hidden, gain, bias, lab, embed, zb, stats, logits_out, rows_out, m_ref, s_ref, l_ref):
@@ -43,21 +44,31 @@
         s_ref[...] = jnp.zeros_like(s_ref)
         l_ref[...] = jnp.zeros_like(l_ref)
 
-    def token_row(i, carry):
-        row = skey[i] - step * chunk
-        first = lax.div(row, 16) * 16
-        block = embed[pl.ds(pl.multiple_of(first, 16), 16), :].astype(F32)
-        pick = lax.broadcasted_iota(jnp.int32, (16, 1), 0) == row - first
-        rows_out[pl.ds(order[i], 1), :] = jnp.sum(jnp.where(pick, block, 0.0), axis=0, keepdims=True)
+    first_tok, end_tok = starts[step], starts[step + 1]
+
+    def token_rows(n, carry):
+        for u in range(4):
+            i = jnp.minimum(first_tok + n * 4 + u, end_tok - 1)
+            row = skey[i] - step * chunk
+            group = lax.div(row, 16) * 16
+            block = embed[pl.ds(pl.multiple_of(group, 16), 16), :].astype(F32)
+            pick = lax.broadcasted_iota(jnp.int32, (16, 1), 0) == row - group
+            rows_out[pl.ds(order[i], 1), :] = jnp.sum(jnp.where(pick, block, 0.0), axis=0, keepdims=True)
         return carry
-    lax.fori_loop(starts[step], starts[step + 1], token_row, 0)
-
-    e = embed[...]
+    lax.fori_loop(0, lax.div(end_tok - first_tok + 3, 4), token_rows, 0)
+
     ids = lax.broadcasted_iota(jnp.int32, (chunk, tile), 0) + step * chunk
+
+    def product(j):
+        cols = slice(j * tile, (j + 1) * tile)
+        logits_out[:, cols] = lax.dot_general(embed[...], zb[cols, :], NT, preferred_element_type=F32)
+
+    product(0)
     for j in range(tiles):
         cols = slice(j * tile, (j + 1) * tile)
-        logits = lax.dot_general(e, zb[cols, :], NT, preferred_element_type=F32)
-        logits_out[:, cols] = logits
+        if j + 1 < tiles:
+            product(j + 1)
+        logits = logits_out[:, cols]
         m_old = m_ref[:, cols]
         m_new = jnp.maximum(m_old, jnp.max(logits, axis=0, keepdims=True))
         m_ref[:, cols] = m_new
@@ -81,16 +92,14 @@
     skey, order = lax.sort_key_val(key, lax.iota(jnp.int32, tokens))
     bounds = lax.iota(jnp.int32, steps + 1) * chunk
     starts = jnp.sum((key[None, :] < bounds[:, None]).astype(jnp.int32), axis=1)
-    whole = lambda *shape: pl.BlockSpec(shape, lambda i, *_: (0,) * len(shape))
+    whole = pl.BlockSpec(memory_space=pltpu.VMEM)
     return pl.pallas_call(
         functools.partial(stats_kernel, chunk, tile),
         grid_spec=pltpu.PrefetchScalarGridSpec(
             num_scalar_prefetch=3,
             grid=(steps,),
-            in_specs=[whole(tokens, d), whole(1, d), whole(1, d), whole(1, tokens),
-                      pl.BlockSpec((chunk, d), lambda i, *_: (i, 0))],
-            out_specs=(whole(tokens, d), whole(tokens // tile, 8, tile), pl.BlockSpec((chunk, tokens), lambda i, *_: (i, 0)),
-                       whole(tokens, d)),
+            in_specs=[whole, whole, whole, whole, pl.BlockSpec((chunk, d), lambda i, *_: (i, 0))],
+            out_specs=(whole, whole, pl.BlockSpec((chunk, tokens), lambda i, *_: (i, 0)), whole),
             scratch_shapes=[pltpu.VMEM((1, tokens), F32)] * 3),
         out_shape=(jax.ShapeDtypeStruct((tokens, d), BF16), jax.ShapeDtypeStruct((tokens // tile, 8, tile), F32),
                    jax.ShapeDtypeStruct((vocab_loc, tokens), F32), jax.ShapeDtypeStruct((tokens, d), F32)),
@@ -102,16 +111,17 @@
 
 
 def grad_kernel(ntp, ndp, chunk, tile, zrows,
-                zb, dx, stats, mask, lab, tok, embed, logits,
-                out, loss, gz, own, d2d, rs_r, rs_l,
-                lse, wgt, st_in, cnt_in, loss_in, lbuf, ebuf, gt, oh, acc, gbuf, ld_own, ld_d2d, s1, s2, fin, rs1, rs2, zin_r, zin_l, zout_r, zout_l, zfin,
-                st_s, st_r, cnt_s, cnt_r, loss_s, loss_r, l_sem, e_sem, own_sem, d2d_s, d2d_r, ld_sem, rs1_s, rs1_r, rs2_s, rs2_r, fin_s, ag1_r, ag2_r, fwd_s, part_r,
+                zb, dx, stats, mask, lab, tok, gain, hidden, embed, logits,
+                out, loss, gz, own, d2d, rs_r, rs_l, gsave,
+                lse, wgt, st_in, cnt_in, loss_in, lbuf, ebuf, gz_t, hbuf, gt, oh, acc, gbuf, ld_own, ld_d2d, s1, s2, fin, rs1, rs2, zin_r, zin_l, zout_r, zout_l, zfin,
+                st_s, st_r, cnt_s, cnt_r, loss_s, loss_r, l_sem, e_sem, gs_sem, gl_sem, h_sem, own_sem, d2d_s, d2d_r, ld_sem, rs1_s, rs1_r, rs2_s, rs2_r, fin_s, ag1_r, ag2_r, fwd_s, part_r,
                 zld, zrs_sr, zrs_sl, zrs_rr, zrs_rl, zfin_s, zag_rr, zag_rl, zfw_r, zfw_l):
     tokens, d = zb.shape
     vocab_loc = embed.shape[0]
     nc = vocab_loc // chunk
     tiles = tokens // tile
     ntile = 256 if d % 256 == 0 and d > 256 else 128
+    ntiles = d // ntile
     half, quarter, eighth = chunk // 2, chunk // 4, chunk // 8
     dp, z = lax.axis_index('dp'), lax.axis_index('tp')
     core = lax.rem(dp, 2)
@@ -149,13 +159,18 @@
     def l_copy(k):
         return pltpu.make_async_copy(logits.at[rows8(k * chunk, chunk)], lbuf.at[lax.rem(k, 2)], l_sem.at[lax.rem(k, 2)])
 
+    def gs_copy(k):
+        b = lax.rem(k, 2)
+        return pltpu.make_async_copy(gz_t.at[b], gsave.at[k], gs_sem.at[b])
+
+    def gl_copy(k):
+        return pltpu.make_async_copy(gsave.at[k], gt, gl_sem.at[0])
+
     def own_copy(k):
-        b = lax.rem(k, 2)
-        return pltpu.make_async_copy(gbuf.at[b, rows8(core * half, half)], own.at[k], own_sem.at[b])
+        return pltpu.make_async_copy(gbuf.at[rows8(core * half, half)], own.at[k], own_sem.at[0])
 
     def d2d_copy(k):
-        b = lax.rem(k, 2)
-        return rdma(gbuf.at[b, rows8((1 - core) * half, half)], d2d.at[k], d2d_s.at[b], d2d_r.at[k], partner)
+        return rdma(gbuf.at[rows8((1 - core) * half, half)], d2d.at[k], d2d_s.at[0], d2d_r.at[k], partner)
 
     def rs1_copy(k):
         n1, _, a1, _ = place(k)
@@ -241,46 +256,69 @@
         for i in range(1, ntp):
             st_copy(i, z).wait_send()
 
-    def compute(k, carry):
+    def z_unit(u, carry):
+        k, j = lax.div(u, tiles), lax.rem(u, tiles)
         slot = lax.rem(k, 2)
-        e_copy(k).wait()
-        l_copy(k).wait()
-
-        @pl.when(k + 1 < nc)
-        def _():
-            e_copy(k + 1).start()
-            l_copy(k + 1).start()
-
+
+        @pl.when(j == 0)
+        def _():
+            e_copy(k).wait()
+            l_copy(k).wait()
+
+            @pl.when(k + 1 < nc)
+            def _():
+                e_copy(k + 1).start()
+                l_copy(k + 1).start()
+
+            @pl.when(k >= 1)
+            def _():
+                gs_copy(k - 1).wait()
+        cols = pl.ds(pl.multiple_of(j * tile, tile), tile)
         ids = lax.broadcasted_iota(jnp.int32, (chunk, tile), 0) + k * chunk
-
-        def per_tile(j, c):
-            cols = pl.ds(pl.multiple_of(j * tile, tile), tile)
-            hit = jnp.where(ids == lab[j], 1.0, 0.0)
-            g = ((jnp.exp(lbuf[slot, :, cols] - lse[j]) - hit) * wgt[j]).astype(BF16)
-            gt[:, cols] = g
-            oh[:, cols] = jnp.where(ids == tok[j], 1.0, 0.0).astype(BF16)
-            acc[cols, :] += lax.dot_general(g, ebuf[slot], TN, preferred_element_type=F32)
-            return c
-        lax.fori_loop(0, tiles, per_tile, 0)
-
-        @pl.when(k >= 1)
-        def _():
-            own_copy(k - 1).wait()
-            d2d_copy(k - 1).wait_send()
-
-        def per_cols(n, c):
-            cols = pl.ds(pl.multiple_of(n * ntile, ntile), ntile)
-            gbuf[slot, :, cols] = (jnp.dot(gt[...], zb[:, cols], preferred_element_type=F32)
-                                   + jnp.dot(oh[...], dx[:, cols], preferred_element_type=F32))
-            return c
-        lax.fori_loop(0, d // ntile, per_cols, 0)
-        own_copy(k).start()
-        d2d_copy(k).start()
-
-        @pl.when(k == nc - 1)
-        def _():
-            own_copy(k).wait()
-            d2d_copy(k).wait_send()
+        hit = jnp.where(ids == lab[j], 1.0, 0.0)
+        g = ((jnp.exp(lbuf[slot, :, cols] - lse[j]) - hit) * wgt[j]).astype(BF16)
+        gz_t[slot, :, cols] = g
+        acc[cols, :] += lax.dot_general(g, ebuf[slot], TN, preferred_element_type=F32)
+
+        @pl.when(j == tiles - 1)
+        def _():
+            gs_copy(k).start()
+
+            @pl.when(k == nc - 1)
+            def _():
+                gs_copy(k).wait()
+        return carry
+
+    def g_unit(u, carry):
+        k, n = lax.div(u, ntiles), lax.rem(u, ntiles)
+
+        @pl.when(n == 0)
+        def _():
+            def one_hot(j, c):
+                cols = pl.ds(pl.multiple_of(j * tile, tile), tile)
+                ids = lax.broadcasted_iota(jnp.int32, (chunk, tile), 0) + k * chunk
+                oh[:, cols] = jnp.where(ids == tok[j], 1.0, 0.0).astype(BF16)
+                return c
+            lax.fori_loop(0, tiles, one_hot, 0)
+
+            @pl.when(k >= 1)
+            def _():
+                own_copy(k - 1).wait()
+                d2d_copy(k - 1).wait_send()
+            gl_copy(k).wait()
+        cols = pl.ds(pl.multiple_of(n * ntile, ntile), ntile)
+        gbuf[:, cols] = (jnp.dot(gt[...], zb[:, cols], preferred_element_type=F32)
+                         + jnp.dot(oh[...], dx[:, cols], preferred_element_type=F32))
+
+        @pl.when(n == ntiles - 1)
+        def _():
+            own_copy(k).start()
+            d2d_copy(k).start()
+
+            @pl.when(k == nc - 1)
+            def _():
+                own_copy(k).wait()
+                d2d_copy(k).wait_send()
         return carry
 
     def load_start(k):
@@ -343,8 +381,10 @@
         for c in fwd_copies(k):
             c.start()
 
+    def stage_w(k):
+        fin_copies(k)[2].wait_recv()
+
     def stage_e(k):
-        fin_copies(k)[2].wait_recv()
         fwd_copies(k)[0].wait_recv()
 
         @pl.when(k >= RING)
@@ -365,11 +405,11 @@
 
     def right_copy(b, i, src=None):
         n = ntp - 1 - i
-        s = zout_r.at[lax.rem(b, 2), pl.ds(i, n)] if src is None else src
-        return zdma(s, rs_r.at[b, pl.ds(i, n)], zrs_sr.at[lax.rem(b, 2)], zrs_rr.at[b], i + 1)
+        s = zout_r.at[lax.rem(b, RING), pl.ds(i, n)] if src is None else src
+        return zdma(s, rs_r.at[b, pl.ds(i, n)], zrs_sr.at[lax.rem(b, RING)], zrs_rr.at[b], i + 1)
 
     def left_copy(b, i):
-        return zdma(zout_l.at[lax.rem(b, 2), pl.ds(0, i)], rs_l.at[b, pl.ds(0, i)], zrs_sl.at[lax.rem(b, 2)],
+        return zdma(zout_l.at[lax.rem(b, RING), pl.ds(0, i)], rs_l.at[b, pl.ds(0, i)], zrs_sl.at[lax.rem(b, RING)],
                     zrs_rl.at[b], i - 1)
 
     def z_right(b):
@@ -383,12 +423,12 @@
                     load.start()
                     load.wait()
 
-                @pl.when(b >= 2)
+                @pl.when(b >= RING)
                 def _():
-                    right_copy(b - 2, i).wait_send()
+                    right_copy(b - RING, i).wait_send()
                 for q in range(i + 1, ntp):
                     mine = acc[pl.ds(zacc(q, b), zrows), :]
-                    zout_r[lax.rem(b, 2), q - 1] = mine if i == 0 else zin_r[q - 1] + mine
+                    zout_r[lax.rem(b, RING), q - 1] = mine if i == 0 else zin_r[q - 1] + mine
                 right_copy(b, i).start()
 
     def z_left(b):
@@ -401,22 +441,24 @@
                     load.start()
                     load.wait()
 
-                @pl.when(b >= 2)
+                @pl.when(b >= RING)
                 def _():
-                    left_copy(b - 2, i).wait_send()
+                    left_copy(b - RING, i).wait_send()
                 for q in range(i):
                     mine = acc[pl.ds(zacc(q, b), zrows), :]
-                    zout_l[lax.rem(b, 2), q] = mine if i == ntp - 1 else zin_l[q] + mine
+                    zout_l[lax.rem(b, RING), q] = mine if i == ntp - 1 else zin_l[q] + mine
                 left_copy(b, i).start()
 
     def zfin_copies(b):
-        s = lax.rem(b, 2)
+        s = lax.rem(b, RING)
         dst = gz.at[rows8(z * qrows + b * zrows, zrows)]
         return (pltpu.make_async_copy(zfin.at[s], dst, zfin_s.at[0, s]),
                 zdma(zfin.at[s], dst, zfin_s.at[1, s], zag_rr.at[b, 0], z + 1),
                 zdma(zfin.at[s], dst, zfin_s.at[2, s], zag_rl.at[b, 0], z - 1))
 
     def z_final(b):
+        load_h = pltpu.make_async_copy(hidden.at[rows8(z * qrows + b * zrows, zrows)], hbuf, h_sem.at[0])
+        load_h.start()
         for i in range(ntp):
             @pl.when(z == i)
             def _(i=i):
@@ -430,13 +472,21 @@
                     load = pltpu.make_async_copy(rs_l.at[b, i], zin_l.at[i], zld.at[0])
                     load.start()
                     load.wait()
-                z_wait_fin(b - 2, b >= 2)
+                z_wait_fin(b - RING, b >= RING)
                 total = acc[pl.ds(zacc(i, b), zrows), :]
                 if i > 0:
                     total = zin_r[i - 1] + total
                 if i < ntp - 1:
                     total = total + zin_l[i]
-                zfin[lax.rem(b, 2)] = total
+                zfin[lax.rem(b, RING)] = total
+        load_h.wait()
+        h = hbuf[...].astype(F32)
+        centered = h - jnp.mean(h, axis=-1, keepdims=True)
+        rstd = lax.rsqrt(jnp.mean(centered * centered, axis=-1, keepdims=True) + 1e-5)
+        unit = centered * rstd
+        dy = zfin[lax.rem(b, RING)] * gain[...]
+        zfin[lax.rem(b, RING)] = rstd * (dy - jnp.mean(dy, axis=-1, keepdims=True)
+                                         - unit * jnp.mean(dy * unit, axis=-1, keepdims=True))
         copies = zfin_copies(b)
         copies[0].start()
 
@@ -486,15 +536,26 @@
                 def _():
                     zag(b, h, -1, zfw_l, zag_rl).start()
 
-    lead = min(5, nc)
-
-    def cs(t):
-        late = t - lead
-        c = lead + lax.div(late * 3, 2)
-        return jnp.minimum(jnp.where(t <= lead, t, c), nc)
-
-    z_start = lead + -(-(nc - lead) * 2 // 3)
-    ticks = max(nc + 9, z_start + nb + 2 * ntp)
+    lead = min(7, nc)
+    g_first = STEPS + 1
+    nz, ng = nc * tiles, nc * ntiles
+    fast = (tiles * 12) // 7
+
+    def uz(i):
+        late = i - lead * STEPS
+        return jnp.minimum(lax.div(jnp.minimum(i, lead * STEPS) * tiles + jnp.maximum(late, 0) * fast, STEPS), nz)
+
+    def ug(i):
+        return jnp.minimum(lax.div(jnp.maximum(i - g_first, 0) * ntiles, STEPS), ng)
+
+    base = g_first + STEPS
+    lags = (('w', base + 16), ('f', base + 26), ('e', base + 22), ('d', base + 12), ('c', base + 8), ('b', base + 5),
+            ('a', base + 1), ('p', base))
+    stages = {'w': stage_w, 'f': stage_f, 'e': stage_e, 'd': stage_d, 'c': stage_c, 'b': stage_b, 'a': stage_a,
+              'p': load_start}
+    z_start = lead * STEPS + -(-(nz - lead * tiles) * STEPS // fast)
+    hop = 3
+    steps = max((nc - 1) * STEPS + base + 27, z_start + nb + hop * 2 * (ntp - 1))
     share_start()
     e_copy(0).start()
     l_copy(0).start()
@@ -505,36 +566,37 @@
     lax.fori_loop(0, tiles, clear, 0)
     share_use()
 
-    def tick(t, carry):
-        ka = t - 2
-
-        @pl.when(valid(ka))
-        def _():
-            load_start(ka)
-        lax.fori_loop(cs(t), cs(t + 1), compute, 0)
-        for stage, lag in ((stage_e, 7), (stage_d, 6), (stage_c, 5), (stage_b, 4), (stage_a, 2), (stage_f, 8)):
-            @pl.when(valid(t - lag))
-            def _(stage=stage, lag=lag):
-                stage(t - lag)
-        zt = t - z_start
-
-        @pl.when(valid(zt - z, nb))
-        def _():
-            z_right(zt - z)
-
-        @pl.when(valid(zt - (ntp - 1 - z), nb))
-        def _():
-            z_left(zt - (ntp - 1 - z))
-
-        @pl.when(valid(zt - (ntp - 1), nb))
-        def _():
-            z_final(zt - (ntp - 1))
+    def one_step(i, carry):
+        gk = i - g_first
+
+        @pl.when((gk >= 0) & (gk < nc * STEPS) & (lax.rem(gk, STEPS) == 0))
+        def _():
+            gl_copy(lax.div(gk, STEPS)).start()
+        lax.fori_loop(uz(i), uz(i + 1), z_unit, 0)
+        lax.fori_loop(ug(i), ug(i + 1), g_unit, 0)
+        for name, lag in lags:
+            @pl.when((i >= lag) & (i - lag < nc * STEPS) & (lax.rem(i - lag + STEPS * 64, STEPS) == 0))
+            def _(name=name, lag=lag):
+                stages[name](lax.div(i - lag, STEPS))
+        zt = i - z_start
+
+        @pl.when(valid(zt - hop * z, nb))
+        def _():
+            z_right(zt - hop * z)
+
+        @pl.when(valid(zt - hop * (ntp - 1 - z), nb))
+        def _():
+            z_left(zt - hop * (ntp - 1 - z))
+
+        @pl.when(valid(zt - hop * (ntp - 1), nb))
+        def _():
+            z_final(zt - hop * (ntp - 1))
         for h in range(1, ntp):
-            @pl.when(valid(zt - (ntp - 1) - h, nb))
+            @pl.when(valid(zt - hop * (ntp - 1 + h), nb))
             def _(h=h):
-                z_hop(zt - (ntp - 1) - h, h)
+                z_hop(zt - hop * (ntp - 1 + h), h)
         return carry
-    lax.fori_loop(0, ticks, tick, 0)
+    lax.fori_loop(0, steps, one_step, 0)
 
     share_end()
 
@@ -546,7 +608,7 @@
         for c in fwd_copies(k):
             c.wait_send()
         last_copy(k).wait_send()
-    for b in range(max(nb - 2, 0), nb):
+    for b in range(max(nb - RING, 0), nb):
         for i in range(ntp - 1):
             @pl.when(z == i)
             def _(i=i, b=b):
@@ -570,7 +632,7 @@
     lax.fori_loop(0, nb, drain, 0)
 
 
-def gradients(ntp, ndp, zb, dx, stats, mask, lab, tok, embed, logits, chunk, tile, zrows):
+def gradients(ntp, ndp, zb, dx, stats, mask, lab, tok, gain, hidden, embed, logits, chunk, tile, zrows):
     tokens, d = zb.shape
     vocab_loc = embed.shape[0]
     nc = vocab_loc // chunk
@@ -587,36 +649,30 @@
     res = pl.pallas_call(
         functools.partial(grad_kernel, ntp, ndp, chunk, tile, zrows),
         out_shape=(sds(vocab_loc, d), sds(8, 128), sds(tokens, d), sds(nc, half, d), sds(nc, half, d),
-                   sds(nb, ntp - 1, zrows, d), sds(nb, ntp - 1, zrows, d)),
-        in_specs=[vm] * 6 + [hbm] * 2,
-        out_specs=(hbm, vm) + (hbm,) * 5,
+                   sds(nb, ntp - 1, zrows, d), sds(nb, ntp - 1, zrows, d), jax.ShapeDtypeStruct((nc, chunk, tokens), BF16)),
+        in_specs=[vm] * 7 + [hbm] * 3,
+        out_specs=(hbm, vm) + (hbm,) * 6,
         scratch_shapes=[
             vf(tiles, 1, tile), vf(tiles, 1, tile), vf(ntp, tiles, 8, tile), vf(ndp, 8, 128), vf(ndp, 8, 128),
             vf(2, chunk, tokens),
-            pltpu.VMEM((2, chunk, d), BF16), pltpu.VMEM((chunk, tokens), BF16), pltpu.VMEM((chunk, tokens), BF16),
-            vf(tokens, d), vf(2, chunk, d), vf(half, d), vf(half, d),
+            pltpu.VMEM((2, chunk, d), BF16), pltpu.VMEM((2, chunk, tokens), BF16), pltpu.VMEM((zrows, d), BF16),
+            pltpu.VMEM((chunk, tokens), BF16), pltpu.VMEM((chunk, tokens), BF16),
+            vf(tokens, d), vf(chunk, d), vf(half, d), vf(half, d),
             vf(RING, half, d), vf(RING, quarter, d), vf(RING, eighth, d), vf(SLOTS, quarter, d), vf(SLOTS, eighth, d),
-            vf(ntp - 1, zrows, d), vf(ntp - 1, zrows, d), vf(2, ntp - 1, zrows, d), vf(2, ntp - 1, zrows, d),
-            vf(2, zrows, d),
+            vf(ntp - 1, zrows, d), vf(ntp - 1, zrows, d), vf(RING, ntp - 1, zrows, d), vf(RING, ntp - 1, zrows, d),
+            vf(RING, zrows, d),
             dma(ntp - 1), dma(ntp), dma(ndp - 1), dma(ndp), dma(ndp - 1), dma(ndp), dma(2),
-            dma(2), dma(2), dma(2), dma(nc), dma(2), dma(RING), dma(SLOTS), dma(RING), dma(SLOTS), dma(4, RING),
+            dma(2), dma(2), dma(1), dma(1), dma(1), dma(1), dma(nc), dma(2), dma(RING), dma(SLOTS), dma(RING), dma(SLOTS), dma(4, RING),
             dma(nc), dma(2, nc), dma(3, RING), dma(3, nc),
-            dma(1), dma(2), dma(2), dma(nb), dma(nb), dma(3, 2), dma(nb, ntp - 1), dma(nb, ntp - 1),
+            dma(1), dma(RING), dma(RING), dma(nb), dma(nb), dma(3, RING), dma(nb, ntp - 1), dma(nb, ntp - 1),
             dma(nb, ntp - 1), dma(nb, ntp - 1),
         ],
         compiler_params=pltpu.CompilerParams(vmem_limit_bytes=VMEM_LIMIT, has_side_effects=True),
         cost_estimate=pl.CostEstimate(flops=3 * flops, bytes_accessed=4 * vocab_loc * (4 * d + tokens),
                                       transcendentals=tokens * vocab_loc),
         name='gradients',
-    )(zb, dx, stats, rows(mask), rows(lab), rows(tok), embed, logits)
+    )(zb, dx, stats, rows(mask), rows(lab), rows(tok), gain, hidden, embed, logits)
     return res[:3]
-
-
-def layer_norm(h_f32, ln_gain, ln_bias):
-    mean_val = jnp.mean(h_f32, axis=-1, keepdims=True)
-    centered = h_f32 - mean_val
-    var_val = jnp.mean(centered * centered, axis=-1, keepdims=True)
-    return centered * lax.rsqrt(var_val + 1e-5) * ln_gain + ln_bias
 
 
 def solution(mesh):
@@ -626,7 +682,7 @@
         vocab_loc, d = embed_loc.shape
         batch, ctx = tokens.shape
         ntok = batch * ctx
-        chunk, tile, zrows = sizes(ntok, vocab_loc)
+        chunk1, chunk, tile, zrows = sizes(ntok, vocab_loc)
         shard_start = lax.axis_index('tp') * vocab_loc
         tok_local = (tokens - shard_start).reshape(1, ntok)
         lab_local = (labels - shard_start).reshape(1, ntok)
@@ -635,14 +691,13 @@
 
         hidden2 = hidden.reshape(ntok, d)
         zb, stats, logits, rows = token_stats(hidden2, ln_gain.reshape(1, d), ln_bias.reshape(1, d), lab_local, tok_local,
-                                              tok_here, embed_loc, chunk, tile)
+                                              tok_here, embed_loc, chunk1, tile)
         rows = lax.psum(rows, 'tp').reshape(batch, ctx, d)
         embed_out = (rows + pos_table.astype(F32)[None]).astype(BF16)
-        grad_embed, loss, grad_z = gradients(ntp, ndp, zb, grad_x0.reshape(ntok, d), stats, lossmask.astype(F32), lab_local,
-                                             tok_local, embed_loc, logits, chunk, tile, zrows)
+        grad_embed, loss, grad_h = gradients(ntp, ndp, zb, grad_x0.reshape(ntok, d), stats, lossmask.astype(F32), lab_local,
+                                             tok_local, ln_gain.reshape(1, d), hidden2, embed_loc, logits, chunk, tile, zrows)
         mean_loss = loss[0, 0]
-        norm_vjp = jax.vjp(lambda h: layer_norm(h, ln_gain, ln_bias), hidden2.astype(F32))[1]
-        grad_hidden = norm_vjp(grad_z)[0].astype(BF16).reshape(batch, ctx, d)
+        grad_hidden = grad_h.astype(BF16).reshape(batch, ctx, d)
         return mean_loss, embed_out, grad_hidden, grad_embed, grad_pos
 
     row_spec = P('dp', None)

time: 898 us -> 834 us (0.929)
  Pallas kernels: 782 us -> 739 us
  other arithmetic: 43.2 us -> 25.3 us
    pallas_call x1, Pallas kernels: 676 us -> 639 us  [gradients(): pl.pallas_call(functools.partial(grad_kernel, ntp, ndp, chunk, tile, zrow...]
    reduce_sum x4 -> x0, other arithmetic: 18.9 us -> none  [the longest x1 6.7 us: layer_norm(): return centered * lax.rsqrt(var_val + 1e-05) * ln_gain + ln_bias]
    unnamed x20 -> x6, local copies, waits for them, and re-layouts: 48.3 us -> 46.3 us
  transfers between devices with their start and end apart: 2 -> 2, of which waited for: 0 -> 0; matrix products, arithmetic and copies ran while one was open for 5% -> 3% of each run, Pallas kernels for 75% -> 77%
where the time goes in v3:
time: 834 us; the launch traced here: 832 us
  Pallas kernels  739 us (89%)
  local copies, waits for them, and re-layouts  52.9 us (6%)
  other arithmetic  25.3 us (3%)
  between operations  14.1 us (2%)
    pallas_call x1, Pallas kernels, gradients(): pl.pallas_call(functools.partial(grad_kernel, ntp, ndp, chunk, tile, zrow...  639 us
    pallas_call x1, Pallas kernels, token_stats(): pl.pallas_call(functools.partial(stats_kernel, chunk, tile), grid_spec=pl...  101 us
    unnamed x6, local copies, waits for them, and re-layouts  46.3 us
  transfers between devices with their start and end apart: 2, of which 0 were waited for; matrix products, arithmetic and copies ran while one was open for 3% of the time, Pallas kernels for 77%

profile of v3, /device:TPU:0, one launch (start us, length us, event | category | flops | bytes accessed | tf_op | source)
XLA Modules:
  0.0 831.8 jit_solution(12702926209427041444)
XLA Ops:
  7.2 0.0 all-reduce.3.cloned.1.call-start
  7.2 1.3 reshape.72.gain
  8.5 1.3 reshape.73.bias
  9.8 0.7 broadcast_subtract_fusion
  10.5 0.7 reshape.74.lab
  11.2 0.1 reshape.70
  11.3 0.7 convert_reduce_fusion.1.starts
  12.0 5.0 sort.15
  17.1 100.6 %token_stats.1 = (bf16[1792,1280]{1,0:T(8,128)(2,1)}, f32[7,8,256]{2,1,0:T(8,128)}, f32[12992,1792]{1,0:T(8,128)}, f32[1792,1280]{1,0:T(8,128)}) custom-call(s32[15]{0:T(128)} %convert_reduce_fusion.1.starts, s32[1792]{0:T(1024)} %get-tuple-element.14.order, s32[1792]{0:T(1024)} %get-tuple-element.15.skey, bf16[1792,1280]{1,0:T(8,128)(2,1)} %bitcast.8, ...), custom_call_target="tpu_custom_call" | custom-call | flops 59601059840 | bytes 126386176 | tf_op jit(solution)/shard_map/token_stats/pallas_call | solution.py:96
  117.7 0.0 all-reduce.3.cloned.1.call-update
  117.7 0.0 copy-start.1
  117.8 0.0 all-reduce.5.cloned.1.call-start
  117.8 4.6 convert_reduce_fusion
  122.4 0.0 all-reduce.5.cloned.1.call-update
  122.4 0.7 reshape_reshape.6.lab
  123.1 0.7 reshape_reshape.7.tok
  123.7 0.0 copy-done.1
  123.7 0.7 reshape.76.mask
  124.4 638.8 %gradients.1 = (f32[12992,1280]{1,0:T(8,128)}, f32[8,128]{1,0:T(8,128)}, f32[1792,1280]{1,0:T(8,128)}, f32[29,224,1280]{2,1,0:T(8,128)}, f32[29,224,1280]{2,1,0:...) custom-call(bf16[1792,1280]{1,0:T(8,128)(2,1)} %get-tuple-element.16.zb, ...), custom_call_target="tpu_custom_call" | custom-call | flops 178803179520 | bytes 359202816 | tf_op jit(solution)/shard_map/gradients/pallas_call | solution.py:649
  763.3 1.4 convert_element_type.20
  764.7 1.2 slice.3
  765.9 6.2 convert_element_type.22
  772.1 0.0 all-reduce.3.cloned.1.call-done
  772.1 6.6 add_convert_fusion
  778.7 0.0 all-reduce.5.cloned.1.call-done
  778.7 0.0 copy-start
  778.7 44.9 %copy.17 = f32[12992,1280]{1,0:T(8,128)} copy(f32[12992,1280]{1,0:T(8,128)} %get-tuple-element.33) | data formatting | bytes 133038080
  823.6 0.0 copy-done
  823.6 1.4 copy.18
  (4 shorter events, 0.0 us)
Async XLA Ops:
  7.2 764.9 %all-reduce.3.cloned.1.call-start = ((), (), s32[]{:S(2)}) async-start(), calls=%async_computation | async-start | bytes 18350080 | tf_op jit(solution)/shard_map/psum | solution.py:695
  117.7 6.0 copy-start.1
  117.8 661.0 %all-reduce.5.cloned.1.call-start = ((), (), s32[]{:S(2)}) async-start(), calls=%async_computation.1 | async-start | bytes 4587520 | tf_op jit(solution)/shard_map/psum | solution.py:690
  778.7 44.9 %copy-start = (f32[448,1280]{1,0:T(8,128)S(1)}, f32[448,1280]{1,0:T(8,128)}, u32[]{:S(2)}) copy-start(f32[448,1280]{1,0:T(8,128)} %all-reduce.5.cloned.1.call-done) | copy-start | bytes 6881284
Sparse Core Ops, SparseCore 0:
  117.9 321.9 all-reduce.2
  443.7 84.9 all-reduce.4

commit v4 on v3

--- a/solution.py
+++ b/solution.py
@@ -24,7 +24,7 @@
     return 64, 64, 128, 8
 
 
-def stats_kernel(chunk, tile, starts, order, skey, hidden, gain, bias, lab, embed, zb, stats, logits_out, rows_out, m_ref, s_ref, l_ref):
+def stats_kernel(chunk, tile, starts, order, skey, hidden, affine, lab, embed, zb, stats, logits_out, rows_out, m_ref, s_ref, l_ref):
     step = pl.program_id(0)
     tokens, d = hidden.shape
     tiles = tokens // tile
@@ -36,7 +36,7 @@
             h = hidden[rows, :].astype(F32)
             centered = h - jnp.mean(h, axis=-1, keepdims=True)
             var = jnp.mean(centered * centered, axis=-1, keepdims=True)
-            zb[rows, :] = (centered * lax.rsqrt(var + 1e-5) * gain[...] + bias[...]).astype(BF16)
+            zb[rows, :] = (centered * lax.rsqrt(var + 1e-5) * affine[0:1, :] + affine[1:2, :]).astype(BF16)
             rows_out[rows, :] = jnp.zeros((tile, d), F32)
             return carry
         lax.fori_loop(0, tiles, norm, 0)
@@ -46,16 +46,20 @@
 
     first_tok, end_tok = starts[step], starts[step + 1]
 
-    def token_rows(n, carry):
+    def token_row(i):
+        real = i < end_tok
+        i = jnp.where(real, i, 0)
+        row = jnp.where(real, skey[i] - step * chunk, 0)
+        group = lax.div(row, 16) * 16
+        block = embed[pl.ds(pl.multiple_of(group, 16), 16), :].astype(F32)
+        pick = lax.broadcasted_iota(jnp.int32, (16, 1), 0) == row - group
+        rows_out[pl.ds(jnp.where(real, order[i], tokens), 1), :] = jnp.sum(jnp.where(pick, block, 0.0), axis=0, keepdims=True)
+
+    def more_rows(n, carry):
         for u in range(4):
-            i = jnp.minimum(first_tok + n * 4 + u, end_tok - 1)
-            row = skey[i] - step * chunk
-            group = lax.div(row, 16) * 16
-            block = embed[pl.ds(pl.multiple_of(group, 16), 16), :].astype(F32)
-            pick = lax.broadcasted_iota(jnp.int32, (16, 1), 0) == row - group
-            rows_out[pl.ds(order[i], 1), :] = jnp.sum(jnp.where(pick, block, 0.0), axis=0, keepdims=True)
+            token_row(first_tok + n * 4 + u)
         return carry
-    lax.fori_loop(0, lax.div(end_tok - first_tok + 3, 4), token_rows, 0)
+    lax.fori_loop(0, lax.div(end_tok - first_tok + 3, 4), more_rows, 0)
 
     ids = lax.broadcasted_iota(jnp.int32, (chunk, tile), 0) + step * chunk
 
@@ -84,7 +88,7 @@
             stats[j, 2:8, :] = jnp.zeros((6, tile), F32)
 
 
-def token_stats(hidden, gain, bias, lab, tok, here, embed, chunk, tile):
+def token_stats(hidden, affine, lab, tok, here, embed, chunk, tile):
     tokens, d = hidden.shape
     vocab_loc = embed.shape[0]
     steps = vocab_loc // chunk
@@ -98,27 +102,28 @@
         grid_spec=pltpu.PrefetchScalarGridSpec(
             num_scalar_prefetch=3,
             grid=(steps,),
-            in_specs=[whole, whole, whole, whole, pl.BlockSpec((chunk, d), lambda i, *_: (i, 0))],
+            in_specs=[whole, whole, whole, pl.BlockSpec((chunk, d), lambda i, *_: (i, 0))],
             out_specs=(whole, whole, pl.BlockSpec((chunk, tokens), lambda i, *_: (i, 0)), whole),
             scratch_shapes=[pltpu.VMEM((1, tokens), F32)] * 3),
         out_shape=(jax.ShapeDtypeStruct((tokens, d), BF16), jax.ShapeDtypeStruct((tokens // tile, 8, tile), F32),
-                   jax.ShapeDtypeStruct((vocab_loc, tokens), F32), jax.ShapeDtypeStruct((tokens, d), F32)),
+                   jax.ShapeDtypeStruct((vocab_loc, tokens), F32), jax.ShapeDtypeStruct((tokens + 8, d), F32)),
         compiler_params=pltpu.CompilerParams(vmem_limit_bytes=VMEM_LIMIT),
         cost_estimate=pl.CostEstimate(flops=2 * tokens * d * vocab_loc, bytes_accessed=2 * embed.size + 4 * vocab_loc * tokens,
                                       transcendentals=tokens * vocab_loc),
         name='token_stats',
-    )(starts, order, skey, hidden, gain, bias, lab, embed)
+    )(starts, order, skey, hidden, affine, lab, embed)
 
 
 def grad_kernel(ntp, ndp, chunk, tile, zrows,
-                zb, dx, stats, mask, lab, tok, gain, hidden, embed, logits,
+                dx, stats, mask, lab, tok, affine, zb_hbm, hidden, embed, logits,
                 out, loss, gz, own, d2d, rs_r, rs_l, gsave,
-                lse, wgt, st_in, cnt_in, loss_in, lbuf, ebuf, gz_t, hbuf, gt, oh, acc, gbuf, ld_own, ld_d2d, s1, s2, fin, rs1, rs2, zin_r, zin_l, zout_r, zout_l, zfin,
-                st_s, st_r, cnt_s, cnt_r, loss_s, loss_r, l_sem, e_sem, gs_sem, gl_sem, h_sem, own_sem, d2d_s, d2d_r, ld_sem, rs1_s, rs1_r, rs2_s, rs2_r, fin_s, ag1_r, ag2_r, fwd_s, part_r,
+                zb, lse, wgt, st_in, cnt_in, loss_in, lbuf, ebuf, gz_t, hbuf, gt, oh, acc, gbuf, ld_own, ld_d2d, s1, s2, fin, rs1, rs2, zin_r, zin_l, zout_r, zout_l, zfin,
+                st_s, st_r, cnt_s, cnt_r, loss_s, loss_r, zb_sem, l_sem, e_sem, gs_sem, gl_sem, h_sem, own_sem, d2d_s, d2d_r, ld_sem, rs1_s, rs1_r, rs2_s, rs2_r, fin_s, ag1_r, ag2_r, fwd_s, part_r,
                 zld, zrs_sr, zrs_sl, zrs_rr, zrs_rl, zfin_s, zag_rr, zag_rl, zfw_r, zfw_l):
-    tokens, d = zb.shape
+    tokens, d = dx.shape
     vocab_loc = embed.shape[0]
     nc = vocab_loc // chunk
+    ncc = nc + 1
     tiles = tokens // tile
     ntile = 256 if d % 256 == 0 and d > 256 else 128
     ntiles = d // ntile
@@ -147,11 +152,14 @@
         return pltpu.make_async_remote_copy(src_ref=src, dst_ref=dst, send_sem=ssem, recv_sem=rsem,
                                             device_id={'tp': dev}, device_id_type=MESH)
 
+    def row0(c):
+        return lax.rem(c + nc, ncc) * chunk
+
     def rows8(start, n):
         return pl.ds(pl.multiple_of(start, 8), n)
 
-    def valid(k, limit=None):
-        return (k >= 0) & (k < (nc if limit is None else limit))
+    def valid(k, limit):
+        return (k >= 0) & (k < limit)
 
     def e_copy(k):
         return pltpu.make_async_copy(embed.at[rows8(k * chunk, chunk)], ebuf.at[lax.rem(k, 2)], e_sem.at[lax.rem(k, 2)])
@@ -185,7 +193,7 @@
     def fin_copies(k):
         n1, n2, a1, a2 = place(k)
         b = lax.rem(k, RING)
-        dst = out.at[rows8(k * chunk + core * half + a1 * quarter + a2 * eighth, eighth)]
+        dst = out.at[rows8(row0(k) + core * half + a1 * quarter + a2 * eighth, eighth)]
         src = fin.at[b]
         return (pltpu.make_async_copy(src, dst, fin_s.at[0, b]),
                 rdma(src, dst, fin_s.at[1, b], ag1_r.at[k], n2),
@@ -195,13 +203,13 @@
     def fwd_copies(k):
         n1, _, a1, a2 = place(k)
         b = lax.rem(k, RING)
-        ref = out.at[rows8(k * chunk + core * half + a1 * quarter + (1 - a2) * eighth, eighth)]
+        ref = out.at[rows8(row0(k) + core * half + a1 * quarter + (1 - a2) * eighth, eighth)]
         return (rdma(ref, ref, fwd_s.at[0, b], ag2_r.at[1, k], n1),
                 rdma(ref, ref, fwd_s.at[1, b], part_r.at[1, k], partner))
 
     def last_copy(k):
         _, _, a1, _ = place(k)
-        ref = out.at[rows8(k * chunk + core * half + (1 - a1) * quarter, quarter)]
+        ref = out.at[rows8(row0(k) + core * half + (1 - a1) * quarter, quarter)]
         return rdma(ref, ref, fwd_s.at[2, lax.rem(k, RING)], part_r.at[2, k], partner)
 
     def peer(i, n, me):
@@ -256,6 +264,8 @@
         for i in range(1, ntp):
             st_copy(i, z).wait_send()
 
+    zb_copy = pltpu.make_async_copy(zb_hbm, zb, zb_sem.at[0])
+
     def z_unit(u, carry):
         k, j = lax.div(u, tiles), lax.rem(u, tiles)
         slot = lax.rem(k, 2)
@@ -270,7 +280,7 @@
                 e_copy(k + 1).start()
                 l_copy(k + 1).start()
 
-            @pl.when(k >= 1)
+            @pl.when(k >= 2)
             def _():
                 gs_copy(k - 1).wait()
         cols = pl.ds(pl.multiple_of(j * tile, tile), tile)
@@ -284,7 +294,7 @@
         def _():
             gs_copy(k).start()
 
-            @pl.when(k == nc - 1)
+            @pl.when((k == 0) | (k == nc - 1))
             def _():
                 gs_copy(k).wait()
         return carry
@@ -294,6 +304,8 @@
 
         @pl.when(n == 0)
         def _():
+            gl_copy(k).start()
+
             def one_hot(j, c):
                 cols = pl.ds(pl.multiple_of(j * tile, tile), tile)
                 ids = lax.broadcasted_iota(jnp.int32, (chunk, tile), 0) + k * chunk
@@ -301,24 +313,26 @@
                 return c
             lax.fori_loop(0, tiles, one_hot, 0)
 
-            @pl.when(k >= 1)
+            own_copy(k).wait()
+            d2d_copy(k).wait_send()
+            gl_copy(k).wait()
+
+            @pl.when(k == 0)
             def _():
-                own_copy(k - 1).wait()
-                d2d_copy(k - 1).wait_send()
-            gl_copy(k).wait()
+                zb_copy.wait()
         cols = pl.ds(pl.multiple_of(n * ntile, ntile), ntile)
         gbuf[:, cols] = (jnp.dot(gt[...], zb[:, cols], preferred_element_type=F32)
                          + jnp.dot(oh[...], dx[:, cols], preferred_element_type=F32))
 
         @pl.when(n == ntiles - 1)
         def _():
-            own_copy(k).start()
-            d2d_copy(k).start()
+            own_copy(k + 1).start()
+            d2d_copy(k + 1).start()
 
             @pl.when(k == nc - 1)
             def _():
-                own_copy(k).wait()
-                d2d_copy(k).wait_send()
+                own_copy(k + 1).wait()
+                d2d_copy(k + 1).wait_send()
         return carry
 
     def load_start(k):
@@ -484,7 +498,7 @@
         centered = h - jnp.mean(h, axis=-1, keepdims=True)
         rstd = lax.rsqrt(jnp.mean(centered * centered, axis=-1, keepdims=True) + 1e-5)
         unit = centered * rstd
-        dy = zfin[lax.rem(b, RING)] * gain[...]
+        dy = zfin[lax.rem(b, RING)] * affine[0:1, :]
         zfin[lax.rem(b, RING)] = rstd * (dy - jnp.mean(dy, axis=-1, keepdims=True)
                                          - unit * jnp.mean(dy * unit, axis=-1, keepdims=True))
         copies = zfin_copies(b)
@@ -536,29 +550,38 @@
                 def _():
                     zag(b, h, -1, zfw_l, zag_rl).start()
 
-    lead = min(7, nc)
-    g_first = STEPS + 1
+    lead, g_first = 10, STEPS
     nz, ng = nc * tiles, nc * ntiles
     fast = (tiles * 12) // 7
 
     def uz(i):
-        late = i - lead * STEPS
-        return jnp.minimum(lax.div(jnp.minimum(i, lead * STEPS) * tiles + jnp.maximum(late, 0) * fast, STEPS), nz)
+        late = jnp.maximum(i - 1 - lead, 0)
+        count = tiles + 1 + lax.div(jnp.minimum(i - 1, lead) * tiles + late * fast, STEPS)
+        return jnp.where(i <= 0, 0, jnp.minimum(count, nz))
 
     def ug(i):
-        return jnp.minimum(lax.div(jnp.maximum(i - g_first, 0) * ntiles, STEPS), ng)
-
-    base = g_first + STEPS
-    lags = (('w', base + 16), ('f', base + 26), ('e', base + 22), ('d', base + 12), ('c', base + 8), ('b', base + 5),
-            ('a', base + 1), ('p', base))
+        return jnp.where(i <= 0, 0, jnp.minimum(ntiles + lax.div(jnp.maximum(i - g_first, 0) * ntiles, STEPS), ng))
+
+    lags = (('p', 0), ('a', 1), ('b', 4), ('c', 6), ('d', 10), ('w', 16), ('e', 16), ('f', 24))
     stages = {'w': stage_w, 'f': stage_f, 'e': stage_e, 'd': stage_d, 'c': stage_c, 'b': stage_b, 'a': stage_a,
               'p': load_start}
-    z_start = lead * STEPS + -(-(nz - lead * tiles) * STEPS // fast)
-    hop = 3
-    steps = max((nc - 1) * STEPS + base + 27, z_start + nb + hop * 2 * (ntp - 1))
+    z_start = lead + -(-max(nz - (tiles + 1 + lead * tiles // STEPS), 0) * STEPS // fast)
+    hop = 4
+    steps = max((ncc - 1) * STEPS + 25, z_start + nb + hop * 2 * (ntp - 1))
     share_start()
+    zb_copy.start()
     e_copy(0).start()
     l_copy(0).start()
+
+    def pos_rows(j, carry):
+        total = dx[rows8(j * eighth, eighth), :].astype(F32)
+        for b in range(1, tokens // chunk):
+            total = total + dx[pl.ds(pl.multiple_of(b * chunk + j * eighth, 8), eighth), :].astype(F32)
+        gbuf[rows8(j * eighth, eighth), :] = total
+        return carry
+    lax.fori_loop(0, 8, pos_rows, 0)
+    own_copy(0).start()
+    d2d_copy(0).start()
 
     def clear(j, carry):
         acc[pl.ds(pl.multiple_of(j * tile, tile), tile), :] = jnp.zeros((tile, d), F32)
@@ -567,15 +590,10 @@
     share_use()
 
     def one_step(i, carry):
-        gk = i - g_first
-
-        @pl.when((gk >= 0) & (gk < nc * STEPS) & (lax.rem(gk, STEPS) == 0))
-        def _():
-            gl_copy(lax.div(gk, STEPS)).start()
         lax.fori_loop(uz(i), uz(i + 1), z_unit, 0)
         lax.fori_loop(ug(i), ug(i + 1), g_unit, 0)
         for name, lag in lags:
-            @pl.when((i >= lag) & (i - lag < nc * STEPS) & (lax.rem(i - lag + STEPS * 64, STEPS) == 0))
+            @pl.when((i >= lag) & (i - lag < ncc * STEPS) & (lax.rem(i - lag + STEPS * 64, STEPS) == 0))
             def _(name=name, lag=lag):
                 stages[name](lax.div(i - lag, STEPS))
         zt = i - z_start
@@ -600,7 +618,7 @@
 
     share_end()
 
-    for k in range(max(nc - RING, 0), nc):
+    for k in range(max(ncc - RING, 0), ncc):
         rs1_copy(k).wait_send()
         rs2_copy(k).wait_send()
         for i, c in enumerate(fin_copies(k)):
@@ -632,10 +650,11 @@
     lax.fori_loop(0, nb, drain, 0)
 
 
-def gradients(ntp, ndp, zb, dx, stats, mask, lab, tok, gain, hidden, embed, logits, chunk, tile, zrows):
+def gradients(ntp, ndp, zb, dx, stats, mask, lab, tok, affine, hidden, embed, logits, chunk, tile, zrows):
     tokens, d = zb.shape
     vocab_loc = embed.shape[0]
     nc = vocab_loc // chunk
+    ncc = nc + 1
     half, quarter, eighth = chunk // 2, chunk // 4, chunk // 8
     tiles = tokens // tile
     nb = tokens // ntp // zrows
@@ -648,12 +667,12 @@
     rows = lambda a: a.reshape(tiles, 1, tile)
     res = pl.pallas_call(
         functools.partial(grad_kernel, ntp, ndp, chunk, tile, zrows),
-        out_shape=(sds(vocab_loc, d), sds(8, 128), sds(tokens, d), sds(nc, half, d), sds(nc, half, d),
+        out_shape=(sds(vocab_loc + chunk, d), sds(8, 128), sds(tokens, d), sds(ncc, half, d), sds(ncc, half, d),
                    sds(nb, ntp - 1, zrows, d), sds(nb, ntp - 1, zrows, d), jax.ShapeDtypeStruct((nc, chunk, tokens), BF16)),
-        in_specs=[vm] * 7 + [hbm] * 3,
+        in_specs=[vm] * 6 + [hbm] * 4,
         out_specs=(hbm, vm) + (hbm,) * 6,
         scratch_shapes=[
-            vf(tiles, 1, tile), vf(tiles, 1, tile), vf(ntp, tiles, 8, tile), vf(ndp, 8, 128), vf(ndp, 8, 128),
+            pltpu.VMEM((tokens, d), BF16), vf(tiles, 1, tile), vf(tiles, 1, tile), vf(ntp, tiles, 8, tile), vf(ndp, 8, 128), vf(ndp, 8, 128),
             vf(2, chunk, tokens),
             pltpu.VMEM((2, chunk, d), BF16), pltpu.VMEM((2, chunk, tokens), BF16), pltpu.VMEM((zrows, d), BF16),
             pltpu.VMEM((chunk, tokens), BF16), pltpu.VMEM((chunk, tokens), BF16),
@@ -661,9 +680,9 @@
             vf(RING, half, d), vf(RING, quarter, d), vf(RING, eighth, d), vf(SLOTS, quarter, d), vf(SLOTS, eighth, d),
             vf(ntp - 1, zrows, d), vf(ntp - 1, zrows, d), vf(RING, ntp - 1, zrows, d), vf(RING, ntp - 1, zrows, d),
             vf(RING, zrows, d),
-            dma(ntp - 1), dma(ntp), dma(ndp - 1), dma(ndp), dma(ndp - 1), dma(ndp), dma(2),
-            dma(2), dma(2), dma(1), dma(1), dma(1), dma(1), dma(nc), dma(2), dma(RING), dma(SLOTS), dma(RING), dma(SLOTS), dma(4, RING),
-            dma(nc), dma(2, nc), dma(3, RING), dma(3, nc),
+            dma(ntp - 1), dma(ntp), dma(ndp - 1), dma(ndp), dma(ndp - 1), dma(ndp), dma(1), dma(2),
+            dma(2), dma(2), dma(1), dma(1), dma(1), dma(1), dma(ncc), dma(2), dma(RING), dma(SLOTS), dma(RING), dma(SLOTS), dma(4, RING),
+            dma(ncc), dma(2, ncc), dma(3, RING), dma(3, ncc),
             dma(1), dma(RING), dma(RING), dma(nb), dma(nb), dma(3, RING), dma(nb, ntp - 1), dma(nb, ntp - 1),
             dma(nb, ntp - 1), dma(nb, ntp - 1),
         ],
@@ -671,8 +690,34 @@
         cost_estimate=pl.CostEstimate(flops=3 * flops, bytes_accessed=4 * vocab_loc * (4 * d + tokens),
                                       transcendentals=tokens * vocab_loc),
         name='gradients',
-    )(zb, dx, stats, rows(mask), rows(lab), rows(tok), gain, hidden, embed, logits)
+    )(dx, stats, rows(mask), rows(lab), rows(tok), affine, zb, hidden, embed, logits)
     return res[:3]
+
+
+def finish_kernel(grad_in, pos_in, rows, gh_in, pos_table, grad_out, pos_out, embed_out, gh_out):
+    grad_out[...] = grad_in[...]
+    pos_out[...] = pos_in[...]
+    embed_out[...] = (rows[...] + pos_table[...].astype(F32)).astype(BF16)
+    gh_out[...] = gh_in[...].astype(BF16)
+
+
+def finish(grads, rows, grad_h, pos_table, vocab_loc):
+    tokens, d = grad_h.shape
+    ctx = pos_table.shape[0]
+    n = tokens // 64
+    big, mid, small = vocab_loc // n, 64, ctx // n
+    at = lambda r, f=lambda i: i: pl.BlockSpec((r, d), lambda i: (f(i), 0))
+    return pl.pallas_call(
+        finish_kernel,
+        grid=(n,),
+        in_specs=[at(big), at(small, lambda i: vocab_loc // small + i), at(mid), at(mid), at(mid, lambda i: lax.rem(i, ctx // mid))],
+        out_specs=(at(big), at(small), at(mid), at(mid)),
+        out_shape=(jax.ShapeDtypeStruct((vocab_loc, d), F32), jax.ShapeDtypeStruct((ctx, d), F32),
+                   jax.ShapeDtypeStruct((tokens, d), BF16), jax.ShapeDtypeStruct((tokens, d), BF16)),
+        compiler_params=pltpu.CompilerParams(vmem_limit_bytes=VMEM_LIMIT),
+        cost_estimate=pl.CostEstimate(flops=tokens * d, bytes_accessed=8 * vocab_loc * d, transcendentals=0),
+        name='finish',
+    )(grads, grads, rows, grad_h, pos_table)
 
 
 def solution(mesh):
@@ -687,17 +732,16 @@
         tok_local = (tokens - shard_start).reshape(1, ntok)
         lab_local = (labels - shard_start).reshape(1, ntok)
         tok_here = (tok_local >= 0) & (tok_local < vocab_loc)
-        grad_pos = lax.psum(jnp.sum(grad_x0.astype(F32), axis=0), 'dp')
-
         hidden2 = hidden.reshape(ntok, d)
-        zb, stats, logits, rows = token_stats(hidden2, ln_gain.reshape(1, d), ln_bias.reshape(1, d), lab_local, tok_local,
-                                              tok_here, embed_loc, chunk1, tile)
-        rows = lax.psum(rows, 'tp').reshape(batch, ctx, d)
-        embed_out = (rows + pos_table.astype(F32)[None]).astype(BF16)
-        grad_embed, loss, grad_h = gradients(ntp, ndp, zb, grad_x0.reshape(ntok, d), stats, lossmask.astype(F32), lab_local,
-                                             tok_local, ln_gain.reshape(1, d), hidden2, embed_loc, logits, chunk, tile, zrows)
+        affine = jnp.stack([ln_gain, ln_bias])
+        zb, stats, logits, rows = token_stats(hidden2, affine, lab_local, tok_local, tok_here, embed_loc, chunk1, tile)
+        rows = lax.psum(rows, 'tp')
+        grads, loss, grad_h = gradients(ntp, ndp, zb, grad_x0.reshape(ntok, d), stats, lossmask.astype(F32), lab_local,
+                                        tok_local, affine, hidden2, embed_loc, logits, chunk, tile, zrows)
+        grad_embed, grad_pos, embed_out, grad_hidden = finish(grads, rows, grad_h, pos_table, vocab_loc)
         mean_loss = loss[0, 0]
-        grad_hidden = grad_h.astype(BF16).reshape(batch, ctx, d)
+        embed_out = embed_out.reshape(batch, ctx, d)
+        grad_hidden = grad_hidden.reshape(batch, ctx, d)
         return mean_loss, embed_out, grad_hidden, grad_embed, grad_pos
 
     row_spec = P('dp', None)

time: 834 us -> 846 us (1.014)
  Pallas kernels: 739 us -> 817 us
  local copies, waits for them, and re-layouts: 52.9 us -> 5.43 us
  other arithmetic: 25.3 us -> 7.09 us
    pallas_call x0 -> x1, Pallas kernels: none -> 59.1 us  [finish(): pl.pallas_call(finish_kernel, grid=(n,), in_specs=[at(big), at(small, lam...]
    unnamed x6 -> x2, local copies, waits for them, and re-layouts: 46.3 us -> 0.01 us
    pallas_call x1, Pallas kernels: 639 us -> 657 us  [gradients(): pl.pallas_call(functools.partial(grad_kernel, ntp, ndp, chunk, tile, zrow...]
    convert_element_type x3 -> x0, other arithmetic: 14.2 us -> none  [the longest x2 8.02 us: device_fn(): embed_out = (rows + pos_table.astype(F32)[None]).astype(BF16)]
  transfers between devices with their start and end apart: 2 -> 1, of which waited for: 0 -> 0; matrix products, arithmetic and copies ran while one was open for 3% -> 0% of each run, Pallas kernels for 77% -> 78%
where the time goes in v4:
time: 846 us; the launch traced here: 843 us
  Pallas kernels  817 us (97%)
  between operations  14.1 us (2%)
    pallas_call x1, Pallas kernels, gradients(): pl.pallas_call(functools.partial(grad_kernel, ntp, ndp, chunk, tile, zrow...  657 us
    pallas_call x1, Pallas kernels, token_stats(): pl.pallas_call(functools.partial(stats_kernel, chunk, tile), grid_spec=pl...  100 us
    pallas_call x1, Pallas kernels, finish(): pl.pallas_call(finish_kernel, grid=(n,), in_specs=[at(big), at(small, lam...  59.1 us
  transfers between devices with their start and end apart: 1, of which 0 were waited for; matrix products, arithmetic and copies ran while one was open for 0% of the time, Pallas kernels for 78%

profile of v4, /device:TPU:0, one launch (start us, length us, event | category | flops | bytes accessed | tf_op | source)
XLA Modules:
  0.0 843.3 jit_solution(18135159100690874381)
XLA Ops:
  7.2 0.0 all-reduce.2.cloned.1.call-start
  7.2 0.7 stack.9
  7.9 0.7 stack.10
  8.6 0.7 broadcast_subtract_fusion
  9.4 0.7 reshape.65.lab
  10.0 0.1 reshape.63
  10.1 0.7 convert_reduce_fusion.starts
  10.8 5.0 sort.15
  15.9 0.6 pad_maximum_fusion.affine
  16.5 100.3 %token_stats.1 = (bf16[1792,1280]{1,0:T(8,128)(2,1)}, f32[7,8,256]{2,1,0:T(8,128)}, f32[12992,1792]{1,0:T(8,128)}, f32[1800,1280]{1,0:T(8,128)}) custom-call(s32[15]{0:T(128)} %convert_reduce_fusion.starts, s32[1792]{0:T(1024)} %get-tuple-element.18.order, s32[1792]{0:T(1024)} %get-tuple-element.19.skey, bf16[1792,1280]{1,0:T(8,128)(2,1)} %bitcast.6, ...), custom_call_target="tpu_custom_call" | custom-call | flops 59601059840 | bytes 126386176 | tf_op jit(solution)/shard_map/token_stats/pallas_call | solution.py:100
  116.8 0.0 copy-start
  116.8 0.0 all-reduce.2.cloned.1.call-update
  116.8 0.7 reshape_reshape.6.lab
  117.5 0.7 reshape_reshape.7.tok
  118.2 0.0 copy-done
  118.2 0.7 reshape.66.mask
  118.9 657.2 %gradients.1 = (f32[13440,1280]{1,0:T(8,128)}, f32[8,128]{1,0:T(8,128)}, f32[1792,1280]{1,0:T(8,128)}, f32[30,224,1280]{2,1,0:T(8,128)}, f32[30,224,1280]{2,1,0:...) custom-call(bf16[1792,1280]{1,0:T(8,128)(2,1)} %bitcast.5, ...), custom_call_target="tpu_custom_call" | custom-call | flops 178803179520 | bytes 359202816 | tf_op jit(solution)/shard_map/gradients/pallas_call | solution.py:668
  776.1 1.2 slice.3
  777.3 0.0 all-reduce.2.cloned.1.call-done.rows
  777.3 59.1 %finish.1 = (f32[12992,1280]{1,0:T(8,128)}, f32[448,1280]{1,0:T(8,128)}, bf16[1792,1280]{1,0:T(8,128)(2,1)}, bf16[1792,1280]{1,0:T(8,128)(2,1)}) custom-call(f32[13440,1280]{1,0:T(8,128)} %get-tuple-element.24.grad_in.pos_in, f32[13440,1280]{1,0:T(8,128)} %get-tuple-element.24.grad_in.pos_in, f32[1800,1280]{1,0:T(8,128)} %all-reduce.2.cloned.1.call-done.rows, ...), custom_call_target="tpu_custom_call" | custom-call | flops 2293760 | bytes 133038080 | tf_op jit(solution)/shard_map/finish/pallas_call | solution.py:710
  (4 shorter events, 0.0 us)
Async XLA Ops:
  7.2 770.2 %all-reduce.2.cloned.1.call-start = ((), (), s32[]{:S(2)}) async-start(), calls=%async_computation | async-start | bytes 18432000 | tf_op jit(solution)/shard_map/psum | solution.py:738
  116.8 1.4 copy-start
Sparse Core Ops, SparseCore 0:
  117.0 323.3 all-reduce.1

commit v5 on v4

--- a/solution.py
+++ b/solution.py
@@ -11,7 +11,6 @@
 F32 = jnp.float32
 BF16 = jnp.bfloat16
 NT = (((1,), (1,)), ((), ()))
-TN = (((0,), (0,)), ((), ()))
 RING = 4
 SLOTS = 8
 STEPS = 2
@@ -24,15 +23,27 @@
     return 64, 64, 128, 8
 
 
-def stats_kernel(chunk, tile, starts, order, skey, hidden, affine, lab, embed, zb, stats, logits_out, rows_out, m_ref, s_ref, l_ref):
+def stats_kernel(chunk, tile, ctx, starts, order, skey, hidden, affine, lab, dx, embed,
+                 zb, stats, logits_out, rows_out, scatter, pos, m_ref, s_ref, l_ref, dx_f32, dx_in, dx_sem):
     step = pl.program_id(0)
     tokens, d = hidden.shape
     tiles = tokens // tile
 
     @pl.when(step == 0)
     def _():
+        def dx_copy(j):
+            rows = pl.ds(pl.multiple_of(j * tile, tile), tile)
+            return pltpu.make_async_copy(dx.at[rows], dx_in.at[lax.rem(j, 2)], dx_sem.at[lax.rem(j, 2)])
+        dx_copy(0).start()
+
         def norm(j, carry):
             rows = pl.ds(pl.multiple_of(j * tile, tile), tile)
+            dx_copy(j).wait()
+
+            @pl.when(j + 1 < tiles)
+            def _():
+                dx_copy(j + 1).start()
+            dx_f32[rows, :] = dx_in[lax.rem(j, 2)].astype(F32)
             h = hidden[rows, :].astype(F32)
             centered = h - jnp.mean(h, axis=-1, keepdims=True)
             var = jnp.mean(centered * centered, axis=-1, keepdims=True)
@@ -40,9 +51,37 @@
             rows_out[rows, :] = jnp.zeros((tile, d), F32)
             return carry
         lax.fori_loop(0, tiles, norm, 0)
+
+        def pos_rows(j, carry):
+            n = ctx // 8
+            pos[pl.ds(pl.multiple_of(j * n, 8), n), :] = functools.reduce(jnp.add, [
+                dx_f32[pl.ds(pl.multiple_of(b * ctx + j * n, 8), n), :] for b in range(tokens // ctx)])
+            return carry
+        lax.fori_loop(0, 8, pos_rows, 0)
         m_ref[...] = jnp.full_like(m_ref, -jnp.inf)
         s_ref[...] = jnp.zeros_like(s_ref)
         l_ref[...] = jnp.zeros_like(l_ref)
+
+    ids = lax.broadcasted_iota(jnp.int32, (chunk, tile), 0) + step * chunk
+
+    def product(j):
+        cols = slice(j * tile, (j + 1) * tile)
+        logits_out[:, cols] = lax.dot_general(embed[...], zb[cols, :], NT, preferred_element_type=F32)
+
+    product(0)
+    band = -(-chunk // tiles // 8) * 8
+    for j in range(tiles):
+        cols = slice(j * tile, (j + 1) * tile)
+        if j + 1 < tiles:
+            product(j + 1)
+        if j * band < chunk:
+            scatter[j * band:min((j + 1) * band, chunk), :] = jnp.zeros((min(band, chunk - j * band), d), F32)
+        logits = logits_out[:, cols]
+        m_old = m_ref[:, cols]
+        m_new = jnp.maximum(m_old, jnp.max(logits, axis=0, keepdims=True))
+        m_ref[:, cols] = m_new
+        s_ref[:, cols] = s_ref[:, cols] * jnp.exp(m_old - m_new) + jnp.sum(jnp.exp(logits - m_new), axis=0, keepdims=True)
+        l_ref[:, cols] += jnp.sum(jnp.where(ids == lab[:, cols], logits, 0.0), axis=0, keepdims=True)
 
     first_tok, end_tok = starts[step], starts[step + 1]
 
@@ -54,30 +93,13 @@
         block = embed[pl.ds(pl.multiple_of(group, 16), 16), :].astype(F32)
         pick = lax.broadcasted_iota(jnp.int32, (16, 1), 0) == row - group
         rows_out[pl.ds(jnp.where(real, order[i], tokens), 1), :] = jnp.sum(jnp.where(pick, block, 0.0), axis=0, keepdims=True)
-
-    def more_rows(n, carry):
+        scatter[pl.ds(row, 1), :] += jnp.where(real, dx_f32[pl.ds(order[i], 1), :], 0.0)
+
+    def token_rows(n, carry):
         for u in range(4):
             token_row(first_tok + n * 4 + u)
         return carry
-    lax.fori_loop(0, lax.div(end_tok - first_tok + 3, 4), more_rows, 0)
-
-    ids = lax.broadcasted_iota(jnp.int32, (chunk, tile), 0) + step * chunk
-
-    def product(j):
-        cols = slice(j * tile, (j + 1) * tile)
-        logits_out[:, cols] = lax.dot_general(embed[...], zb[cols, :], NT, preferred_element_type=F32)
-
-    product(0)
-    for j in range(tiles):
-        cols = slice(j * tile, (j + 1) * tile)
-        if j + 1 < tiles:
-            product(j + 1)
-        logits = logits_out[:, cols]
-        m_old = m_ref[:, cols]
-        m_new = jnp.maximum(m_old, jnp.max(logits, axis=0, keepdims=True))
-        m_ref[:, cols] = m_new
-        s_ref[:, cols] = s_ref[:, cols] * jnp.exp(m_old - m_new) + jnp.sum(jnp.exp(logits - m_new), axis=0, keepdims=True)
-        l_ref[:, cols] += jnp.sum(jnp.where(ids == lab[:, cols], logits, 0.0), axis=0, keepdims=True)
+    lax.fori_loop(0, lax.div(end_tok - first_tok + 3, 4), token_rows, 0)
 
     @pl.when(step == pl.num_programs(0) - 1)
     def _():
@@ -88,7 +110,7 @@
             stats[j, 2:8, :] = jnp.zeros((6, tile), F32)
 
 
-def token_stats(hidden, affine, lab, tok, here, embed, chunk, tile):
+def token_stats(hidden, affine, lab, tok, here, dx, embed, chunk, tile, ctx):
     tokens, d = hidden.shape
     vocab_loc = embed.shape[0]
     steps = vocab_loc // chunk
@@ -98,29 +120,32 @@
     starts = jnp.sum((key[None, :] < bounds[:, None]).astype(jnp.int32), axis=1)
     whole = pl.BlockSpec(memory_space=pltpu.VMEM)
     return pl.pallas_call(
-        functools.partial(stats_kernel, chunk, tile),
+        functools.partial(stats_kernel, chunk, tile, ctx),
         grid_spec=pltpu.PrefetchScalarGridSpec(
             num_scalar_prefetch=3,
             grid=(steps,),
-            in_specs=[whole, whole, whole, pl.BlockSpec((chunk, d), lambda i, *_: (i, 0))],
-            out_specs=(whole, whole, pl.BlockSpec((chunk, tokens), lambda i, *_: (i, 0)), whole),
-            scratch_shapes=[pltpu.VMEM((1, tokens), F32)] * 3),
+            in_specs=[whole, whole, whole, pl.BlockSpec(memory_space=pl.ANY), pl.BlockSpec((chunk, d), lambda i, *_: (i, 0))],
+            out_specs=(whole, whole, pl.BlockSpec((chunk, tokens), lambda i, *_: (i, 0)), whole,
+                       pl.BlockSpec((chunk, d), lambda i, *_: (i, 0)), whole),
+            scratch_shapes=[pltpu.VMEM((1, tokens), F32)] * 3 + [pltpu.VMEM((tokens, d), F32), pltpu.VMEM((2, tile, d), BF16),
+                                                               pltpu.SemaphoreType.DMA((2,))]),
         out_shape=(jax.ShapeDtypeStruct((tokens, d), BF16), jax.ShapeDtypeStruct((tokens // tile, 8, tile), F32),
-                   jax.ShapeDtypeStruct((vocab_loc, tokens), F32), jax.ShapeDtypeStruct((tokens + 8, d), F32)),
+                   jax.ShapeDtypeStruct((vocab_loc, tokens), F32), jax.ShapeDtypeStruct((tokens + 8, d), F32),
+                   jax.ShapeDtypeStruct((vocab_loc, d), F32), jax.ShapeDtypeStruct((ctx, d), F32)),
         compiler_params=pltpu.CompilerParams(vmem_limit_bytes=VMEM_LIMIT),
-        cost_estimate=pl.CostEstimate(flops=2 * tokens * d * vocab_loc, bytes_accessed=2 * embed.size + 4 * vocab_loc * tokens,
+        cost_estimate=pl.CostEstimate(flops=2 * tokens * d * vocab_loc, bytes_accessed=6 * embed.size + 4 * vocab_loc * tokens,
                                       transcendentals=tokens * vocab_loc),
         name='token_stats',
-    )(starts, order, skey, hidden, affine, lab, embed)
+    )(starts, order, skey, hidden, affine, lab, dx, embed)
 
 
 def grad_kernel(ntp, ndp, chunk, tile, zrows,
-                dx, stats, mask, lab, tok, affine, zb_hbm, hidden, embed, logits,
+                stats, mask, lab, affine, zb_hbm, hidden, embed, logits, scatter, pos,
                 out, loss, gz, own, d2d, rs_r, rs_l, gsave,
-                zb, lse, wgt, st_in, cnt_in, loss_in, lbuf, ebuf, gz_t, hbuf, gt, oh, acc, gbuf, ld_own, ld_d2d, s1, s2, fin, rs1, rs2, zin_r, zin_l, zout_r, zout_l, zfin,
-                st_s, st_r, cnt_s, cnt_r, loss_s, loss_r, zb_sem, l_sem, e_sem, gs_sem, gl_sem, h_sem, own_sem, d2d_s, d2d_r, ld_sem, rs1_s, rs1_r, rs2_s, rs2_r, fin_s, ag1_r, ag2_r, fwd_s, part_r,
+                zb, lse, wgt, st_in, cnt_in, loss_in, lbuf, ebuf, gz_t, gtile, hbuf, gt, sbuf, acc, gbuf, ld_own, ld_d2d, s1, s2, fin, rs1, rs2, zin_r, zin_l, zout_r, zout_l, zfin,
+                st_s, st_r, cnt_s, cnt_r, loss_s, loss_r, zb_sem, l_sem, e_sem, gs_sem, gl_sem, h_sem, s_sem, own_sem, d2d_s, d2d_r, ld_sem, rs1_s, rs1_r, rs2_s, rs2_r, fin_s, ag1_r, ag2_r, fwd_s, part_r,
                 zld, zrs_sr, zrs_sl, zrs_rr, zrs_rl, zfin_s, zag_rr, zag_rl, zfw_r, zfw_l):
-    tokens, d = dx.shape
+    tokens, d = zb_hbm.shape
     vocab_loc = embed.shape[0]
     nc = vocab_loc // chunk
     ncc = nc + 1
@@ -266,6 +291,14 @@
 
     zb_copy = pltpu.make_async_copy(zb_hbm, zb, zb_sem.at[0])
 
+    def s_copy(k):
+        return pltpu.make_async_copy(scatter.at[rows8(k * chunk, chunk)], sbuf, s_sem.at[0])
+
+    def z_product(u):
+        k, j = lax.div(u, tiles), lax.rem(u, tiles)
+        cols = pl.ds(pl.multiple_of(j * tile, tile), tile)
+        acc[cols, :] += jnp.dot(gtile[lax.rem(u, 2)], ebuf[lax.rem(k, 2)], preferred_element_type=F32)
+
     def z_unit(u, carry):
         k, j = lax.div(u, tiles), lax.rem(u, tiles)
         slot = lax.rem(k, 2)
@@ -275,20 +308,21 @@
             e_copy(k).wait()
             l_copy(k).wait()
 
-            @pl.when(k + 1 < nc)
-            def _():
-                e_copy(k + 1).start()
-                l_copy(k + 1).start()
-
             @pl.when(k >= 2)
             def _():
                 gs_copy(k - 1).wait()
+        z_product(jnp.maximum(u - 1, 0) + jnp.where(u == 0, 1, 0))
         cols = pl.ds(pl.multiple_of(j * tile, tile), tile)
         ids = lax.broadcasted_iota(jnp.int32, (chunk, tile), 0) + k * chunk
         hit = jnp.where(ids == lab[j], 1.0, 0.0)
         g = ((jnp.exp(lbuf[slot, :, cols] - lse[j]) - hit) * wgt[j]).astype(BF16)
         gz_t[slot, :, cols] = g
-        acc[cols, :] += lax.dot_general(g, ebuf[slot], TN, preferred_element_type=F32)
+        gtile[lax.rem(u, 2)] = g.T
+
+        @pl.when((j == 0) & (k + 1 < nc))
+        def _():
+            e_copy(k + 1).start()
+            l_copy(k + 1).start()
 
         @pl.when(j == tiles - 1)
         def _():
@@ -297,6 +331,10 @@
             @pl.when((k == 0) | (k == nc - 1))
             def _():
                 gs_copy(k).wait()
+
+        @pl.when(u == nc * tiles - 1)
+        def _():
+            z_product(u)
         return carry
 
     def g_unit(u, carry):
@@ -305,29 +343,25 @@
         @pl.when(n == 0)
         def _():
             gl_copy(k).start()
-
-            def one_hot(j, c):
-                cols = pl.ds(pl.multiple_of(j * tile, tile), tile)
-                ids = lax.broadcasted_iota(jnp.int32, (chunk, tile), 0) + k * chunk
-                oh[:, cols] = jnp.where(ids == tok[j], 1.0, 0.0).astype(BF16)
-                return c
-            lax.fori_loop(0, tiles, one_hot, 0)
-
             own_copy(k).wait()
             d2d_copy(k).wait_send()
-            gl_copy(k).wait()
+            s_copy(k).wait()
 
             @pl.when(k == 0)
             def _():
                 zb_copy.wait()
+            gl_copy(k).wait()
         cols = pl.ds(pl.multiple_of(n * ntile, ntile), ntile)
-        gbuf[:, cols] = (jnp.dot(gt[...], zb[:, cols], preferred_element_type=F32)
-                         + jnp.dot(oh[...], dx[:, cols], preferred_element_type=F32))
+        gbuf[:, cols] = sbuf[:, cols] + jnp.dot(gt[...], zb[:, cols], preferred_element_type=F32)
 
         @pl.when(n == ntiles - 1)
         def _():
             own_copy(k + 1).start()
             d2d_copy(k + 1).start()
+
+            @pl.when(k + 1 < nc)
+            def _():
+                s_copy(k + 1).start()
 
             @pl.when(k == nc - 1)
             def _():
@@ -550,36 +584,34 @@
                 def _():
                     zag(b, h, -1, zfw_l, zag_rl).start()
 
-    lead, g_first = 10, STEPS
+    lead, g_first = 8, STEPS
     nz, ng = nc * tiles, nc * ntiles
-    fast = (tiles * 12) // 7
+    slow, fast = -(-tiles * 8 // 7), tiles * 11 // 7
 
     def uz(i):
         late = jnp.maximum(i - 1 - lead, 0)
-        count = tiles + 1 + lax.div(jnp.minimum(i - 1, lead) * tiles + late * fast, STEPS)
+        count = tiles + lax.div(jnp.minimum(i - 1, lead) * slow + late * fast, STEPS)
         return jnp.where(i <= 0, 0, jnp.minimum(count, nz))
 
     def ug(i):
         return jnp.where(i <= 0, 0, jnp.minimum(ntiles + lax.div(jnp.maximum(i - g_first, 0) * ntiles, STEPS), ng))
 
-    lags = (('p', 0), ('a', 1), ('b', 4), ('c', 6), ('d', 10), ('w', 16), ('e', 16), ('f', 24))
+    lags = (('w', 17), ('f', 25), ('e', 21), ('d', 11), ('c', 8), ('b', 4), ('a', 1), ('p', 0))
     stages = {'w': stage_w, 'f': stage_f, 'e': stage_e, 'd': stage_d, 'c': stage_c, 'b': stage_b, 'a': stage_a,
               'p': load_start}
-    z_start = lead + -(-max(nz - (tiles + 1 + lead * tiles // STEPS), 0) * STEPS // fast)
-    hop = 4
-    steps = max((ncc - 1) * STEPS + 25, z_start + nb + hop * 2 * (ntp - 1))
+    z_start = lead + -(-max(nz - (tiles + lead * slow // STEPS), 0) * STEPS // fast)
+    hop = 3
+    steps = max((ncc - 1) * STEPS + 26, z_start + nb + hop * 2 * (ntp - 1))
     share_start()
     zb_copy.start()
     e_copy(0).start()
     l_copy(0).start()
 
-    def pos_rows(j, carry):
-        total = dx[rows8(j * eighth, eighth), :].astype(F32)
-        for b in range(1, tokens // chunk):
-            total = total + dx[pl.ds(pl.multiple_of(b * chunk + j * eighth, 8), eighth), :].astype(F32)
-        gbuf[rows8(j * eighth, eighth), :] = total
-        return carry
-    lax.fori_loop(0, 8, pos_rows, 0)
+    pos_copy = pltpu.make_async_copy(pos, gbuf, s_sem.at[0])
+    pos_copy.start()
+    gtile[...] = jnp.zeros_like(gtile)
+    pos_copy.wait()
+    s_copy(0).start()
     own_copy(0).start()
     d2d_copy(0).start()
 
@@ -650,7 +682,7 @@
     lax.fori_loop(0, nb, drain, 0)
 
 
-def gradients(ntp, ndp, zb, dx, stats, mask, lab, tok, affine, hidden, embed, logits, chunk, tile, zrows):
+def gradients(ntp, ndp, zb, stats, mask, lab, affine, hidden, embed, logits, scatter, pos, chunk, tile, zrows):
     tokens, d = zb.shape
     vocab_loc = embed.shape[0]
     nc = vocab_loc // chunk
@@ -669,28 +701,28 @@
         functools.partial(grad_kernel, ntp, ndp, chunk, tile, zrows),
         out_shape=(sds(vocab_loc + chunk, d), sds(8, 128), sds(tokens, d), sds(ncc, half, d), sds(ncc, half, d),
                    sds(nb, ntp - 1, zrows, d), sds(nb, ntp - 1, zrows, d), jax.ShapeDtypeStruct((nc, chunk, tokens), BF16)),
-        in_specs=[vm] * 6 + [hbm] * 4,
+        in_specs=[vm] * 4 + [hbm] * 6,
         out_specs=(hbm, vm) + (hbm,) * 6,
         scratch_shapes=[
             pltpu.VMEM((tokens, d), BF16), vf(tiles, 1, tile), vf(tiles, 1, tile), vf(ntp, tiles, 8, tile), vf(ndp, 8, 128), vf(ndp, 8, 128),
             vf(2, chunk, tokens),
-            pltpu.VMEM((2, chunk, d), BF16), pltpu.VMEM((2, chunk, tokens), BF16), pltpu.VMEM((zrows, d), BF16),
-            pltpu.VMEM((chunk, tokens), BF16), pltpu.VMEM((chunk, tokens), BF16),
+            pltpu.VMEM((2, chunk, d), BF16), pltpu.VMEM((2, chunk, tokens), BF16), pltpu.VMEM((2, tile, chunk), BF16),
+            pltpu.VMEM((zrows, d), BF16), pltpu.VMEM((chunk, tokens), BF16), vf(chunk, d),
             vf(tokens, d), vf(chunk, d), vf(half, d), vf(half, d),
             vf(RING, half, d), vf(RING, quarter, d), vf(RING, eighth, d), vf(SLOTS, quarter, d), vf(SLOTS, eighth, d),
             vf(ntp - 1, zrows, d), vf(ntp - 1, zrows, d), vf(RING, ntp - 1, zrows, d), vf(RING, ntp - 1, zrows, d),
             vf(RING, zrows, d),
             dma(ntp - 1), dma(ntp), dma(ndp - 1), dma(ndp), dma(ndp - 1), dma(ndp), dma(1), dma(2),
-            dma(2), dma(2), dma(1), dma(1), dma(1), dma(1), dma(ncc), dma(2), dma(RING), dma(SLOTS), dma(RING), dma(SLOTS), dma(4, RING),
+            dma(2), dma(2), dma(1), dma(1), dma(1), dma(1), dma(1), dma(ncc), dma(2), dma(RING), dma(SLOTS), dma(RING), dma(SLOTS), dma(4, RING),
             dma(ncc), dma(2, ncc), dma(3, RING), dma(3, ncc),
             dma(1), dma(RING), dma(RING), dma(nb), dma(nb), dma(3, RING), dma(nb, ntp - 1), dma(nb, ntp - 1),
             dma(nb, ntp - 1), dma(nb, ntp - 1),
         ],
         compiler_params=pltpu.CompilerParams(vmem_limit_bytes=VMEM_LIMIT, has_side_effects=True),
-        cost_estimate=pl.CostEstimate(flops=3 * flops, bytes_accessed=4 * vocab_loc * (4 * d + tokens),
+        cost_estimate=pl.CostEstimate(flops=2 * flops, bytes_accessed=4 * vocab_loc * (4 * d + tokens),
                                       transcendentals=tokens * vocab_loc),
         name='gradients',
-    )(dx, stats, rows(mask), rows(lab), rows(tok), affine, zb, hidden, embed, logits)
+    )(stats, rows(mask), rows(lab), affine, zb, hidden, embed, logits, scatter, pos)
     return res[:3]
 
 
@@ -734,10 +766,11 @@
         tok_here = (tok_local >= 0) & (tok_local < vocab_loc)
         hidden2 = hidden.reshape(ntok, d)
         affine = jnp.stack([ln_gain, ln_bias])
-        zb, stats, logits, rows = token_stats(hidden2, affine, lab_local, tok_local, tok_here, embed_loc, chunk1, tile)
+        zb, stats, logits, rows, scatter, pos = token_stats(hidden2, affine, lab_local, tok_local, tok_here,
+                                                            grad_x0.reshape(ntok, d), embed_loc, chunk1, tile, ctx)
         rows = lax.psum(rows, 'tp')
-        grads, loss, grad_h = gradients(ntp, ndp, zb, grad_x0.reshape(ntok, d), stats, lossmask.astype(F32), lab_local,
-                                        tok_local, affine, hidden2, embed_loc, logits, chunk, tile, zrows)
+        grads, loss, grad_h = gradients(ntp, ndp, zb, stats, lossmask.astype(F32), lab_local, affine, hidden2, embed_loc,
+                                        logits, scatter, pos, chunk, tile, zrows)
         grad_embed, grad_pos, embed_out, grad_hidden = finish(grads, rows, grad_h, pos_table, vocab_loc)
         mean_loss = loss[0, 0]
         embed_out = embed_out.reshape(batch, ctx, d)

time: 846 us -> 829 us (0.980)
  Pallas kernels: 817 us -> 800 us
    pallas_call x1, Pallas kernels: 657 us -> 629 us  [gradients(): pl.pallas_call(functools.partial(grad_kernel, ntp, ndp, chunk, tile, zrow...]
    pallas_call x1, Pallas kernels: 100 us -> 112 us  [token_stats(): pl.pallas_call(functools.partial(stats_kernel, chunk, tile, ctx), grid_sp...]
  transfers between devices with their start and end apart: 1 -> 1, of which waited for: 0 -> 0; matrix products, arithmetic and copies ran while one was open for 0% -> 0% of each run, Pallas kernels for 78% -> 76%
where the time goes in v5:
time: 829 us; the launch traced here: 826 us
  Pallas kernels  800 us (97%)
  between operations  14.1 us (2%)
    pallas_call x1, Pallas kernels, gradients(): pl.pallas_call(functools.partial(grad_kernel, ntp, ndp, chunk, tile, zrow...  629 us
    pallas_call x1, Pallas kernels, token_stats(): pl.pallas_call(functools.partial(stats_kernel, chunk, tile, ctx), grid_sp...  112 us
    pallas_call x1, Pallas kernels, finish(): pl.pallas_call(finish_kernel, grid=(n,), in_specs=[at(big), at(small, lam...  59.1 us
  transfers between devices with their start and end apart: 1, of which 0 were waited for; matrix products, arithmetic and copies ran while one was open for 0% of the time, Pallas kernels for 76%

profile of v5, /device:TPU:0, one launch (start us, length us, event | category | flops | bytes accessed | tf_op | source)
XLA Modules:
  0.0 826.2 jit_solution(4436021570520121357)
XLA Ops:
  7.2 0.0 all-reduce.2.cloned.1.call-start
  7.2 0.7 stack.9
  7.9 0.7 stack.10
  8.6 0.7 broadcast_subtract_fusion
  9.4 0.1 reshape.62
  9.4 0.7 convert_reduce_fusion.starts
  10.2 5.0 sort.15
  15.2 0.7 reshape.64.lab
  15.9 0.6 pad_maximum_fusion.affine
  16.5 111.6 %token_stats.1 = (bf16[1792,1280]{1,0:T(8,128)(2,1)}, f32[7,8,256]{2,1,0:T(8,128)}, f32[12992,1792]{1,0:T(8,128)}, f32[1800,1280]{1,0:T(8,128)}, f32[12992,1280]{1,0:T(8,128)}, /*index=5*/f32[448,1280]{1,0:T(8,128)}) custom-call(s32[15]{0:T(128)} %convert_reduce_fusion.starts, s32[1792]{0:T(1024)} %get-tuple-element.20.order, s32[1792]{0:T(1024)} %get-tuple-element.21.skey, ...), custom_call_target="tpu_custom_call" | custom-call | flops 59601059840 | bytes 192905216 | tf_op jit(solution)/shard_map/token_stats/pallas_call | solution.py:122
  128.1 0.0 copy-start
  128.1 0.0 all-reduce.2.cloned.1.call-update
  128.1 0.7 reshape_reshape.3.lab
  128.8 0.0 copy-done
  128.8 0.7 reshape.66.mask
  129.5 629.5 %gradients.1 = (f32[13440,1280]{1,0:T(8,128)}, f32[8,128]{1,0:T(8,128)}, f32[1792,1280]{1,0:T(8,128)}, f32[30,224,1280]{2,1,0:T(8,128)}, f32[30,224,1280]{2,1,0:...) custom-call(f32[7,8,256]{2,1,0:T(8,128)} %get-tuple-element.22.stats, ...), custom_call_target="tpu_custom_call" | custom-call | flops 119202119680 | bytes 359202816 | tf_op jit(solution)/shard_map/gradients/pallas_call | solution.py:700
  759.0 1.2 slice.3
  760.2 0.0 all-reduce.2.cloned.1.call-done.rows
  760.2 59.1 %finish.1 = (f32[12992,1280]{1,0:T(8,128)}, f32[448,1280]{1,0:T(8,128)}, bf16[1792,1280]{1,0:T(8,128)(2,1)}, bf16[1792,1280]{1,0:T(8,128)(2,1)}) custom-call(f32[13440,1280]{1,0:T(8,128)} %get-tuple-element.28.grad_in.pos_in, f32[13440,1280]{1,0:T(8,128)} %get-tuple-element.28.grad_in.pos_in, f32[1800,1280]{1,0:T(8,128)} %all-reduce.2.cloned.1.call-done.rows, ...), custom_call_target="tpu_custom_call" | custom-call | flops 2293760 | bytes 133038080 | tf_op jit(solution)/shard_map/finish/pallas_call | solution.py:742
  (4 shorter events, 0.0 us)
Async XLA Ops:
  7.2 753.0 %all-reduce.2.cloned.1.call-start = ((), (), s32[]{:S(2)}) async-start(), calls=%async_computation | async-start | bytes 18432000 | tf_op jit(solution)/shard_map/psum | solution.py:771
  128.1 0.7 copy-start
Sparse Core Ops, SparseCore 0:
  128.2 323.1 all-reduce.1

commit v6 on v5

--- a/solution.py
+++ b/solution.py
@@ -24,10 +24,11 @@
 
 
 def stats_kernel(chunk, tile, ctx, starts, order, skey, hidden, affine, lab, dx, embed,
-                 zb, stats, logits_out, rows_out, scatter, pos, m_ref, s_ref, l_ref, dx_f32, dx_in, dx_sem):
+                 zb_out, stats, logits_out, rows_out, scatter, pos_out, zb, pos, m_ref, s_ref, l_ref, dx_f32, dx_in, dx_sem, out_sem):
     step = pl.program_id(0)
     tokens, d = hidden.shape
     tiles = tokens // tile
+    early = (pltpu.make_async_copy(zb, zb_out, out_sem.at[0]), pltpu.make_async_copy(pos, pos_out, out_sem.at[1]))
 
     @pl.when(step == 0)
     def _():
@@ -58,6 +59,8 @@
                 dx_f32[pl.ds(pl.multiple_of(b * ctx + j * n, 8), n), :] for b in range(tokens // ctx)])
             return carry
         lax.fori_loop(0, 8, pos_rows, 0)
+        for c in early:
+            c.start()
         m_ref[...] = jnp.full_like(m_ref, -jnp.inf)
         s_ref[...] = jnp.zeros_like(s_ref)
         l_ref[...] = jnp.zeros_like(l_ref)
@@ -103,6 +106,8 @@
 
     @pl.when(step == pl.num_programs(0) - 1)
     def _():
+        for c in early:
+            c.wait()
         for j in range(tiles):
             cols = slice(j * tile, (j + 1) * tile)
             stats[j, 0:1, :] = m_ref[:, cols] + jnp.log(s_ref[:, cols])
@@ -125,10 +130,10 @@
             num_scalar_prefetch=3,
             grid=(steps,),
             in_specs=[whole, whole, whole, pl.BlockSpec(memory_space=pl.ANY), pl.BlockSpec((chunk, d), lambda i, *_: (i, 0))],
-            out_specs=(whole, whole, pl.BlockSpec((chunk, tokens), lambda i, *_: (i, 0)), whole,
-                       pl.BlockSpec((chunk, d), lambda i, *_: (i, 0)), whole),
-            scratch_shapes=[pltpu.VMEM((1, tokens), F32)] * 3 + [pltpu.VMEM((tokens, d), F32), pltpu.VMEM((2, tile, d), BF16),
-                                                               pltpu.SemaphoreType.DMA((2,))]),
+            out_specs=(pl.BlockSpec(memory_space=pl.ANY), whole, pl.BlockSpec((chunk, tokens), lambda i, *_: (i, 0)), whole,
+                       pl.BlockSpec((chunk, d), lambda i, *_: (i, 0)), pl.BlockSpec(memory_space=pl.ANY)),
+            scratch_shapes=[pltpu.VMEM((tokens, d), BF16), pltpu.VMEM((ctx, d), F32)] + [pltpu.VMEM((1, tokens), F32)] * 3 + [pltpu.VMEM((tokens, d), F32), pltpu.VMEM((2, tile, d), BF16),
+                                                               pltpu.SemaphoreType.DMA((2,)), pltpu.SemaphoreType.DMA((2,))]),
         out_shape=(jax.ShapeDtypeStruct((tokens, d), BF16), jax.ShapeDtypeStruct((tokens // tile, 8, tile), F32),
                    jax.ShapeDtypeStruct((vocab_loc, tokens), F32), jax.ShapeDtypeStruct((tokens + 8, d), F32),
                    jax.ShapeDtypeStruct((vocab_loc, d), F32), jax.ShapeDtypeStruct((ctx, d), F32)),
@@ -343,7 +348,10 @@
         @pl.when(n == 0)
         def _():
             gl_copy(k).start()
-            own_copy(k).wait()
+
+            @pl.when(k >= 1)
+            def _():
+                own_copy(k).wait()
             d2d_copy(k).wait_send()
             s_copy(k).wait()
 
@@ -584,22 +592,22 @@
                 def _():
                     zag(b, h, -1, zfw_l, zag_rl).start()
 
-    lead, g_first = 8, STEPS
+    lead, g_first = 18, STEPS
     nz, ng = nc * tiles, nc * ntiles
-    slow, fast = -(-tiles * 8 // 7), tiles * 11 // 7
+    fast = tiles * 13 // 7
 
     def uz(i):
         late = jnp.maximum(i - 1 - lead, 0)
-        count = tiles + lax.div(jnp.minimum(i - 1, lead) * slow + late * fast, STEPS)
+        count = tiles + 1 + lax.div(jnp.minimum(i - 1, lead) * tiles + late * fast, STEPS)
         return jnp.where(i <= 0, 0, jnp.minimum(count, nz))
 
     def ug(i):
         return jnp.where(i <= 0, 0, jnp.minimum(ntiles + lax.div(jnp.maximum(i - g_first, 0) * ntiles, STEPS), ng))
 
-    lags = (('w', 17), ('f', 25), ('e', 21), ('d', 11), ('c', 8), ('b', 4), ('a', 1), ('p', 0))
+    lags = (('w', 12, 10), ('f', 24, 18), ('c', 8, 6), ('b', 5, 3), ('d', 11, 9), ('e', 16, 14), ('p', 0, -1), ('a', 1, -1))
     stages = {'w': stage_w, 'f': stage_f, 'e': stage_e, 'd': stage_d, 'c': stage_c, 'b': stage_b, 'a': stage_a,
               'p': load_start}
-    z_start = lead + -(-max(nz - (tiles + lead * slow // STEPS), 0) * STEPS // fast)
+    z_start = lead + -(-max(nz - (tiles + 1 + lead * tiles // STEPS), 0) * STEPS // fast)
     hop = 3
     steps = max((ncc - 1) * STEPS + 26, z_start + nb + hop * 2 * (ntp - 1))
     share_start()
@@ -615,19 +623,25 @@
     own_copy(0).start()
     d2d_copy(0).start()
 
+    own_copy(0).wait()
+    load_start(0)
+
     def clear(j, carry):
         acc[pl.ds(pl.multiple_of(j * tile, tile), tile), :] = jnp.zeros((tile, d), F32)
         return carry
     lax.fori_loop(0, tiles, clear, 0)
+    stage_a(0)
     share_use()
 
     def one_step(i, carry):
         lax.fori_loop(uz(i), uz(i + 1), z_unit, 0)
         lax.fori_loop(ug(i), ug(i + 1), g_unit, 0)
-        for name, lag in lags:
-            @pl.when((i >= lag) & (i - lag < ncc * STEPS) & (lax.rem(i - lag + STEPS * 64, STEPS) == 0))
-            def _(name=name, lag=lag):
-                stages[name](lax.div(i - lag, STEPS))
+        for name, lag, first in lags:
+            later = (i - lag >= STEPS) & (i - lag < ncc * STEPS) & (lax.rem(i - lag + STEPS * 64, STEPS) == 0)
+
+            @pl.when(later | (i == first))
+            def _(name=name, lag=lag, first=first):
+                stages[name](jnp.where(i == first, 0, lax.div(i - lag, STEPS)))
         zt = i - z_start
 
         @pl.when(valid(zt - hop * z, nb))
@@ -726,11 +740,46 @@
     return res[:3]
 
 
-def finish_kernel(grad_in, pos_in, rows, gh_in, pos_table, grad_out, pos_out, embed_out, gh_out):
-    grad_out[...] = grad_in[...]
+def finish_kernel(grads, pos_in, rows, gh_in, pos_table, grad_out, pos_out, embed_out, gh_out, ring, in_sem, out_sem):
+    i, n = pl.program_id(0), pl.num_programs(0)
+    slots, size = ring.shape[0], ring.shape[1]
+    ahead = slots - 2
+
+    def block(k):
+        return pl.ds(pl.multiple_of(k * size, 8), size)
+
+    def take(k):
+        return pltpu.make_async_copy(grads.at[block(k)], ring.at[lax.rem(k, slots)], in_sem.at[lax.rem(k, slots)])
+
+    def give(k):
+        return pltpu.make_async_copy(ring.at[lax.rem(k, slots)], grad_out.at[block(k)], out_sem.at[lax.rem(k, slots)])
+
+    @pl.when(i == 0)
+    def _():
+        def first(k, carry):
+            take(k).start()
+            return carry
+        lax.fori_loop(0, jnp.minimum(ahead, n), first, 0)
+
+    @pl.when(i >= 2)
+    def _():
+        give(i - 2).wait()
+
+    @pl.when(i + ahead < n)
+    def _():
+        take(i + ahead).start()
+    take(i).wait()
+    give(i).start()
     pos_out[...] = pos_in[...]
     embed_out[...] = (rows[...] + pos_table[...].astype(F32)).astype(BF16)
     gh_out[...] = gh_in[...].astype(BF16)
+
+    @pl.when(i == n - 1)
+    def _():
+        @pl.when(i >= 1)
+        def _():
+            give(i - 1).wait()
+        give(i).wait()
 
 
 def finish(grads, rows, grad_h, pos_table, vocab_loc):
@@ -742,8 +791,9 @@
     return pl.pallas_call(
         finish_kernel,
         grid=(n,),
-        in_specs=[at(big), at(small, lambda i: vocab_loc // small + i), at(mid), at(mid), at(mid, lambda i: lax.rem(i, ctx // mid))],
-        out_specs=(at(big), at(small), at(mid), at(mid)),
+        in_specs=[pl.BlockSpec(memory_space=pl.ANY), at(small, lambda i: vocab_loc // small + i), at(mid), at(mid), at(mid, lambda i: lax.rem(i, ctx // mid))],
+        out_specs=(pl.BlockSpec(memory_space=pl.ANY), at(small), at(mid), at(mid)),
+        scratch_shapes=[pltpu.VMEM((8, big, d), F32), pltpu.SemaphoreType.DMA((8,)), pltpu.SemaphoreType.DMA((8,))],
         out_shape=(jax.ShapeDtypeStruct((vocab_loc, d), F32), jax.ShapeDtypeStruct((ctx, d), F32),
                    jax.ShapeDtypeStruct((tokens, d), BF16), jax.ShapeDtypeStruct((tokens, d), BF16)),
         compiler_params=pltpu.CompilerParams(vmem_limit_bytes=VMEM_LIMIT),

time: 829 us -> 828 us (level)
  transfers between devices with their start and end apart: 1 -> 1, of which waited for: 0 -> 0; matrix products, arithmetic and copies ran while one was open for 0% -> 0% of each run, Pallas kernels for 76% -> 77%
where the time goes in v6:
time: 828 us; the launch traced here: 825 us
  Pallas kernels  799 us (96%)
  between operations  14.1 us (2%)
    pallas_call x1, Pallas kernels, gradients(): pl.pallas_call(functools.partial(grad_kernel, ntp, ndp, chunk, tile, zrow...  632 us
    pallas_call x1, Pallas kernels, token_stats(): pl.pallas_call(functools.partial(stats_kernel, chunk, tile, ctx), grid_sp...  110 us
    pallas_call x1, Pallas kernels, finish(): pl.pallas_call(finish_kernel, grid=(n,), in_specs=[pl.BlockSpec(memory_sp...  57.2 us
  transfers between devices with their start and end apart: 1, of which 0 were waited for; matrix products, arithmetic and copies ran while one was open for 0% of the time, Pallas kernels for 77%

profile of v6, /device:TPU:0, one launch (start us, length us, event | category | flops | bytes accessed | tf_op | source)
XLA Modules:
  0.0 825.2 jit_solution(14209439656636917760)
XLA Ops:
  7.2 0.0 all-reduce.2.cloned.1.call-start
  7.2 0.7 stack.9
  7.9 0.7 stack.10
  8.6 0.7 broadcast_subtract_fusion
  9.4 0.1 reshape.62
  9.4 0.7 convert_reduce_fusion.starts
  10.2 5.0 sort.15
  15.2 0.7 reshape.64.lab
  15.9 0.6 pad_maximum_fusion.affine
  16.5 110.1 %token_stats.1 = (bf16[1792,1280]{1,0:T(8,128)(2,1)}, f32[7,8,256]{2,1,0:T(8,128)}, f32[12992,1792]{1,0:T(8,128)}, f32[1800,1280]{1,0:T(8,128)}, f32[12992,1280]{1,0:T(8,128)}, /*index=5*/f32[448,1280]{1,0:T(8,128)}) custom-call(s32[15]{0:T(128)} %convert_reduce_fusion.starts, s32[1792]{0:T(1024)} %get-tuple-element.20.order, s32[1792]{0:T(1024)} %get-tuple-element.21.skey, ...), custom_call_target="tpu_custom_call" | custom-call | flops 59601059840 | bytes 192905216 | tf_op jit(solution)/shard_map/token_stats/pallas_call | solution.py:127
  126.6 0.0 copy-start
  126.6 0.0 all-reduce.2.cloned.1.call-update
  126.7 0.7 reshape_reshape.3.lab
  127.4 0.0 copy-done
  127.4 0.7 reshape.66.mask
  128.1 631.9 %gradients.1 = (f32[13440,1280]{1,0:T(8,128)}, f32[8,128]{1,0:T(8,128)}, f32[1792,1280]{1,0:T(8,128)}, f32[30,224,1280]{2,1,0:T(8,128)}, f32[30,224,1280]{2,1,0:...) custom-call(f32[7,8,256]{2,1,0:T(8,128)} %get-tuple-element.22.stats, ...), custom_call_target="tpu_custom_call" | custom-call | flops 119202119680 | bytes 359202816 | tf_op jit(solution)/shard_map/gradients/pallas_call | solution.py:714
  759.9 1.2 slice.3
  761.1 0.0 all-reduce.2.cloned.1.call-done.rows
  761.1 57.2 %finish.1 = (f32[12992,1280]{1,0:T(8,128)}, f32[448,1280]{1,0:T(8,128)}, bf16[1792,1280]{1,0:T(8,128)(2,1)}, bf16[1792,1280]{1,0:T(8,128)(2,1)}) custom-call(f32[13440,1280]{1,0:T(8,128)} %get-tuple-element.28.grads.pos_in, f32[13440,1280]{1,0:T(8,128)} %get-tuple-element.28.grads.pos_in, f32[1800,1280]{1,0:T(8,128)} %all-reduce.2.cloned.1.call-done.rows, ...), custom_call_target="tpu_custom_call" | custom-call | flops 2293760 | bytes 133038080 | tf_op jit(solution)/shard_map/finish/pallas_call | solution.py:791
  (4 shorter events, 0.0 us)
Async XLA Ops:
  7.2 753.9 %all-reduce.2.cloned.1.call-start = ((), (), s32[]{:S(2)}) async-start(), calls=%async_computation | async-start | bytes 18432000 | tf_op jit(solution)/shard_map/psum | solution.py:821
  126.6 0.7 copy-start
Sparse Core Ops, SparseCore 0:
  126.8 322.5 all-reduce.1

commit v7 on v6

--- a/solution.py
+++ b/solution.py
@@ -147,7 +147,7 @@
 def grad_kernel(ntp, ndp, chunk, tile, zrows,
                 stats, mask, lab, affine, zb_hbm, hidden, embed, logits, scatter, pos,
                 out, loss, gz, own, d2d, rs_r, rs_l, gsave,
-                zb, lse, wgt, st_in, cnt_in, loss_in, lbuf, ebuf, gz_t, gtile, hbuf, gt, sbuf, acc, gbuf, ld_own, ld_d2d, s1, s2, fin, rs1, rs2, zin_r, zin_l, zout_r, zout_l, zfin,
+                zb, lse, wgt, st_in, cnt_in, loss_in, lbuf, ebuf, gz_t, gtile, hbuf, gt, sbuf, acc, gbuf, ld_own, ld_d2d, s1, s2, fin, rs1, rs2, zin_r, zin_l, zfin_r, zfin_l, zout_r, zout_l, zfin,
                 st_s, st_r, cnt_s, cnt_r, loss_s, loss_r, zb_sem, l_sem, e_sem, gs_sem, gl_sem, h_sem, s_sem, own_sem, d2d_s, d2d_r, ld_sem, rs1_s, rs1_r, rs2_s, rs2_r, fin_s, ag1_r, ag2_r, fwd_s, part_r,
                 zld, zrs_sr, zrs_sl, zrs_rr, zrs_rl, zfin_s, zag_rr, zag_rl, zfw_r, zfw_l):
     tokens, d = zb_hbm.shape
@@ -468,16 +468,53 @@
         return zdma(zout_l.at[lax.rem(b, RING), pl.ds(0, i)], rs_l.at[b, pl.ds(0, i)], zrs_sl.at[lax.rem(b, RING)],
                     zrs_rl.at[b], i - 1)
 
+    def right_load(b, i):
+        n = ntp - 1 - i
+        return pltpu.make_async_copy(rs_r.at[b, pl.ds(i, n)], zin_r.at[pl.ds(i, n)], zld.at[0])
+
+    def left_load(b, i):
+        return pltpu.make_async_copy(rs_l.at[b, pl.ds(0, i)], zin_l.at[pl.ds(0, i)], zld.at[1])
+
+    def final_loads(b, i):
+        loads = [pltpu.make_async_copy(hidden.at[rows8(z * qrows + b * zrows, zrows)], hbuf, h_sem.at[0])]
+        if i > 0:
+            loads.append(pltpu.make_async_copy(rs_r.at[b, i - 1], zfin_r, zld.at[2]))
+        if i < ntp - 1:
+            loads.append(pltpu.make_async_copy(rs_l.at[b, i], zfin_l, zld.at[3]))
+        return loads
+
+    def z_right_head(b):
+        for i in range(1, ntp - 1):
+            @pl.when(z == i)
+            def _(i=i):
+                right_copy(b, i - 1).wait_recv()
+                right_load(b, i).start()
+
+    def z_left_head(b):
+        for i in range(1, ntp - 1):
+            @pl.when(z == i)
+            def _(i=i):
+                left_copy(b, i + 1).wait_recv()
+                left_load(b, i).start()
+
+    def z_final_head(b):
+        for i in range(ntp):
+            @pl.when(z == i)
+            def _(i=i):
+                if i == ntp - 1:
+                    right_copy(b, i - 1).wait_recv()
+                if i == 0:
+                    left_copy(b, i + 1).wait_recv()
+                for c in final_loads(b, i):
+                    c.start()
+
     def z_right(b):
         for i in range(ntp - 1):
             @pl.when(z == i)
             def _(i=i):
                 n = ntp - 1 - i
                 if i > 0:
-                    right_copy(b, i - 1).wait_recv()
-                    load = pltpu.make_async_copy(rs_r.at[b, pl.ds(i, n)], zin_r.at[pl.ds(i, n)], zld.at[0])
-                    load.start()
-                    load.wait()
+                    right_load(b, i).wait()
 
                 @pl.when(b >= RING)
                 def _():
@@ -492,10 +529,7 @@
             @pl.when(z == i)
             def _(i=i):
                 if i < ntp - 1:
-                    left_copy(b, i + 1).wait_recv()
-                    load = pltpu.make_async_copy(rs_l.at[b, pl.ds(0, i)], zin_l.at[pl.ds(0, i)], zld.at[0])
-                    load.start()
-                    load.wait()
+                    left_load(b, i).wait()
 
                 @pl.when(b >= RING)
                 def _():
@@ -513,29 +547,18 @@
                 zdma(zfin.at[s], dst, zfin_s.at[2, s], zag_rl.at[b, 0], z - 1))
 
     def z_final(b):
-        load_h = pltpu.make_async_copy(hidden.at[rows8(z * qrows + b * zrows, zrows)], hbuf, h_sem.at[0])
-        load_h.start()
         for i in range(ntp):
             @pl.when(z == i)
             def _(i=i):
-                if i > 0:
-                    right_copy(b, i - 1).wait_recv() if i == ntp - 1 else None
-                    load = pltpu.make_async_copy(rs_r.at[b, i - 1], zin_r.at[i - 1], zld.at[0])
-                    load.start()
-                    load.wait()
-                if i < ntp - 1:
-                    left_copy(b, i + 1).wait_recv() if i == 0 else None
-                    load = pltpu.make_async_copy(rs_l.at[b, i], zin_l.at[i], zld.at[0])
-                    load.start()
-                    load.wait()
+                for c in final_loads(b, i):
+                    c.wait()
                 z_wait_fin(b - RING, b >= RING)
                 total = acc[pl.ds(zacc(i, b), zrows), :]
                 if i > 0:
-                    total = zin_r[i - 1] + total
+                    total = zfin_r[...] + total
                 if i < ntp - 1:
-                    total = total + zin_l[i]
+                    total = total + zfin_l[...]
                 zfin[lax.rem(b, RING)] = total
-        load_h.wait()
         h = hbuf[...].astype(F32)
         centered = h - jnp.mean(h, axis=-1, keepdims=True)
         rstd = lax.rsqrt(jnp.mean(centered * centered, axis=-1, keepdims=True) + 1e-5)
@@ -634,6 +657,15 @@
     share_use()
 
     def one_step(i, carry):
+        zt = i - z_start
+        right_b, left_b, final_b = zt - hop * z, zt - hop * (ntp - 1 - z), zt - hop * (ntp - 1)
+
+        def z_stages(*stage_of):
+            for b, stage in zip((right_b, left_b, final_b), stage_of):
+                @pl.when(valid(b, nb))
+                def _(b=b, stage=stage):
+                    stage(b)
+        z_stages(z_right_head, z_left_head, z_final_head)
         lax.fori_loop(uz(i), uz(i + 1), z_unit, 0)
         lax.fori_loop(ug(i), ug(i + 1), g_unit, 0)
         for name, lag, first in lags:
@@ -642,19 +674,7 @@
             @pl.when(later | (i == first))
             def _(name=name, lag=lag, first=first):
                 stages[name](jnp.where(i == first, 0, lax.div(i - lag, STEPS)))
-        zt = i - z_start
-
-        @pl.when(valid(zt - hop * z, nb))
-        def _():
-            z_right(zt - hop * z)
-
-        @pl.when(valid(zt - hop * (ntp - 1 - z), nb))
-        def _():
-            z_left(zt - hop * (ntp - 1 - z))
-
-        @pl.when(valid(zt - hop * (ntp - 1), nb))
-        def _():
-            z_final(zt - hop * (ntp - 1))
+        z_stages(z_right, z_left, z_final)
         for h in range(1, ntp):
             @pl.when(valid(zt - hop * (ntp - 1 + h), nb))
             def _(h=h):
@@ -724,12 +744,12 @@
             pltpu.VMEM((zrows, d), BF16), pltpu.VMEM((chunk, tokens), BF16), vf(chunk, d),
             vf(tokens, d), vf(chunk, d), vf(half, d), vf(half, d),
             vf(RING, half, d), vf(RING, quarter, d), vf(RING, eighth, d), vf(SLOTS, quarter, d), vf(SLOTS, eighth, d),
-            vf(ntp - 1, zrows, d), vf(ntp - 1, zrows, d), vf(RING, ntp - 1, zrows, d), vf(RING, ntp - 1, zrows, d),
+            vf(ntp - 1, zrows, d), vf(ntp - 1, zrows, d), vf(zrows, d), vf(zrows, d), vf(RING, ntp - 1, zrows, d), vf(RING, ntp - 1, zrows, d),
             vf(RING, zrows, d),
             dma(ntp - 1), dma(ntp), dma(ndp - 1), dma(ndp), dma(ndp - 1), dma(ndp), dma(1), dma(2),
             dma(2), dma(2), dma(1), dma(1), dma(1), dma(1), dma(1), dma(ncc), dma(2), dma(RING), dma(SLOTS), dma(RING), dma(SLOTS), dma(4, RING),
             dma(ncc), dma(2, ncc), dma(3, RING), dma(3, ncc),
-            dma(1), dma(RING), dma(RING), dma(nb), dma(nb), dma(3, RING), dma(nb, ntp - 1), dma(nb, ntp - 1),
+            dma(4), dma(RING), dma(RING), dma(nb), dma(nb), dma(3, RING), dma(nb, ntp - 1), dma(nb, ntp - 1),
             dma(nb, ntp - 1), dma(nb, ntp - 1),
         ],
         compiler_params=pltpu.CompilerParams(vmem_limit_bytes=VMEM_LIMIT, has_side_effects=True),

time: 828 us -> 829 us (level)
  no operation moved by 1% of the time
where the time goes in v7:
time: 829 us; the launch traced here: 826 us
  Pallas kernels  800 us (97%)
  between operations  14.1 us (2%)
    pallas_call x1, Pallas kernels, gradients(): pl.pallas_call(functools.partial(grad_kernel, ntp, ndp, chunk, tile, zrow...  634 us
    pallas_call x1, Pallas kernels, token_stats(): pl.pallas_call(functools.partial(stats_kernel, chunk, tile, ctx), grid_sp...  108 us
    pallas_call x1, Pallas kernels, finish(): pl.pallas_call(finish_kernel, grid=(n,), in_specs=[pl.BlockSpec(memory_sp...  57.2 us
  transfers between devices with their start and end apart: 1, of which 0 were waited for; matrix products, arithmetic and copies ran while one was open for 0% of the time, Pallas kernels for 77%

profile of v7, /device:TPU:0, one launch (start us, length us, event | category | flops | bytes accessed | tf_op | source)
XLA Modules:
  0.0 825.9 jit_solution(17973667548080530536)
XLA Ops:
  7.2 0.0 all-reduce.2.cloned.1.call-start
  7.2 0.7 stack.9
  7.9 0.7 stack.10
  8.6 0.7 broadcast_subtract_fusion
  9.4 0.1 reshape.62
  9.4 0.7 convert_reduce_fusion.starts
  10.2 5.0 sort.15
  15.2 0.7 reshape.64.lab
  15.9 0.6 pad_maximum_fusion.affine
  16.5 108.5 %token_stats.1 = (bf16[1792,1280]{1,0:T(8,128)(2,1)}, f32[7,8,256]{2,1,0:T(8,128)}, f32[12992,1792]{1,0:T(8,128)}, f32[1800,1280]{1,0:T(8,128)}, f32[12992,1280]{1,0:T(8,128)}, /*index=5*/f32[448,1280]{1,0:T(8,128)}) custom-call(s32[15]{0:T(128)} %convert_reduce_fusion.starts, s32[1792]{0:T(1024)} %get-tuple-element.20.order, s32[1792]{0:T(1024)} %get-tuple-element.21.skey, ...), custom_call_target="tpu_custom_call" | custom-call | flops 59601059840 | bytes 192905216 | tf_op jit(solution)/shard_map/token_stats/pallas_call | solution.py:127
  125.0 0.0 copy-start
  125.0 0.0 all-reduce.2.cloned.1.call-update
  125.0 0.7 reshape_reshape.3.lab
  125.7 0.0 copy-done
  125.7 0.7 reshape.66.mask
  126.4 634.3 %gradients.1 = (f32[13440,1280]{1,0:T(8,128)}, f32[8,128]{1,0:T(8,128)}, f32[1792,1280]{1,0:T(8,128)}, f32[30,224,1280]{2,1,0:T(8,128)}, f32[30,224,1280]{2,1,0:...) custom-call(f32[7,8,256]{2,1,0:T(8,128)} %get-tuple-element.22.stats, ...), custom_call_target="tpu_custom_call" | custom-call | flops 119202119680 | bytes 359202816 | tf_op jit(solution)/shard_map/gradients/pallas_call | solution.py:734
  760.7 1.2 slice.3
  761.9 0.0 all-reduce.2.cloned.1.call-done.rows
  761.9 57.2 %finish.1 = (f32[12992,1280]{1,0:T(8,128)}, f32[448,1280]{1,0:T(8,128)}, bf16[1792,1280]{1,0:T(8,128)(2,1)}, bf16[1792,1280]{1,0:T(8,128)(2,1)}) custom-call(f32[13440,1280]{1,0:T(8,128)} %get-tuple-element.28.grads.pos_in, f32[13440,1280]{1,0:T(8,128)} %get-tuple-element.28.grads.pos_in, f32[1800,1280]{1,0:T(8,128)} %all-reduce.2.cloned.1.call-done.rows, ...), custom_call_target="tpu_custom_call" | custom-call | flops 2293760 | bytes 133038080 | tf_op jit(solution)/shard_map/finish/pallas_call | solution.py:811
  (4 shorter events, 0.0 us)
Async XLA Ops:
  7.2 754.7 %all-reduce.2.cloned.1.call-start = ((), (), s32[]{:S(2)}) async-start(), calls=%async_computation | async-start | bytes 18432000 | tf_op jit(solution)/shard_map/psum | solution.py:841
  125.0 0.7 copy-start
Sparse Core Ops, SparseCore 0:
  125.1 324.3 all-reduce.1

commit v8 on v7

--- a/solution.py
+++ b/solution.py
@@ -23,12 +23,12 @@
     return 64, 64, 128, 8
 
 
-def stats_kernel(chunk, tile, ctx, starts, order, skey, hidden, affine, lab, dx, embed,
-                 zb_out, stats, logits_out, rows_out, scatter, pos_out, zb, pos, m_ref, s_ref, l_ref, dx_f32, dx_in, dx_sem, out_sem):
+def stats_kernel(chunk, tile, starts, order, skey, hidden, affine, lab, dx, embed,
+                 zb_out, stats, logits_out, rows_out, scatter, zb, m_ref, s_ref, l_ref, dx_f32, dx_in, dx_sem, out_sem):
     step = pl.program_id(0)
     tokens, d = hidden.shape
     tiles = tokens // tile
-    early = (pltpu.make_async_copy(zb, zb_out, out_sem.at[0]), pltpu.make_async_copy(pos, pos_out, out_sem.at[1]))
+    early = pltpu.make_async_copy(zb, zb_out, out_sem.at[0])
 
     @pl.when(step == 0)
     def _():
@@ -53,14 +53,7 @@
             return carry
         lax.fori_loop(0, tiles, norm, 0)
 
-        def pos_rows(j, carry):
-            n = ctx // 8
-            pos[pl.ds(pl.multiple_of(j * n, 8), n), :] = functools.reduce(jnp.add, [
-                dx_f32[pl.ds(pl.multiple_of(b * ctx + j * n, 8), n), :] for b in range(tokens // ctx)])
-            return carry
-        lax.fori_loop(0, 8, pos_rows, 0)
-        for c in early:
-            c.start()
+        early.start()
         m_ref[...] = jnp.full_like(m_ref, -jnp.inf)
         s_ref[...] = jnp.zeros_like(s_ref)
         l_ref[...] = jnp.zeros_like(l_ref)
@@ -106,8 +99,7 @@
 
     @pl.when(step == pl.num_programs(0) - 1)
     def _():
-        for c in early:
-            c.wait()
+        early.wait()
         for j in range(tiles):
             cols = slice(j * tile, (j + 1) * tile)
             stats[j, 0:1, :] = m_ref[:, cols] + jnp.log(s_ref[:, cols])
@@ -115,7 +107,7 @@
             stats[j, 2:8, :] = jnp.zeros((6, tile), F32)
 
 
-def token_stats(hidden, affine, lab, tok, here, dx, embed, chunk, tile, ctx):
+def token_stats(hidden, affine, lab, tok, here, dx, embed, chunk, tile):
     tokens, d = hidden.shape
     vocab_loc = embed.shape[0]
     steps = vocab_loc // chunk
@@ -125,18 +117,18 @@
     starts = jnp.sum((key[None, :] < bounds[:, None]).astype(jnp.int32), axis=1)
     whole = pl.BlockSpec(memory_space=pltpu.VMEM)
     return pl.pallas_call(
-        functools.partial(stats_kernel, chunk, tile, ctx),
+        functools.partial(stats_kernel, chunk, tile),
         grid_spec=pltpu.PrefetchScalarGridSpec(
             num_scalar_prefetch=3,
             grid=(steps,),
             in_specs=[whole, whole, whole, pl.BlockSpec(memory_space=pl.ANY), pl.BlockSpec((chunk, d), lambda i, *_: (i, 0))],
             out_specs=(pl.BlockSpec(memory_space=pl.ANY), whole, pl.BlockSpec((chunk, tokens), lambda i, *_: (i, 0)), whole,
-                       pl.BlockSpec((chunk, d), lambda i, *_: (i, 0)), pl.BlockSpec(memory_space=pl.ANY)),
-            scratch_shapes=[pltpu.VMEM((tokens, d), BF16), pltpu.VMEM((ctx, d), F32)] + [pltpu.VMEM((1, tokens), F32)] * 3 + [pltpu.VMEM((tokens, d), F32), pltpu.VMEM((2, tile, d), BF16),
-                                                               pltpu.SemaphoreType.DMA((2,)), pltpu.SemaphoreType.DMA((2,))]),
+                       pl.BlockSpec((chunk, d), lambda i, *_: (i, 0))),
+            scratch_shapes=[pltpu.VMEM((tokens, d), BF16)] + [pltpu.VMEM((1, tokens), F32)] * 3 + [pltpu.VMEM((tokens, d), F32), pltpu.VMEM((2, tile, d), BF16),
+                                                               pltpu.SemaphoreType.DMA((2,)), pltpu.SemaphoreType.DMA((1,))]),
         out_shape=(jax.ShapeDtypeStruct((tokens, d), BF16), jax.ShapeDtypeStruct((tokens // tile, 8, tile), F32),
                    jax.ShapeDtypeStruct((vocab_loc, tokens), F32), jax.ShapeDtypeStruct((tokens + 8, d), F32),
-                   jax.ShapeDtypeStruct((vocab_loc, d), F32), jax.ShapeDtypeStruct((ctx, d), F32)),
+                   jax.ShapeDtypeStruct((vocab_loc, d), F32)),
         compiler_params=pltpu.CompilerParams(vmem_limit_bytes=VMEM_LIMIT),
         cost_estimate=pl.CostEstimate(flops=2 * tokens * d * vocab_loc, bytes_accessed=6 * embed.size + 4 * vocab_loc * tokens,
                                       transcendentals=tokens * vocab_loc),
@@ -145,7 +137,7 @@
 
 
 def grad_kernel(ntp, ndp, chunk, tile, zrows,
-                stats, mask, lab, affine, zb_hbm, hidden, embed, logits, scatter, pos,
+                stats, mask, lab, affine, zb_hbm, hidden, embed, logits, scatter,
                 out, loss, gz, own, d2d, rs_r, rs_l, gsave,
                 zb, lse, wgt, st_in, cnt_in, loss_in, lbuf, ebuf, gz_t, gtile, hbuf, gt, sbuf, acc, gbuf, ld_own, ld_d2d, s1, s2, fin, rs1, rs2, zin_r, zin_l, zfin_r, zfin_l, zout_r, zout_l, zfin,
                 st_s, st_r, cnt_s, cnt_r, loss_s, loss_r, zb_sem, l_sem, e_sem, gs_sem, gl_sem, h_sem, s_sem, own_sem, d2d_s, d2d_r, ld_sem, rs1_s, rs1_r, rs2_s, rs2_r, fin_s, ag1_r, ag2_r, fwd_s, part_r,
@@ -153,7 +145,6 @@
     tokens, d = zb_hbm.shape
     vocab_loc = embed.shape[0]
     nc = vocab_loc // chunk
-    ncc = nc + 1
     tiles = tokens // tile
     ntile = 256 if d % 256 == 0 and d > 256 else 128
     ntiles = d // ntile
@@ -182,9 +173,6 @@
         return pltpu.make_async_remote_copy(src_ref=src, dst_ref=dst, send_sem=ssem, recv_sem=rsem,
                                             device_id={'tp': dev}, device_id_type=MESH)
 
-    def row0(c):
-        return lax.rem(c + nc, ncc) * chunk
-
     def rows8(start, n):
         return pl.ds(pl.multiple_of(start, 8), n)
 
@@ -223,7 +211,7 @@
     def fin_copies(k):
         n1, n2, a1, a2 = place(k)
         b = lax.rem(k, RING)
-        dst = out.at[rows8(row0(k) + core * half + a1 * quarter + a2 * eighth, eighth)]
+        dst = out.at[rows8(k * chunk + core * half + a1 * quarter + a2 * eighth, eighth)]
         src = fin.at[b]
         return (pltpu.make_async_copy(src, dst, fin_s.at[0, b]),
                 rdma(src, dst, fin_s.at[1, b], ag1_r.at[k], n2),
@@ -233,13 +221,13 @@
     def fwd_copies(k):
         n1, _, a1, a2 = place(k)
         b = lax.rem(k, RING)
-        ref = out.at[rows8(row0(k) + core * half + a1 * quarter + (1 - a2) * eighth, eighth)]
+        ref = out.at[rows8(k * chunk + core * half + a1 * quarter + (1 - a2) * eighth, eighth)]
         return (rdma(ref, ref, fwd_s.at[0, b], ag2_r.at[1, k], n1),
                 rdma(ref, ref, fwd_s.at[1, b], part_r.at[1, k], partner))
 
     def last_copy(k):
         _, _, a1, _ = place(k)
-        ref = out.at[rows8(row0(k) + core * half + (1 - a1) * quarter, quarter)]
+        ref = out.at[rows8(k * chunk + core * half + (1 - a1) * quarter, quarter)]
         return rdma(ref, ref, fwd_s.at[2, lax.rem(k, RING)], part_r.at[2, k], partner)
 
     def peer(i, n, me):
@@ -351,8 +339,7 @@
 
             @pl.when(k >= 1)
             def _():
-                own_copy(k).wait()
-            d2d_copy(k).wait_send()
+                d2d_copy(k - 1).wait_send()
             s_copy(k).wait()
 
             @pl.when(k == 0)
@@ -364,8 +351,8 @@
 
         @pl.when(n == ntiles - 1)
         def _():
-            own_copy(k + 1).start()
-            d2d_copy(k + 1).start()
+            own_copy(k).start()
+            d2d_copy(k).start()
 
             @pl.when(k + 1 < nc)
             def _():
@@ -373,11 +360,11 @@
 
             @pl.when(k == nc - 1)
             def _():
-                own_copy(k + 1).wait()
-                d2d_copy(k + 1).wait_send()
+                d2d_copy(k).wait_send()
         return carry
 
     def load_start(k):
+        own_copy(k).wait()
         d2d_copy(k).wait_recv()
         pltpu.make_async_copy(own.at[k], ld_own, ld_sem.at[0]).start()
         pltpu.make_async_copy(d2d.at[k], ld_d2d, ld_sem.at[1]).start()
@@ -627,33 +614,24 @@
     def ug(i):
         return jnp.where(i <= 0, 0, jnp.minimum(ntiles + lax.div(jnp.maximum(i - g_first, 0) * ntiles, STEPS), ng))
 
-    lags = (('w', 12, 10), ('f', 24, 18), ('c', 8, 6), ('b', 5, 3), ('d', 11, 9), ('e', 16, 14), ('p', 0, -1), ('a', 1, -1))
+    lags = (('w', 13, 11), ('f', 25, 20), ('c', 9, 7), ('b', 6, 4), ('d', 12, 10), ('e', 17, 15), ('p', 1, 0), ('a', 2, 1))
     stages = {'w': stage_w, 'f': stage_f, 'e': stage_e, 'd': stage_d, 'c': stage_c, 'b': stage_b, 'a': stage_a,
               'p': load_start}
     z_start = lead + -(-max(nz - (tiles + 1 + lead * tiles // STEPS), 0) * STEPS // fast)
     hop = 3
-    steps = max((ncc - 1) * STEPS + 26, z_start + nb + hop * 2 * (ntp - 1))
+    steps = max((nc - 1) * STEPS + 27, z_start + nb + hop * 2 * (ntp - 1))
     share_start()
     zb_copy.start()
     e_copy(0).start()
     l_copy(0).start()
 
-    pos_copy = pltpu.make_async_copy(pos, gbuf, s_sem.at[0])
-    pos_copy.start()
     gtile[...] = jnp.zeros_like(gtile)
-    pos_copy.wait()
     s_copy(0).start()
-    own_copy(0).start()
-    d2d_copy(0).start()
-
-    own_copy(0).wait()
-    load_start(0)
 
     def clear(j, carry):
         acc[pl.ds(pl.multiple_of(j * tile, tile), tile), :] = jnp.zeros((tile, d), F32)
         return carry
     lax.fori_loop(0, tiles, clear, 0)
-    stage_a(0)
     share_use()
 
     def one_step(i, carry):
@@ -669,7 +647,7 @@
         lax.fori_loop(uz(i), uz(i + 1), z_unit, 0)
         lax.fori_loop(ug(i), ug(i + 1), g_unit, 0)
         for name, lag, first in lags:
-            later = (i - lag >= STEPS) & (i - lag < ncc * STEPS) & (lax.rem(i - lag + STEPS * 64, STEPS) == 0)
+            later = (i - lag >= STEPS) & (i - lag < nc * STEPS) & (lax.rem(i - lag + STEPS * 64, STEPS) == 0)
 
             @pl.when(later | (i == first))
             def _(name=name, lag=lag, first=first):
@@ -684,7 +662,7 @@
 
     share_end()
 
-    for k in range(max(ncc - RING, 0), ncc):
+    for k in range(max(nc - RING, 0), nc):
         rs1_copy(k).wait_send()
         rs2_copy(k).wait_send()
         for i, c in enumerate(fin_copies(k)):
@@ -716,11 +694,10 @@
     lax.fori_loop(0, nb, drain, 0)
 
 
-def gradients(ntp, ndp, zb, stats, mask, lab, affine, hidden, embed, logits, scatter, pos, chunk, tile, zrows):
+def gradients(ntp, ndp, zb, stats, mask, lab, affine, hidden, embed, logits, scatter, chunk, tile, zrows):
     tokens, d = zb.shape
     vocab_loc = embed.shape[0]
     nc = vocab_loc // chunk
-    ncc = nc + 1
     half, quarter, eighth = chunk // 2, chunk // 4, chunk // 8
     tiles = tokens // tile
     nb = tokens // ntp // zrows
@@ -729,13 +706,12 @@
     dma = lambda *s: pltpu.SemaphoreType.DMA(s)
     vf = lambda *s: pltpu.VMEM(s, F32)
     sds = lambda *s: jax.ShapeDtypeStruct(s, F32)
-    flops = 2 * tokens * d * vocab_loc
     rows = lambda a: a.reshape(tiles, 1, tile)
     res = pl.pallas_call(
         functools.partial(grad_kernel, ntp, ndp, chunk, tile, zrows),
-        out_shape=(sds(vocab_loc + chunk, d), sds(8, 128), sds(tokens, d), sds(ncc, half, d), sds(ncc, half, d),
+        out_shape=(sds(vocab_loc, d), sds(8, 128), sds(tokens, d), sds(nc, half, d), sds(nc, half, d),
                    sds(nb, ntp - 1, zrows, d), sds(nb, ntp - 1, zrows, d), jax.ShapeDtypeStruct((nc, chunk, tokens), BF16)),
-        in_specs=[vm] * 4 + [hbm] * 6,
+        in_specs=[vm] * 4 + [hbm] * 5,
         out_specs=(hbm, vm) + (hbm,) * 6,
         scratch_shapes=[
             pltpu.VMEM((tokens, d), BF16), vf(tiles, 1, tile), vf(tiles, 1, tile), vf(ntp, tiles, 8, tile), vf(ndp, 8, 128), vf(ndp, 8, 128),
@@ -747,20 +723,20 @@
             vf(ntp - 1, zrows, d), vf(ntp - 1, zrows, d), vf(zrows, d), vf(zrows, d), vf(RING, ntp - 1, zrows, d), vf(RING, ntp - 1, zrows, d),
             vf(RING, zrows, d),
             dma(ntp - 1), dma(ntp), dma(ndp - 1), dma(ndp), dma(ndp - 1), dma(ndp), dma(1), dma(2),
-            dma(2), dma(2), dma(1), dma(1), dma(1), dma(1), dma(1), dma(ncc), dma(2), dma(RING), dma(SLOTS), dma(RING), dma(SLOTS), dma(4, RING),
-            dma(ncc), dma(2, ncc), dma(3, RING), dma(3, ncc),
+            dma(2), dma(2), dma(1), dma(1), dma(1), dma(1), dma(1), dma(nc), dma(2), dma(RING), dma(SLOTS), dma(RING), dma(SLOTS), dma(4, RING),
+            dma(nc), dma(2, nc), dma(3, RING), dma(3, nc),
             dma(4), dma(RING), dma(RING), dma(nb), dma(nb), dma(3, RING), dma(nb, ntp - 1), dma(nb, ntp - 1),
             dma(nb, ntp - 1), dma(nb, ntp - 1),
         ],
         compiler_params=pltpu.CompilerParams(vmem_limit_bytes=VMEM_LIMIT, has_side_effects=True),
-        cost_estimate=pl.CostEstimate(flops=2 * flops, bytes_accessed=4 * vocab_loc * (4 * d + tokens),
+        cost_estimate=pl.CostEstimate(flops=4 * tokens * d * vocab_loc, bytes_accessed=4 * vocab_loc * (4 * d + tokens),
                                       transcendentals=tokens * vocab_loc),
         name='gradients',
-    )(stats, rows(mask), rows(lab), affine, zb, hidden, embed, logits, scatter, pos)
+    )(stats, rows(mask), rows(lab), affine, zb, hidden, embed, logits, scatter)
     return res[:3]
 
 
-def finish_kernel(grads, pos_in, rows, gh_in, pos_table, grad_out, pos_out, embed_out, gh_out, ring, in_sem, out_sem):
+def finish_kernel(grads, rows, gh_in, pos_table, grad_out, embed_out, gh_out, ring, in_sem, out_sem):
     i, n = pl.program_id(0), pl.num_programs(0)
     slots, size = ring.shape[0], ring.shape[1]
     ahead = slots - 2
@@ -790,7 +766,6 @@
         take(i + ahead).start()
     take(i).wait()
     give(i).start()
-    pos_out[...] = pos_in[...]
     embed_out[...] = (rows[...] + pos_table[...].astype(F32)).astype(BF16)
     gh_out[...] = gh_in[...].astype(BF16)
 
@@ -806,20 +781,20 @@
     tokens, d = grad_h.shape
     ctx = pos_table.shape[0]
     n = tokens // 64
-    big, mid, small = vocab_loc // n, 64, ctx // n
+    big, mid = vocab_loc // n, 64
     at = lambda r, f=lambda i: i: pl.BlockSpec((r, d), lambda i: (f(i), 0))
     return pl.pallas_call(
         finish_kernel,
         grid=(n,),
-        in_specs=[pl.BlockSpec(memory_space=pl.ANY), at(small, lambda i: vocab_loc // small + i), at(mid), at(mid), at(mid, lambda i: lax.rem(i, ctx // mid))],
-        out_specs=(pl.BlockSpec(memory_space=pl.ANY), at(small), at(mid), at(mid)),
+        in_specs=[pl.BlockSpec(memory_space=pl.ANY), at(mid), at(mid), at(mid, lambda i: lax.rem(i, ctx // mid))],
+        out_specs=(pl.BlockSpec(memory_space=pl.ANY), at(mid), at(mid)),
         scratch_shapes=[pltpu.VMEM((8, big, d), F32), pltpu.SemaphoreType.DMA((8,)), pltpu.SemaphoreType.DMA((8,))],
-        out_shape=(jax.ShapeDtypeStruct((vocab_loc, d), F32), jax.ShapeDtypeStruct((ctx, d), F32),
+        out_shape=(jax.ShapeDtypeStruct((vocab_loc, d), F32),
                    jax.ShapeDtypeStruct((tokens, d), BF16), jax.ShapeDtypeStruct((tokens, d), BF16)),
         compiler_params=pltpu.CompilerParams(vmem_limit_bytes=VMEM_LIMIT),
         cost_estimate=pl.CostEstimate(flops=tokens * d, bytes_accessed=8 * vocab_loc * d, transcendentals=0),
         name='finish',
-    )(grads, grads, rows, grad_h, pos_table)
+    )(grads, rows, grad_h, pos_table)
 
 
 def solution(mesh):
@@ -834,14 +809,16 @@
         tok_local = (tokens - shard_start).reshape(1, ntok)
         lab_local = (labels - shard_start).reshape(1, ntok)
         tok_here = (tok_local >= 0) & (tok_local < vocab_loc)
-        hidden2 = hidden.reshape(ntok, d)
+        hidden2, pos_part = lax.optimization_barrier((hidden.reshape(ntok, d), jnp.sum(grad_x0.astype(F32), axis=0)))
+        grad_pos = lax.psum(pos_part, 'dp')
         affine = jnp.stack([ln_gain, ln_bias])
-        zb, stats, logits, rows, scatter, pos = token_stats(hidden2, affine, lab_local, tok_local, tok_here,
-                                                            grad_x0.reshape(ntok, d), embed_loc, chunk1, tile, ctx)
+        zb, stats, logits, rows, scatter = token_stats(hidden2, affine, lab_local, tok_local, tok_here,
+                                                            grad_x0.reshape(ntok, d), embed_loc, chunk1, tile)
+        rows, grad_pos = lax.optimization_barrier((rows, grad_pos))
         rows = lax.psum(rows, 'tp')
         grads, loss, grad_h = gradients(ntp, ndp, zb, stats, lossmask.astype(F32), lab_local, affine, hidden2, embed_loc,
-                                        logits, scatter, pos, chunk, tile, zrows)
-        grad_embed, grad_pos, embed_out, grad_hidden = finish(grads, rows, grad_h, pos_table, vocab_loc)
+                                        logits, scatter, chunk, tile, zrows)
+        grad_embed, embed_out, grad_hidden = finish(grads, rows, grad_h, pos_table, vocab_loc)
         mean_loss = loss[0, 0]
         embed_out = embed_out.reshape(batch, ctx, d)
         grad_hidden = grad_hidden.reshape(batch, ctx, d)

time: 829 us -> 846 us (1.021)
  Pallas kernels: 800 us -> 809 us
    pallas_call x1, Pallas kernels: 634 us -> 645 us  [gradients(): pl.pallas_call(functools.partial(grad_kernel, ntp, ndp, chunk, tile, zrow...]
  transfers between devices with their start and end apart: 1 -> 2, of which waited for: 0 -> 0; matrix products, arithmetic and copies ran while one was open for 0% -> 1% of each run, Pallas kernels for 77% -> 90%
where the time goes in v8:
time: 846 us; the launch traced here: 841 us
  Pallas kernels  809 us (96%)
  between operations  14.2 us (2%)
  other arithmetic  10.9 us (1%)
    pallas_call x1, Pallas kernels, gradients(): pl.pallas_call(functools.partial(grad_kernel, ntp, ndp, chunk, tile, zrow...  645 us
    pallas_call x1, Pallas kernels, token_stats(): pl.pallas_call(functools.partial(stats_kernel, chunk, tile), grid_spec=pl...  109 us
    pallas_call x1, Pallas kernels, finish(): pl.pallas_call(finish_kernel, grid=(n,), in_specs=[pl.BlockSpec(memory_sp...  56 us
  transfers between devices with their start and end apart: 2, of which 0 were waited for; matrix products, arithmetic and copies ran while one was open for 1% of the time, Pallas kernels for 90%

profile of v8, /device:TPU:0, one launch (start us, length us, event | category | flops | bytes accessed | tf_op | source)
XLA Modules:
  0.0 841.2 jit_solution(15018756785991031347)
XLA Ops:
  7.2 0.0 copy-start.1
  7.2 0.0 copy-start.2
  7.2 0.0 copy-start.3
  7.2 0.0 copy-start.4
  7.2 0.0 all-reduce.3.cloned.1.call-start
  7.3 4.6 convert_reduce_fusion
  11.8 0.0 all-reduce.3.cloned.1.call-update
  11.8 0.0 all-reduce.5.cloned.1.call-start
  11.9 0.0 copy-done.1
  11.9 0.0 copy-done.2
  12.0 0.0 copy-done.3
  12.0 0.0 copy-done.4
  12.0 0.1 reshape.62
  12.1 0.7 convert_reduce_fusion.1.starts
  12.8 5.0 sort.15
  17.8 0.7 reshape.64.lab
  18.5 0.6 pad_maximum_fusion.affine
  19.1 0.0 copy-start
  19.1 108.9 %token_stats.1 = (bf16[1792,1280]{1,0:T(8,128)(2,1)}, f32[7,8,256]{2,1,0:T(8,128)}, f32[12992,1792]{1,0:T(8,128)}, f32[1800,1280]{1,0:T(8,128)}, f32[12992,1280]{1,0:T(8,128)}) custom-call(s32[15]{0:T(128)} %convert_reduce_fusion.1.starts, s32[1792]{0:T(1024)} %get-tuple-element.22.order, s32[1792]{0:T(1024)} %get-tuple-element.23.skey, ...), custom_call_target="tpu_custom_call" | custom-call | flops 59601059840 | bytes 192905216 | tf_op jit(solution)/shard_map/token_stats/pallas_call | solution.py:119
  128.0 0.7 reshape_reshape.3.lab
  128.7 0.0 copy-done
  128.7 0.7 reshape.66.mask
  129.4 0.0 all-reduce.3.cloned.1.call-done
  129.4 0.0 all-reduce.5.cloned.1.call-update
  129.4 644.6 %gradients.1 = (f32[12992,1280]{1,0:T(8,128)}, f32[8,128]{1,0:T(8,128)}, f32[1792,1280]{1,0:T(8,128)}, f32[29,224,1280]{2,1,0:T(8,128)}, f32[29,224,1280]{2,1,0:...) custom-call(f32[7,8,256]{2,1,0:T(8,128)} %get-tuple-element.25.stats, ...), custom_call_target="tpu_custom_call" | custom-call | flops 119202119680 | bytes 359202816 | tf_op jit(solution)/shard_map/gradients/pallas_call | solution.py:710
  774.0 1.2 slice.3
  775.2 0.0 all-reduce.5.cloned.1.call-done.rows
  775.2 56.0 %finish.1 = (f32[12992,1280]{1,0:T(8,128)}, bf16[1792,1280]{1,0:T(8,128)(2,1)}, bf16[1792,1280]{1,0:T(8,128)(2,1)}) custom-call(f32[12992,1280]{1,0:T(8,128)} %get-tuple-element.30.grads, f32[1800,1280]{1,0:T(8,128)} %all-reduce.5.cloned.1.call-done.rows, f32[1792,1280]{1,0:T(8,128)} %get-tuple-element.34.gh_in, bf16[448,1280]{1,0:T(8,128)(2,1)} %pos_table.1), custom_call_target="tpu_custom_call" | custom-call | flops 2293760 | bytes 133038080 | tf_op jit(solution)/shard_map/finish/pallas_call | solution.py:786
  831.2 3.2 copy.16
  (7 shorter events, 0.0 us)
Async XLA Ops:
  7.2 4.7 copy-start.1
  7.2 4.8 copy-start.2
  7.2 4.8 copy-start.3
  7.2 4.8 copy-start.4
  7.2 122.2 %all-reduce.3.cloned.1.call-start = ((), (), s32[]{:S(2)}) async-start(), calls=%async_computation | async-start | bytes 4587520 | tf_op jit(solution)/shard_map/psum | solution.py:813
  11.8 763.4 %all-reduce.5.cloned.1.call-start = ((), (), s32[]{:S(2)}) async-start(), calls=%async_computation.1 | async-start | bytes 18432000 | tf_op jit(solution)/shard_map/psum | solution.py:818
  19.1 109.6 %copy-start = (s32[4,448]{1,0:T(4,128)S(1)}, s32[4,448]{1,0:T(4,128)}, u32[]{:S(2)}) copy-start(s32[4,448]{1,0:T(4,128)} %param.11) | copy-start | bytes 21508
Sparse Core Ops, SparseCore 0:
  12.0 65.0 all-reduce.2
  129.5 322.9 all-reduce.4
